TPU v7x, 128 devices: a whole 4x4x4 slice. The times are simulated.
128 devices in a mesh: row: 16 (over x, z), col: 8 (over y, core).
Axes of the slice: x: 4, y: 4, z: 4, core: 2. Of those that a mesh axis runs over, the one named last changes fastest.
Arguments:
- krylov_basis: float32 [4, 2, 3, 128, 128, 256], P(None, None, None, 'col', 'row'), may hold values from -50 to 50
- susceptibility: float32 [128, 128, 256], P('col', 'row'), may hold values from 0.1 to 1
- green_spectra: bfloat16 [6, 256, 256, 512], P(None, None, 'col', 'row'), may hold values from -3 to 3, as said below
Outputs:
- projections: float32 [4, 2, 2], replicated
- next_block: float32 [2, 3, 128, 128, 256], P(None, None, 'col', 'row')
- block_factor: float32 [2, 2], replicated
Inputs may be any that keep to these rules, and one draw needn't show every extreme that they name: `green_spectra`: each of the six arrays is even on the padded grid: its value at (a, b, c) equals its value at ((-a) mod 256, (-b) mod 256, (-c) mod 512).
All inputs are finite; a program needn't handle non-finite values.
Results may differ from a plain program's by a relative error of at most 0.0003.
Values sent between devices are 32-bit elements; how exact they have to be, the bound alone decides.
No kernel may reach another device: no remote copies, remote signals or barrier semaphores. Data moves between devices by JAX's collectives and lax.ppermute only.
A program may use at most 128 MiB of HBM per device.

v0:
```python
import math

import jax
import jax.numpy as jnp
import ml_dtypes
import numpy as np
from jax import lax
from jax.experimental import pallas as pl
from jax.experimental.pallas import tpu as pltpu
from jax.sharding import Mesh
from jax.sharding import PartitionSpec as P

GX = 256
GY = 128
GZ = 128
NB = 4
ROW = ("row_0", "row_1")
COL = ("col_0", "col_1")
ROW_COL = ROW + COL
NROW = 16
NCOL = 8
LZ = GZ // NCOL
LY = GY // NROW
PX = 2 * GX // NROW
HX = PX // 2
PY = 2 * GY // NCOL
F32 = jnp.float32
BF16 = jnp.bfloat16
tensor_pairs = ((0, 3, 4), (3, 1, 5), (4, 5, 2))
ENTRY = 3.0 * GX * GY * GZ
SCALING = 1.0 / (8 * GX * GY * GZ)
PAIRS = [(i, k) for i in range(2 * NB) for k in range(i, 2 * NB)]
VMEM = 63 * 1024 * 1024


def split_np(table):
    table = table.astype(np.float32)
    high = table.astype(ml_dtypes.bfloat16)
    low = (table - high.astype(np.float32)).astype(ml_dtypes.bfloat16)
    return [high, low]


def tables():
    kx = np.arange(2 * GX).reshape(NROW, 2, PX // 2).transpose(1, 0, 2).reshape(-1)
    angle = (np.outer(np.arange(GX), kx) % (2 * GX)) * (2.0 * math.pi / (2 * GX))
    x_tables = split_np(np.cos(angle)) + split_np(np.sin(angle))
    angle = (np.outer(np.arange(2 * GY), np.arange(GY)) % (2 * GY)) * (2.0 * math.pi / (2 * GY))
    side = np.concatenate([np.cos(angle), np.sin(angle)], axis=0)
    return x_tables, split_np(side), split_np(side.T.copy())


def split(x):
    high = x.astype(BF16)
    low = (x - high.astype(F32)).astype(BF16)
    return high, low


def dot(a, b, ca, cb):
    return lax.dot_general(a, b, (((ca,), (cb,)), ((), ())), preferred_element_type=F32)


def ahead(ref):
    c, s = ref[:256], ref[256:]
    return jnp.concatenate([jnp.concatenate([c, s], axis=1), jnp.concatenate([-s, c], axis=1)], axis=0)


def behind(ref):
    c, s = ref[:, :256], ref[:, 256:]
    return jnp.concatenate([jnp.concatenate([c, -s], axis=1), jnp.concatenate([s, c], axis=1)], axis=0)


def left(th, tl, x, cb):
    h, l = split(x)
    n = th.shape[0]
    wide = dot(jnp.concatenate([th, tl], axis=0), h, 1, cb)
    return wide[:n] + (wide[n:] + dot(th, l, 1, cb))


def right(x, th, tl, cb):
    h, l = split(x)
    n = x.shape[0]
    wide = dot(jnp.concatenate([h, l], axis=0), th, 1, cb)
    return wide[:n] + (wide[n:] + dot(h, tl, 1, cb))


def swap_blocks(v, width):
    v = list(v)
    block = lax.broadcasted_iota(jnp.int32, v[0].shape, 1) // width
    step = len(v) // 2
    while step:
        keep = (block & step) == 0
        for i in range(len(v)):
            if i & step == 0:
                p, q = v[i], v[i + step]
                v[i] = jnp.where(keep, p, pltpu.roll(q, step * width, 1))
                v[i + step] = jnp.where(keep, pltpu.roll(p, 128 - step * width, 1), q)
        step //= 2
    return v


def x_forward(*refs):
    u_ref, ch_ref, cl_ref, sh_ref, sl_ref, o_ref = refs[-6:]
    n = LZ * LY
    u = jnp.concatenate([u_ref[0, 0, 0].reshape(n, GX), u_ref[0, 1, 0].reshape(n, GX)], axis=0)
    c = right(u, ch_ref[...], cl_ref[...], 0)
    s = right(u, sh_ref[...], sl_ref[...], 0)
    acc = jnp.concatenate([c[:n] + s[n:], c[n:] - s[:n]], axis=0)
    acc = acc.reshape(2, 2, 8, LY, GX)
    for t in range(2):
        part = acc[..., t * 128 : (t + 1) * 128]
        v = [part[:, :, zi].reshape(4 * LY, 128) for zi in range(8)]
        for di, w in enumerate(swap_blocks(v, HX)):
            o_ref[8 * t + di, 0] = w.reshape(2, 2, LY, 128)


def y_forward(me_ref, x_ref, th_ref, tl_ref, *refs):
    o_refs, block_ref, s_refs = refs[:NCOL], refs[NCOL], refs[NCOL + 1 :]
    rows = []
    for zq in range(2):
        x = jnp.concatenate([x_ref[:, 0, r, zq].reshape(GY, 128) for r in range(2)], axis=0)
        rows.append(x.T)
    acc = right(jnp.concatenate(rows, axis=0), ahead(th_ref), ahead(tl_ref), 1)
    for r in range(2):
        for t in range(2):
            s_ref = s_refs[2 * r + t]
            lane = r * 256 + t * 128
            s_ref[...] = acc[:, lane : lane + 128]
            v = []
            for ki in range(4):
                v.append(jnp.concatenate([s_ref[pl.ds(4 * kq + ki, LZ, stride=HX), :] for kq in range(4)], axis=0))
            for ei, w in enumerate(swap_blocks(v, PY)):
                block_ref[4 * t + ei, r] = w.reshape(4, LZ, 128)
    for d in range(NCOL):
        o_refs[d][0] = block_ref[me_ref[0] ^ d]


def z_both(_, me_ref, g_ref, th_ref, tl_ref, bh_ref, bl_ref, *refs):
    x_refs, o_refs, s_ref = refs[:NCOL], refs[NCOL : 2 * NCOL], refs[2 * NCOL]
    nk = x_refs[0].shape[2]
    th, tl = ahead(th_ref), ahead(tl_ref)
    bh, bl = behind(bh_ref), behind(bl_ref)
    spectra = []
    for c in range(3):
        for d in range(NCOL):
            for r in range(2):
                row = pl.multiple_of(r * GZ + (me_ref[0] ^ d) * LZ, LZ)
                for k in range(nk):
                    s_ref[c, pl.ds(row, LZ), k * 128 : (k + 1) * 128] = x_refs[d][c, r, k]
        spectra.append(left(th, tl, s_ref[c], 0))
    for c in range(3):
        pieces = []
        for r in range(2):
            total = None
            for j in range(3):
                term = g_ref[tensor_pairs[c][j]].astype(F32) * spectra[j][r * 256 : (r + 1) * 256]
                total = term if total is None else total + term
            pieces.append(total)
        s_ref[c] = left(bh, bl, jnp.concatenate(pieces, axis=0), 0)
        for d in range(NCOL):
            for r in range(2):
                row = pl.multiple_of(r * GZ + (me_ref[0] ^ d) * LZ, LZ)
                for k in range(nk):
                    o_refs[d][c, r, k] = s_ref[c, pl.ds(row, LZ), k * 128 : (k + 1) * 128]


def y_back(_, me_ref, bh_ref, bl_ref, *refs):
    x_refs, o_ref, block_ref, s_refs = refs[:NCOL], refs[NCOL], refs[NCOL + 1], refs[NCOL + 2 :]
    for d in range(NCOL):
        block_ref[me_ref[0] ^ d] = x_refs[d][0]
    for r in range(2):
        for t in range(2):
            s_ref = s_refs[2 * r + t]
            v = [block_ref[4 * t + ei, r].reshape(4 * LZ, 128) for ei in range(4)]
            for ki, w in enumerate(swap_blocks(v, PY)):
                for kq in range(4):
                    s_ref[pl.ds(4 * kq + ki, LZ, stride=HX), :] = w[kq * LZ : (kq + 1) * LZ]
    x = jnp.concatenate([s_ref[...] for s_ref in s_refs], axis=1)
    acc = left(behind(bh_ref), behind(bl_ref), x, 1)
    for r in range(2):
        for zq in range(2):
            o_ref[:, 0, r, zq] = acc[r * GY : (r + 1) * GY, zq * 128 : (zq + 1) * 128].reshape(NROW, LY, 128)


def put_row(sums, first):
    rows = [jnp.sum(s, axis=0, keepdims=True) for s in sums]
    rows += [jnp.zeros((1, 128), F32)] * (-len(sums) % 8)
    stacked = jnp.concatenate(rows, axis=0)
    total = jnp.sum(stacked, axis=1, keepdims=True)
    row = lax.broadcasted_iota(jnp.int32, stacked.shape, 0)
    lane = lax.broadcasted_iota(jnp.int32, stacked.shape, 1)
    return jnp.sum(jnp.where(lane == row + first, total, 0.0), axis=0, keepdims=True)


def basis_gram(b_ref, o_ref):
    c = pl.program_id(0)
    zeros = tuple(jnp.zeros((8, 128), F32) for _ in PAIRS)

    def body(z, acc):
        for half in range(2):
            b = [b_ref[i // 2, i % 2, 0, z, :, half * 128 : (half + 1) * 128] for i in range(2 * NB)]
            acc = tuple(a + b[i] * b[k] for a, (i, k) in zip(acc, PAIRS))
        return acc

    acc = lax.fori_loop(0, LZ, body, zeros)

    @pl.when(c == 0)
    def _():
        o_ref[...] = jnp.zeros_like(o_ref)

    o_ref[...] += put_row(list(acc), 19)


def x_part(x_ref, ch_ref, cl_ref, sh_ref, sl_ref):
    n = LZ * LY
    planes = []
    for r in range(2):
        tiles = []
        for t in range(2):
            v = [x_ref[8 * t + di, 0, r].reshape(2 * LY, 128) for di in range(8)]
            w = [q.reshape(2, 1, LY, 128) for q in swap_blocks(v, HX)]
            tiles.append(jnp.concatenate(w, axis=1).reshape(n, 128))
        planes.append(jnp.concatenate(tiles, axis=1))
    planes = jnp.concatenate(planes, axis=0)
    cos = right(planes, ch_ref[...], cl_ref[...], 1)
    sin = right(planes, sh_ref[...], sl_ref[...], 1)
    return [(cos[:n] - sin[n:]).reshape(LZ, LY, GX), (cos[n:] + sin[:n]).reshape(LZ, LY, GX)]


def x_back_first(x_ref, ch_ref, cl_ref, sh_ref, sl_ref, u_ref, chi_ref, o_ref):
    chi = chi_ref[...] * SCALING
    for j, part in enumerate(x_part(x_ref, ch_ref, cl_ref, sh_ref, sl_ref)):
        o_ref[j, 0] = u_ref[0, j, 0] - chi * part


def x_back(x_ref, ch_ref, cl_ref, sh_ref, sl_ref, p_ref, b_ref, chi_ref, g_ref, img_ref, all_ref, o_ref):
    c = pl.program_id(0)
    chi = chi_ref[...] * SCALING
    for j, part in enumerate(x_part(x_ref, ch_ref, cl_ref, sh_ref, sl_ref)):
        img_ref[j, 0] = p_ref[j, 0] - chi * part

    def body(z, sums):
        for half in range(2):
            lanes = slice(half * 128, (half + 1) * 128)
            b = [b_ref[i // 2, i % 2, 0, z, :, lanes] for i in range(2 * NB)]
            p = [img_ref[j, 0, z, :, lanes] for j in range(2)]
            terms = [b[i] * p[j] for i in range(2 * NB) for j in range(2)]
            terms += [p[0] * p[0], p[0] * p[1], p[1] * p[1]]
            sums = tuple(a + q for a, q in zip(sums, terms))
        return sums

    sums = lax.fori_loop(0, LZ, body, tuple(jnp.zeros((8, 128), F32) for _ in range(19)))

    @pl.when(c == 0)
    def _():
        o_ref[...] = g_ref[...]

    o_ref[...] += put_row(list(sums), 0)

    @pl.when(c == pl.num_programs(0) - 1)
    def _():
        all_ref[...] = jnp.broadcast_to(o_ref[...], all_ref.shape)


def finish(all_ref, img_ref, b_ref, o_ref, coef_ref, factor_ref, row_ref, s_ref, v_ref):
    @pl.when(pl.program_id(0) == 0)
    def _():
        row_ref[...] = jnp.sum(all_ref[...], axis=0, keepdims=True) / ENTRY
        pltpu.sync_copy(row_ref, s_ref)
        coef = [[s_ref[0, 2 * i + j] for j in range(2)] for i in range(2 * NB)]
        cells = [[None] * (2 * NB) for _ in range(2 * NB)]
        for place, (i, k) in enumerate(PAIRS):
            cells[i][k] = cells[k][i] = s_ref[0, 19 + place]
        mixed = []
        for i in range(2 * NB):
            entry = []
            for j in range(2):
                total = -2.0 * coef[i][j]
                for k in range(2 * NB):
                    total = total + cells[i][k] * coef[k][j]
                entry.append(total)
            mixed.append(entry)
        gram = []
        for place, (j, k) in enumerate(((0, 0), (0, 1), (1, 1))):
            total = s_ref[0, 16 + place]
            for i in range(2 * NB):
                total = total + coef[i][j] * mixed[i][k]
            gram.append(jnp.full((8, 128), total, F32))
        lead = jnp.sqrt(gram[0] + 1e-06)
        cross = gram[1] / lead
        tail = jnp.sqrt(gram[2] - cross * cross + 1e-06)
        v_ref[0] = 1.0 / lead
        v_ref[1] = cross
        v_ref[2] = 1.0 / tail
        for i in range(2 * NB):
            for j in range(2):
                coef_ref[i % 2, j, i // 2] = coef[i][j]
        factor_ref[0, 0] = lead[0, 0]
        factor_ref[0, 1] = cross[0, 0]
        factor_ref[1, 0] = 0.0
        factor_ref[1, 1] = tail[0, 0]

    def body(z, carry):
        for half in range(2):
            lanes = slice(half * 128, (half + 1) * 128)
            p0 = img_ref[0, 0, z, :, lanes]
            p1 = img_ref[1, 0, z, :, lanes]
            for i in range(2 * NB):
                b = b_ref[i // 2, i % 2, 0, z, :, lanes]
                p0 = p0 - s_ref[0, 2 * i] * b
                p1 = p1 - s_ref[0, 2 * i + 1] * b
            p0 = p0 * v_ref[0]
            o_ref[0, 0, z, :, lanes] = p0
            o_ref[1, 0, z, :, lanes] = (p1 - v_ref[1] * p0) * v_ref[2]
        return carry

    lax.fori_loop(0, LZ, body, 0)


def call(body, grid, ins, outs, shapes, scratch=()):
    return pl.pallas_call(
        body,
        grid=grid,
        in_specs=ins,
        out_specs=outs,
        out_shape=shapes,
        scratch_shapes=list(scratch),
        compiler_params=pltpu.CompilerParams(vmem_limit_bytes=VMEM, dimension_semantics=("arbitrary",) * len(grid)),
    )


def whole(shape):
    return pl.BlockSpec(shape, lambda *_: (0,) * len(shape))


def exchange_cols(blocks):
    moved = []
    for d in range(1, NCOL):
        moved.append(lax.ppermute(blocks[d], COL, [(i, i ^ d) for i in range(NCOL)]))
    return [blocks[0]] + moved


def exchange_rows(x):
    return lax.all_to_all(x, ROW, split_axis=0, concat_axis=0, tiled=True)


def per_device(krylov_basis, susceptibility, green_spectra):
    x_tables, side, back = ([jnp.asarray(t) for t in group] for group in tables())
    me = lax.axis_index(COL).astype(jnp.int32).reshape(1)
    row_spec = pl.BlockSpec((NROW, 1, 2, 2, LY, 128), lambda c: (0, c, 0, 0, 0, 0))
    row_shape = jax.ShapeDtypeStruct((NROW, 3, 2, 2, LY, 128), F32)
    col_spec = pl.BlockSpec((1, 2, 4, LZ, 128), lambda c: (c, 0, 0, 0, 0))
    col_shape = jax.ShapeDtypeStruct((3, 2, 4, LZ, 128), F32)
    latest_spec = pl.BlockSpec((1, 2, 1, LZ, LY, GX), lambda c: (NB - 1, 0, c, 0, 0, 0))
    basis_spec = pl.BlockSpec((NB, 2, 1, LZ, LY, GX), lambda c: (0, 0, c, 0, 0, 0))
    image_spec = pl.BlockSpec((2, 1, LZ, LY, GX), lambda c: (0, c, 0, 0, 0))
    image_shape = jax.ShapeDtypeStruct((2, 3, LZ, LY, GX), F32)
    line = jax.ShapeDtypeStruct((1, 128), F32)
    smem = pl.BlockSpec(memory_space=pltpu.SMEM)
    turn = [pltpu.VMEM((NCOL, 2, 4, LZ, 128), F32)] + [pltpu.VMEM((LZ * HX, 128), F32)] * 4
    nk = 2
    z_spec = pl.BlockSpec((3, 2, nk, LZ, 128), lambda k: (0, 0, k, 0, 0))
    green = jnp.swapaxes(green_spectra, 2, 3).reshape(6, 2 * GZ, PX * PY)

    after = pl.BlockSpec(memory_space=pl.ANY)
    table_specs = [[pl.BlockSpec((GX, GX), lambda c, half=half: (0, half))] * 4 for half in range(2)]
    sent = []
    for half in range(2):
        earlier = [green, sent[0]] if half else []
        kernel = call(x_forward, (3,), [after] * len(earlier) + [latest_spec] + table_specs[half], row_spec, row_shape)
        sent.append(kernel(*earlier, krylov_basis, *x_tables))
    rows = [exchange_rows(x) for x in sent]
    own = [
        call(
            y_forward,
            (3,),
            [smem, row_spec, whole(side[0].shape), whole(side[1].shape)],
            [col_spec] * NCOL,
            [col_shape] * NCOL,
            turn,
        )(me, rows[half], *side)
        for half in range(2)
    ]
    cols = [exchange_cols(blocks) for blocks in own]
    mixed = []
    for half in range(2):
        mixed.append(
            call(
                z_both,
                (4 // nk,),
                [
                    after,
                    smem,
                    pl.BlockSpec((6, 2 * GZ, nk * 128), lambda k, half=half: (0, 0, half * (4 // nk) + k)),
                    whole(side[0].shape),
                    whole(side[1].shape),
                    whole(back[0].shape),
                    whole(back[1].shape),
                ]
                + [z_spec] * NCOL,
                [z_spec] * NCOL,
                [col_shape] * NCOL,
                [pltpu.VMEM((3, 2 * GZ, nk * 128), F32)],
            )(own[1 - half][0], me, green, *side, *back, *cols[half])
        )
    cols = [exchange_cols(blocks) for blocks in mixed]
    sent = []
    for half in range(2):
        kernel = call(
            y_back,
            (3,),
            [after, smem, whole(back[0].shape), whole(back[1].shape)] + [col_spec] * NCOL,
            row_spec,
            row_shape,
            turn,
        )
        sent.append(kernel(mixed[1 - half][0], me, *back, *cols[half]))
    arrived = [exchange_rows(x) for x in sent]
    gram_part = call(basis_gram, (3,), [basis_spec], whole((1, 128)), line)(krylov_basis)
    chi_spec = whole((LZ, LY, GX))
    first = call(
        x_back_first, (3,), [row_spec] + table_specs[0] + [latest_spec, chi_spec], image_spec, image_shape
    )(arrived[0], *x_tables, krylov_basis, susceptibility)
    image, everyone = call(
        x_back,
        (3,),
        [row_spec] + table_specs[1] + [image_spec, basis_spec, chi_spec, whole((1, 128))],
        [image_spec, whole((NROW * NCOL, 128))],
        [image_shape, jax.ShapeDtypeStruct((NROW * NCOL, 128), F32)],
        [pltpu.VMEM((1, 128), F32)],
    )(arrived[1], *x_tables, first, krylov_basis, susceptibility, gram_part)
    everyone = everyone.reshape(NROW * NCOL, 1, 128)
    everyone = lax.all_to_all(everyone, ROW_COL, split_axis=0, concat_axis=0, tiled=True)
    next_block, coefficients, factor = call(
        finish,
        (3,),
        [whole((NROW * NCOL, 128)), image_spec, basis_spec],
        [image_spec, smem, smem],
        [image_shape, jax.ShapeDtypeStruct((2, 2, NB), F32), jax.ShapeDtypeStruct((2, 2), F32)],
        [pltpu.VMEM((1, 128), F32), pltpu.SMEM((1, 128), F32), pltpu.VMEM((3, 8, 128), F32)],
    )(everyone.reshape(NROW * NCOL, 128), image, krylov_basis)
    return (jnp.transpose(coefficients, (2, 0, 1)), next_block, factor)


def solution(mesh):
    split_mesh = Mesh(mesh.devices.reshape(4, 4, 4, 2), ("row_0", "row_1", "col_0", "col_1"))

    return jax.shard_map(
        per_device,
        mesh=split_mesh,
        in_specs=(P(None, None, None, COL, ROW, None), P(COL, ROW, None), P(None, None, COL, ROW)),
        out_specs=(P(), P(None, None, COL, ROW, None), P()),
        check_vma=False,
    )
```

profile of v0, /device:TPU:1, one launch (start us, length us, event | category | flops | bytes accessed | tf_op | source)
XLA Modules:
  0.0 205.7 jit_solution(3093885366723859962)
XLA Ops:
  0.6 4.2 %shard_map.130.refs_1_ = f32[16,3,2,2,8,128]{5,4,3,2,1,0:T(8,128)} custom-call(f32[4,2,3,16,8,256]{5,4,3,2,1,0:T(8,128)} %b_ref.5, bf16[256,512]{1,0:T(8,128)(2,1)} %constant.26.clone.refs_1_.refs_3_.ch_ref, bf16[256,512]{1,0:T(8,128)(2,1)} %constant.27.clone.refs_2_.refs_4_.cl_ref, bf16[256,512]{1,0:T(8,128)(2,1)} %constant.28.clone.refs_3_.refs_5_.sh_ref, ...), custom_call_target="tpu_custom_call" | custom-call | tf_op jit(solution)/shard_map/pallas_call | solution.py:370
  4.9 8.5 %all-to-all-start.1 = ((f32[16,3,2,2,8,128]{5,4,3,2,1,0:T(8,128)}), f32[16,3,2,2,8,128]{5,4,3,2,1,0:T(8,128)}, u32[]{:S(2)}, u32[]{:S(2)}) async-start(f32[16,3,2,2,8,128]{5,4,3,2,1,0:T(8,128)} %shard_map.130.refs_1_), calls=%async_computation.1 | async-start | bytes 1572864 | tf_op jit(solution)/shard_map/all_to_all | solution.py:343
  13.3 3.8 %copy.19 = bf16[6,256,32,32]{1,2,3,0:T(8,128)(2,1)S(1)} copy(bf16[6,256,32,32]{1,3,2,0:T(8,128)(2,1)} %param.13) | data formatting | bytes 6291456 | tf_op args[2]
  17.1 3.0 %copy.20.refs_0_.g_ref = bf16[6,256,1024]{2,1,0:T(8,128)(2,1)} copy(bf16[6,256,1024]{1,2,0:T(8,128)(2,1)S(1)} %bitcast.9) | data formatting | bytes 6291456 | tf_op jit(solution)/shard_map/reshape | solution.py:362
  20.2 4.2 %shard_map.131 = f32[16,3,2,2,8,128]{5,4,3,2,1,0:T(8,128)} custom-call(bf16[6,256,1024]{2,1,0:T(8,128)(2,1)} %copy.20.refs_0_.g_ref, f32[16,3,2,2,8,128]{5,4,3,2,1,0:T(8,128)} %shard_map.130.refs_1_, f32[4,2,3,16,8,256]{5,4,3,2,1,0:T(8,128)} %b_ref.5, bf16[256,512]{1,0:T(8,128)(2,1)} %constant.26.clone.refs_1_.refs_3_.ch_ref, ...), custom_call_target="tpu_custom_call" | custom-call | tf_op jit(solution)/shard_map/pallas_call | solution.py:370
  24.4 1.8 all-to-all-done.1.x_ref
  26.2 4.8 %all-to-all-start = ((f32[16,3,2,2,8,128]{5,4,3,2,1,0:T(8,128)}), f32[16,3,2,2,8,128]{5,4,3,2,1,0:T(8,128)S(1)}, u32[]{:S(2)}, u32[]{:S(2)}) async-start(f32[16,3,2,2,8,128]{5,4,3,2,1,0:T(8,128)} %shard_map.131), calls=%async_computation | async-start | bytes 1572864 | tf_op jit(solution)/shard_map/all_to_all | solution.py:343
  31.0 4.6 %shard_map.133 = (f32[3,2,4,16,128]{4,3,2,1,0:T(8,128)}, f32[3,2,4,16,128]{4,3,2,1,0:T(8,128)}, f32[3,2,4,16,128]{4,3,2,1,0:T(8,128)}, f32[3,2,4,16,128]{4,3,2,1...) custom-call(s32[1]{0:T(128)} %bitcast.me_ref, ...), custom_call_target="tpu_custom_call" | custom-call | tf_op jit(solution)/shard_map/pallas_call | solution.py:373
  35.6 1.6 collective-permute-start
  37.2 1.3 collective-permute-start.1
  38.9 2.9 %collective-permute-start.3 = (f32[3,2,4,16,128]{4,3,2,1,0:T(8,128)}, f32[3,2,4,16,128]{4,3,2,1,0:T(8,128)}, u32[]{:S(2)}, u32[]{:S(2)}) collective-permute-start(f32[3,2,4,16,128]{4,3,2,1,0:T(8,128)} %get-tuple-element.45), channel_id=1, source_target_pairs={{0,4},{1,5},{2,6},{3,7},{4,0},{5,1},{6,2},{7,3},{8,12},{9,13},{10,... | collective-permute-start | bytes 589832 | tf_op jit(solution)/shard_map/ppermute | solution.py:338
  42.2 2.7 %collective-permute-start.5 = (f32[3,2,4,16,128]{4,3,2,1,0:T(8,128)}, f32[3,2,4,16,128]{4,3,2,1,0:T(8,128)}, u32[]{:S(2)}, u32[]{:S(2)}) collective-permute-start(f32[3,2,4,16,128]{4,3,2,1,0:T(8,128)} %get-tuple-element.47), channel_id=1, source_target_pairs={{0,6},{1,7},{2,4},{3,5},{4,2},{5,3},{6,0},{7,1},{8,14},{9,15},{10,... | collective-permute-start | bytes 589832 | tf_op jit(solution)/shard_map/ppermute | solution.py:338
  45.6 3.0 %collective-permute-start.6 = (f32[3,2,4,16,128]{4,3,2,1,0:T(8,128)}, f32[3,2,4,16,128]{4,3,2,1,0:T(8,128)}, u32[]{:S(2)}, u32[]{:S(2)}) collective-permute-start(f32[3,2,4,16,128]{4,3,2,1,0:T(8,128)} %get-tuple-element.48), channel_id=1, source_target_pairs={{0,7},{1,6},{2,5},{3,4},{4,3},{5,2},{6,1},{7,0},{8,15},{9,14},{10,... | collective-permute-start | bytes 589832 | tf_op jit(solution)/shard_map/ppermute | solution.py:338
  49.4 4.6 %shard_map.132 = (f32[3,2,4,16,128]{4,3,2,1,0:T(8,128)}, f32[3,2,4,16,128]{4,3,2,1,0:T(8,128)}, f32[3,2,4,16,128]{4,3,2,1,0:T(8,128)}, f32[3,2,4,16,128]{4,3,2,1...) custom-call(s32[1]{0:T(128)} %bitcast.me_ref, ...), custom_call_target="tpu_custom_call" | custom-call | tf_op jit(solution)/shard_map/pallas_call | solution.py:373
  54.8 1.8 collective-permute-start.11
  56.6 3.3 %collective-permute-done.4.refs_5_ = f32[3,2,4,16,128]{4,3,2,1,0:T(8,128)} collective-permute-done((f32[3,2,4,16,128]{4,3,2,1,0:T(8,128)}, f32[3,2,4,16,128]{4,3,2,1,0:T(8,128)}, u32[]{:S(2)}, u32[]{:S(2)}) %collective-permute-start.4) | collective-permute-done | bytes 196640 | tf_op jit(solution)/shard_map/ppermute | solution.py:338
  59.9 6.4 %collective-permute-done.5.refs_6_ = f32[3,2,4,16,128]{4,3,2,1,0:T(8,128)} collective-permute-done((f32[3,2,4,16,128]{4,3,2,1,0:T(8,128)}, f32[3,2,4,16,128]{4,3,2,1,0:T(8,128)}, u32[]{:S(2)}, u32[]{:S(2)}) %collective-permute-start.5) | collective-permute-done | bytes 196640 | tf_op jit(solution)/shard_map/ppermute | solution.py:338
  66.3 4.8 %collective-permute-start.13 = (f32[3,2,4,16,128]{4,3,2,1,0:T(8,128)}, f32[3,2,4,16,128]{4,3,2,1,0:T(8,128)S(1)}, u32[]{:S(2)}, u32[]{:S(2)}) collective-permute-start(f32[3,2,4,16,128]{4,3,2,1,0:T(8,128)} %get-tuple-element.56), channel_id=1, source_target_pairs={{0,7},{1,6},{2,5},{3,4},{4,3},{5,2},{6,1},{7,0},{8,15},{9,14},{10,... | collective-permute-start | bytes 589832 | tf_op jit(solution)/shard_map/ppermute | solution.py:338
  71.1 1.0 collective-permute-done.6.refs_7_
  72.0 6.8 %shard_map.134 = (f32[3,2,4,16,128]{4,3,2,1,0:T(8,128)}, f32[3,2,4,16,128]{4,3,2,1,0:T(8,128)}, f32[3,2,4,16,128]{4,3,2,1,0:T(8,128)}, f32[3,2,4,16,128]{4,3,2,1...) custom-call(f32[3,2,4,16,128]{4,3,2,1,0:T(8,128)} %get-tuple-element, ...), custom_call_target="tpu_custom_call" | custom-call | tf_op jit(solution)/shard_map/pallas_call | solution.py:387
  79.0 2.1 %collective-permute-start.9 = (f32[3,2,4,16,128]{4,3,2,1,0:T(8,128)}, f32[3,2,4,16,128]{4,3,2,1,0:T(8,128)}, u32[]{:S(2)}, u32[]{:S(2)}) collective-permute-start(f32[3,2,4,16,128]{4,3,2,1,0:T(8,128)} %get-tuple-element.52), channel_id=1, source_target_pairs={{0,3},{1,2},{2,1},{3,0},{4,7},{5,6},{6,5},{7,4},{8,11},{9,10},{10,... | collective-permute-start | bytes 589832 | tf_op jit(solution)/shard_map/ppermute | solution.py:338
  81.3 1.9 collective-permute-start.23
  83.2 2.0 collective-permute-done.8.refs_2_
  85.2 2.7 %collective-permute-start.24 = (f32[3,2,4,16,128]{4,3,2,1,0:T(8,128)}, f32[3,2,4,16,128]{4,3,2,1,0:T(8,128)}, u32[]{:S(2)}, u32[]{:S(2)}) collective-permute-start(f32[3,2,4,16,128]{4,3,2,1,0:T(8,128)} %get-tuple-element.68), channel_id=1, source_target_pairs={{0,4},{1,5},{2,6},{3,7},{4,0},{5,1},{6,2},{7,3},{8,12},{9,13},{10,... | collective-permute-start | bytes 589832 | tf_op jit(solution)/shard_map/ppermute | solution.py:338
  87.9 3.1 %collective-permute-done.9.refs_3_ = f32[3,2,4,16,128]{4,3,2,1,0:T(8,128)} collective-permute-done((f32[3,2,4,16,128]{4,3,2,1,0:T(8,128)}, f32[3,2,4,16,128]{4,3,2,1,0:T(8,128)}, u32[]{:S(2)}, u32[]{:S(2)}) %collective-permute-start.9) | collective-permute-done | bytes 196640 | tf_op jit(solution)/shard_map/ppermute | solution.py:338
  91.1 2.3 %collective-permute-start.25 = (f32[3,2,4,16,128]{4,3,2,1,0:T(8,128)}, f32[3,2,4,16,128]{4,3,2,1,0:T(8,128)}, u32[]{:S(2)}, u32[]{:S(2)}) collective-permute-start(f32[3,2,4,16,128]{4,3,2,1,0:T(8,128)} %get-tuple-element.69), channel_id=1, source_target_pairs={{0,5},{1,4},{2,7},{3,6},{4,1},{5,0},{6,3},{7,2},{8,13},{9,12},{10,... | collective-permute-start | bytes 589832 | tf_op jit(solution)/shard_map/ppermute | solution.py:338
  93.8 4.8 %collective-permute-start.27 = (f32[3,2,4,16,128]{4,3,2,1,0:T(8,128)}, f32[3,2,4,16,128]{4,3,2,1,0:T(8,128)}, u32[]{:S(2)}, u32[]{:S(2)}) collective-permute-start(f32[3,2,4,16,128]{4,3,2,1,0:T(8,128)} %get-tuple-element.71), channel_id=1, source_target_pairs={{0,7},{1,6},{2,5},{3,4},{4,3},{5,2},{6,1},{7,0},{8,15},{9,14},{10,... | collective-permute-start | bytes 589832 | tf_op jit(solution)/shard_map/ppermute | solution.py:338
  98.6 6.9 %shard_map.135 = (f32[3,2,4,16,128]{4,3,2,1,0:T(8,128)}, f32[3,2,4,16,128]{4,3,2,1,0:T(8,128)}, f32[3,2,4,16,128]{4,3,2,1,0:T(8,128)}, f32[3,2,4,16,128]{4,3,2,1...) custom-call(f32[3,2,4,16,128]{4,3,2,1,0:T(8,128)} %get-tuple-element, ...), custom_call_target="tpu_custom_call" | custom-call | tf_op jit(solution)/shard_map/pallas_call | solution.py:387
  105.5 4.0 %collective-permute-done.25.refs_5_ = f32[3,2,4,16,128]{4,3,2,1,0:T(8,128)} collective-permute-done((f32[3,2,4,16,128]{4,3,2,1,0:T(8,128)}, f32[3,2,4,16,128]{4,3,2,1,0:T(8,128)}, u32[]{:S(2)}, u32[]{:S(2)}) %collective-permute-start.25) | collective-permute-done | bytes 196640 | tf_op jit(solution)/shard_map/ppermute | solution.py:338
  109.5 4.6 %collective-permute-done.27.refs_7_ = f32[3,2,4,16,128]{4,3,2,1,0:T(8,128)} collective-permute-done((f32[3,2,4,16,128]{4,3,2,1,0:T(8,128)}, f32[3,2,4,16,128]{4,3,2,1,0:T(8,128)}, u32[]{:S(2)}, u32[]{:S(2)}) %collective-permute-start.27) | collective-permute-done | bytes 196640 | tf_op jit(solution)/shard_map/ppermute | solution.py:338
  114.1 4.8 %shard_map.137 = f32[16,3,2,2,8,128]{5,4,3,2,1,0:T(8,128)} custom-call(f32[3,2,4,16,128]{4,3,2,1,0:T(8,128)} %get-tuple-element.57.refs_0_._, s32[1]{0:T(128)} %bitcast.me_ref, bf16[128,512]{1,0:T(8,128)(2,1)} %constant.32.clone.bh_ref, bf16[128,512]{1,0:T(8,128)(2,1)} %constant.33.clone.bl_ref, f32[3,2,4,16,128]{4,3,2,1,0:T(8,128)} %get-tuple-element.49._.refs_0_, ...), custom_call_target="tpu_custom_call" | custom-call | tf_op jit(solution)/shard_map/pallas_call | solution.py:416
  118.9 6.9 %all-to-all-start.3 = ((f32[16,3,2,2,8,128]{5,4,3,2,1,0:T(8,128)}), f32[16,3,2,2,8,128]{5,4,3,2,1,0:T(8,128)S(1)}, u32[]{:S(2)}, u32[]{:S(2)}) async-start(f32[16,3,2,2,8,128]{5,4,3,2,1,0:T(8,128)} %shard_map.137), calls=%async_computation.3 | async-start | bytes 1572864 | tf_op jit(solution)/shard_map/all_to_all | solution.py:343
  126.2 1.9 collective-permute-start.16
  128.1 3.1 %collective-permute-start.18 = (f32[3,2,4,16,128]{4,3,2,1,0:T(8,128)}, f32[3,2,4,16,128]{4,3,2,1,0:T(8,128)}, u32[]{:S(2)}, u32[]{:S(2)}) collective-permute-start(f32[3,2,4,16,128]{4,3,2,1,0:T(8,128)} %get-tuple-element.62), channel_id=1, source_target_pairs={{0,5},{1,4},{2,7},{3,6},{4,1},{5,0},{6,3},{7,2},{8,13},{9,12},{10,... | collective-permute-start | bytes 589832 | tf_op jit(solution)/shard_map/ppermute | solution.py:338
  132.7 2.2 %collective-permute-start.20 = (f32[3,2,4,16,128]{4,3,2,1,0:T(8,128)}, f32[3,2,4,16,128]{4,3,2,1,0:T(8,128)}, u32[]{:S(2)}, u32[]{:S(2)}) collective-permute-start(f32[3,2,4,16,128]{4,3,2,1,0:T(8,128)} %get-tuple-element.64), channel_id=1, source_target_pairs={{0,7},{1,6},{2,5},{3,4},{4,3},{5,2},{6,1},{7,0},{8,15},{9,14},{10,... | collective-permute-start | bytes 589832 | tf_op jit(solution)/shard_map/ppermute | solution.py:338
  134.9 3.5 %collective-permute-done.16.refs_3_ = f32[3,2,4,16,128]{4,3,2,1,0:T(8,128)} collective-permute-done((f32[3,2,4,16,128]{4,3,2,1,0:T(8,128)}, f32[3,2,4,16,128]{4,3,2,1,0:T(8,128)}, u32[]{:S(2)}, u32[]{:S(2)}) %collective-permute-start.16) | collective-permute-done | bytes 196640 | tf_op jit(solution)/shard_map/ppermute | solution.py:338
  138.4 3.3 %collective-permute-done.17.refs_4_ = f32[3,2,4,16,128]{4,3,2,1,0:T(8,128)} collective-permute-done((f32[3,2,4,16,128]{4,3,2,1,0:T(8,128)}, f32[3,2,4,16,128]{4,3,2,1,0:T(8,128)}, u32[]{:S(2)}, u32[]{:S(2)}) %collective-permute-start.17) | collective-permute-done | bytes 196640 | tf_op jit(solution)/shard_map/ppermute | solution.py:338
  141.6 4.5 %collective-permute-done.18.refs_5_ = f32[3,2,4,16,128]{4,3,2,1,0:T(8,128)} collective-permute-done((f32[3,2,4,16,128]{4,3,2,1,0:T(8,128)}, f32[3,2,4,16,128]{4,3,2,1,0:T(8,128)}, u32[]{:S(2)}, u32[]{:S(2)}) %collective-permute-start.18) | collective-permute-done | bytes 196640 | tf_op jit(solution)/shard_map/ppermute | solution.py:338
  146.2 1.1 collective-permute-done.19.refs_6_
  147.3 4.7 %collective-permute-done.20.refs_7_ = f32[3,2,4,16,128]{4,3,2,1,0:T(8,128)} collective-permute-done((f32[3,2,4,16,128]{4,3,2,1,0:T(8,128)}, f32[3,2,4,16,128]{4,3,2,1,0:T(8,128)}, u32[]{:S(2)}, u32[]{:S(2)}) %collective-permute-start.20) | collective-permute-done | bytes 196640 | tf_op jit(solution)/shard_map/ppermute | solution.py:338
  152.0 4.8 %shard_map.136 = f32[16,3,2,2,8,128]{5,4,3,2,1,0:T(8,128)} custom-call(f32[3,2,4,16,128]{4,3,2,1,0:T(8,128)} %get-tuple-element.49._.refs_0_, s32[1]{0:T(128)} %bitcast.me_ref, bf16[128,512]{1,0:T(8,128)(2,1)} %constant.32.clone.bh_ref, bf16[128,512]{1,0:T(8,128)(2,1)} %constant.33.clone.bl_ref, f32[3,2,4,16,128]{4,3,2,1,0:T(8,128)} %get-tuple-element.57.refs_0_._, ...), custom_call_target="tpu_custom_call" | custom-call | tf_op jit(solution)/shard_map/pallas_call | solution.py:416
  157.7 6.9 %all-to-all-start.2 = ((f32[16,3,2,2,8,128]{5,4,3,2,1,0:T(8,128)}), f32[16,3,2,2,8,128]{5,4,3,2,1,0:T(8,128)S(1)}, u32[]{:S(2)}, u32[]{:S(2)}) async-start(f32[16,3,2,2,8,128]{5,4,3,2,1,0:T(8,128)} %shard_map.136), calls=%async_computation.2 | async-start | bytes 1572864 | tf_op jit(solution)/shard_map/all_to_all | solution.py:343
  164.5 4.2 %shard_map.139.g_ref = f32[1,128]{1,0:T(1,128)} custom-call(f32[4,2,3,16,8,256]{5,4,3,2,1,0:T(8,128)} %b_ref.5), custom_call_target="tpu_custom_call" | custom-call | tf_op jit(solution)/shard_map/pallas_call | solution.py:418
  168.7 4.2 %shard_map.138.p_ref = f32[2,3,16,8,256]{4,3,2,1,0:T(8,128)} custom-call(f32[16,3,2,2,8,128]{5,4,3,2,1,0:T(8,128)} %copy-done.2, bf16[256,512]{1,0:T(8,128)(2,1)} %constant.26.clone.refs_1_.refs_3_.ch_ref, bf16[256,512]{1,0:T(8,128)(2,1)} %constant.27.clone.refs_2_.refs_4_.cl_ref, bf16[256,512]{1,0:T(8,128)(2,1)} %constant.28.clone.refs_3_.refs_5_.sh_ref, ...), custom_call_target="tpu_custom_call" | custom-call | tf_op jit(solution)/shard_map/pallas_call | solution.py:420
  172.9 4.3 %all-to-all-done.2.x_ref = f32[16,3,2,2,8,128]{5,4,3,2,1,0:T(8,128)S(1)} async-done(((f32[16,3,2,2,8,128]{5,4,3,2,1,0:T(8,128)}), f32[16,3,2,2,8,128]{5,4,3,2,1,0:T(8,128)S(1)}, u32[]{:S(2)}, u32[]{:S(2)}) %all-to-all-start.2) | async-done | bytes 786464 | tf_op jit(solution)/shard_map/all_to_all | solution.py:343
  178.1 5.7 %shard_map.140 = (f32[2,3,16,8,256]{4,3,2,1,0:T(8,128)}, f32[128,128]{1,0:T(8,128)}) custom-call(f32[16,3,2,2,8,128]{5,4,3,2,1,0:T(8,128)} %copy-done, bf16[256,512]{1,0:T(8,128)(2,1)} %constant.26.clone.refs_1_.refs_3_.ch_ref, bf16[256,512]{1,0:T(8,128)(2,1)} %constant.27.clone.refs_2_.refs_4_.cl_ref, ...), custom_call_target="tpu_custom_call" | custom-call | tf_op jit(solution)/shard_map/pallas_call | solution.py:423
  183.7 16.9 %all_to_all.25 = f32[128,1,128]{2,1,0:T(1,128)} all-to-all(f32[128,1,128]{2,1,0:T(1,128)} %bitcast.11), channel_id=1, replica_groups=mesh['row_0'=4,'row_1'=4,'col_0'=4,'col_1'=2] {'row_0','row_1','col_0','..., dimensions={0} | all-to-all | bytes 131072 | tf_op jit(solution)/shard_map/all_to_all | solution.py:432
  200.7 5.0 %shard_map.141 = (f32[2,3,16,8,256]{4,3,2,1,0:T(8,128)}, f32[2,2,4]{2,1,0:T(2,128)}, f32[2,2]{1,0:T(2,128)}) custom-call(f32[128,128]{1,0:T(8,128)} %bitcast.10, f32[2,3,16,8,256]{4,3,2,1,0:T(8,128)} %get-tuple-element.73.img_ref, f32[4,2,3,16,8,256]{5,4,3,2,1,0:T(8,128)} %b_ref.5), custom_call_target="tpu_custom_call" | custom-call | tf_op jit(solution)/shard_map/pallas_call | solution.py:433
  (55 shorter events, 7.5 us)
Async XLA Ops:
  4.9 21.3 %all-to-all-start.1 = ((f32[16,3,2,2,8,128]{5,4,3,2,1,0:T(8,128)}), f32[16,3,2,2,8,128]{5,4,3,2,1,0:T(8,128)}, u32[]{:S(2)}, u32[]{:S(2)}) async-start(f32[16,3,2,2,8,128]{5,4,3,2,1,0:T(8,128)} %shard_map.130.refs_1_), calls=%async_computation.1 | async-start | bytes 1572864 | tf_op jit(solution)/shard_map/all_to_all | solution.py:343
  26.2 22.4 %all-to-all-start = ((f32[16,3,2,2,8,128]{5,4,3,2,1,0:T(8,128)}), f32[16,3,2,2,8,128]{5,4,3,2,1,0:T(8,128)S(1)}, u32[]{:S(2)}, u32[]{:S(2)}) async-start(f32[16,3,2,2,8,128]{5,4,3,2,1,0:T(8,128)} %shard_map.131), calls=%async_computation | async-start | bytes 1572864 | tf_op jit(solution)/shard_map/all_to_all | solution.py:343
  35.6 6.6 %collective-permute-start = (f32[3,2,4,16,128]{4,3,2,1,0:T(8,128)}, f32[3,2,4,16,128]{4,3,2,1,0:T(8,128)S(1)}, u32[]{:S(2)}, u32[]{:S(2)}) collective-permute-start(f32[3,2,4,16,128]{4,3,2,1,0:T(8,128)} %get-tuple-element.42), channel_id=1, source_target_pairs={{0,1},{1,0},{2,3},{3,2},{4,5},{5,4},{6,7},{7,6},{8,9},{9,8},{10,11... | collective-permute-start | bytes 589832 | tf_op jit(solution)/shard_map/ppermute | solution.py:338
  37.2 7.7 %collective-permute-start.1 = (f32[3,2,4,16,128]{4,3,2,1,0:T(8,128)}, f32[3,2,4,16,128]{4,3,2,1,0:T(8,128)S(1)}, u32[]{:S(2)}, u32[]{:S(2)}) collective-permute-start(f32[3,2,4,16,128]{4,3,2,1,0:T(8,128)} %get-tuple-element.43), channel_id=1, source_target_pairs={{0,2},{1,3},{2,0},{3,1},{4,6},{5,7},{6,4},{7,5},{8,10},{9,11},{10,... | collective-permute-start | bytes 589832 | tf_op jit(solution)/shard_map/ppermute | solution.py:338
  38.5 15.5 %collective-permute-start.2 = (f32[3,2,4,16,128]{4,3,2,1,0:T(8,128)}, f32[3,2,4,16,128]{4,3,2,1,0:T(8,128)S(1)}, u32[]{:S(2)}, u32[]{:S(2)}) collective-permute-start(f32[3,2,4,16,128]{4,3,2,1,0:T(8,128)} %get-tuple-element.44), channel_id=1, source_target_pairs={{0,3},{1,2},{2,1},{3,0},{4,7},{5,6},{6,5},{7,4},{8,11},{9,10},{10,... | collective-permute-start | bytes 589832 | tf_op jit(solution)/shard_map/ppermute | solution.py:338
  38.9 15.9 %collective-permute-start.3 = (f32[3,2,4,16,128]{4,3,2,1,0:T(8,128)}, f32[3,2,4,16,128]{4,3,2,1,0:T(8,128)}, u32[]{:S(2)}, u32[]{:S(2)}) collective-permute-start(f32[3,2,4,16,128]{4,3,2,1,0:T(8,128)} %get-tuple-element.45), channel_id=1, source_target_pairs={{0,4},{1,5},{2,6},{3,7},{4,0},{5,1},{6,2},{7,3},{8,12},{9,13},{10,... | collective-permute-start | bytes 589832 | tf_op jit(solution)/shard_map/ppermute | solution.py:338
  41.8 18.0 %collective-permute-start.4 = (f32[3,2,4,16,128]{4,3,2,1,0:T(8,128)}, f32[3,2,4,16,128]{4,3,2,1,0:T(8,128)}, u32[]{:S(2)}, u32[]{:S(2)}) collective-permute-start(f32[3,2,4,16,128]{4,3,2,1,0:T(8,128)} %get-tuple-element.46), channel_id=1, source_target_pairs={{0,5},{1,4},{2,7},{3,6},{4,1},{5,0},{6,3},{7,2},{8,13},{9,12},{10,... | collective-permute-start | bytes 589832 | tf_op jit(solution)/shard_map/ppermute | solution.py:338
  42.2 2.7 %copy-start.8 = (f32[3,2,4,16,128]{4,3,2,1,0:T(8,128)}, f32[3,2,4,16,128]{4,3,2,1,0:T(8,128)S(1)}, u32[]{:S(2)}) copy-start(f32[3,2,4,16,128]{4,3,2,1,0:T(8,128)S(1)} %collective-permute-done.refs_1_) | copy-start | bytes 589828
  42.2 24.1 %collective-permute-start.5 = (f32[3,2,4,16,128]{4,3,2,1,0:T(8,128)}, f32[3,2,4,16,128]{4,3,2,1,0:T(8,128)}, u32[]{:S(2)}, u32[]{:S(2)}) collective-permute-start(f32[3,2,4,16,128]{4,3,2,1,0:T(8,128)} %get-tuple-element.47), channel_id=1, source_target_pairs={{0,6},{1,7},{2,4},{3,5},{4,2},{5,3},{6,0},{7,1},{8,14},{9,15},{10,... | collective-permute-start | bytes 589832 | tf_op jit(solution)/shard_map/ppermute | solution.py:338
  44.9 0.7 copy-start.9
  45.6 26.4 %collective-permute-start.6 = (f32[3,2,4,16,128]{4,3,2,1,0:T(8,128)}, f32[3,2,4,16,128]{4,3,2,1,0:T(8,128)}, u32[]{:S(2)}, u32[]{:S(2)}) collective-permute-start(f32[3,2,4,16,128]{4,3,2,1,0:T(8,128)} %get-tuple-element.48), channel_id=1, source_target_pairs={{0,7},{1,6},{2,5},{3,4},{4,3},{5,2},{6,1},{7,0},{8,15},{9,14},{10,... | collective-permute-start | bytes 589832 | tf_op jit(solution)/shard_map/ppermute | solution.py:338
  48.6 0.9 copy-start.1
  54.0 18.0 %copy-start.10 = (f32[3,2,4,16,128]{4,3,2,1,0:T(8,128)}, f32[3,2,4,16,128]{4,3,2,1,0:T(8,128)S(1)}, u32[]{:S(2)}) copy-start(f32[3,2,4,16,128]{4,3,2,1,0:T(8,128)S(1)} %collective-permute-done.2.refs_3_) | copy-start | bytes 589828
  54.0 24.8 %collective-permute-start.10 = (f32[3,2,4,16,128]{4,3,2,1,0:T(8,128)}, f32[3,2,4,16,128]{4,3,2,1,0:T(8,128)S(1)}, u32[]{:S(2)}, u32[]{:S(2)}) collective-permute-start(f32[3,2,4,16,128]{4,3,2,1,0:T(8,128)} %get-tuple-element.53), channel_id=1, source_target_pairs={{0,4},{1,5},{2,6},{3,7},{4,0},{5,1},{6,2},{7,3},{8,12},{9,13},{10,... | collective-permute-start | bytes 589832 | tf_op jit(solution)/shard_map/ppermute | solution.py:338
  54.8 24.2 %collective-permute-start.11 = (f32[3,2,4,16,128]{4,3,2,1,0:T(8,128)}, f32[3,2,4,16,128]{4,3,2,1,0:T(8,128)S(1)}, u32[]{:S(2)}, u32[]{:S(2)}) collective-permute-start(f32[3,2,4,16,128]{4,3,2,1,0:T(8,128)} %get-tuple-element.54), channel_id=1, source_target_pairs={{0,5},{1,4},{2,7},{3,6},{4,1},{5,0},{6,3},{7,2},{8,13},{9,12},{10,... | collective-permute-start | bytes 589832 | tf_op jit(solution)/shard_map/ppermute | solution.py:338
  59.9 21.2 %collective-permute-start.12 = (f32[3,2,4,16,128]{4,3,2,1,0:T(8,128)}, f32[3,2,4,16,128]{4,3,2,1,0:T(8,128)S(1)}, u32[]{:S(2)}, u32[]{:S(2)}) collective-permute-start(f32[3,2,4,16,128]{4,3,2,1,0:T(8,128)} %get-tuple-element.55), channel_id=1, source_target_pairs={{0,6},{1,7},{2,4},{3,5},{4,2},{5,3},{6,0},{7,1},{8,14},{9,15},{10,... | collective-permute-start | bytes 589832 | tf_op jit(solution)/shard_map/ppermute | solution.py:338
  66.3 14.8 %collective-permute-start.13 = (f32[3,2,4,16,128]{4,3,2,1,0:T(8,128)}, f32[3,2,4,16,128]{4,3,2,1,0:T(8,128)S(1)}, u32[]{:S(2)}, u32[]{:S(2)}) collective-permute-start(f32[3,2,4,16,128]{4,3,2,1,0:T(8,128)} %get-tuple-element.56), channel_id=1, source_target_pairs={{0,7},{1,6},{2,5},{3,4},{4,3},{5,2},{6,1},{7,0},{8,15},{9,14},{10,... | collective-permute-start | bytes 589832 | tf_op jit(solution)/shard_map/ppermute | solution.py:338
  72.0 9.3 %collective-permute-start.7 = (f32[3,2,4,16,128]{4,3,2,1,0:T(8,128)}, f32[3,2,4,16,128]{4,3,2,1,0:T(8,128)S(1)}, u32[]{:S(2)}, u32[]{:S(2)}) collective-permute-start(f32[3,2,4,16,128]{4,3,2,1,0:T(8,128)} %get-tuple-element.50), channel_id=1, source_target_pairs={{0,1},{1,0},{2,3},{3,2},{4,5},{5,4},{6,7},{7,6},{8,9},{9,8},{10,11... | collective-permute-start | bytes 589832 | tf_op jit(solution)/shard_map/ppermute | solution.py:338
  78.9 19.7 %copy-start.3 = (f32[3,2,4,16,128]{4,3,2,1,0:T(8,128)}, f32[3,2,4,16,128]{4,3,2,1,0:T(8,128)S(1)}, u32[]{:S(2)}) copy-start(f32[3,2,4,16,128]{4,3,2,1,0:T(8,128)S(1)} %collective-permute-done.10.refs_4_) | copy-start | bytes 589828
  78.9 6.4 %collective-permute-start.8 = (f32[3,2,4,16,128]{4,3,2,1,0:T(8,128)}, f32[3,2,4,16,128]{4,3,2,1,0:T(8,128)}, u32[]{:S(2)}, u32[]{:S(2)}) collective-permute-start(f32[3,2,4,16,128]{4,3,2,1,0:T(8,128)} %get-tuple-element.51), channel_id=1, source_target_pairs={{0,2},{1,3},{2,0},{3,1},{4,6},{5,7},{6,4},{7,5},{8,10},{9,11},{10,... | collective-permute-start | bytes 589832 | tf_op jit(solution)/shard_map/ppermute | solution.py:338
  79.0 19.6 %copy-start.4 = (f32[3,2,4,16,128]{4,3,2,1,0:T(8,128)}, f32[3,2,4,16,128]{4,3,2,1,0:T(8,128)S(1)}, u32[]{:S(2)}) copy-start(f32[3,2,4,16,128]{4,3,2,1,0:T(8,128)S(1)} %collective-permute-done.11.refs_5_) | copy-start | bytes 589828
  79.0 12.1 %collective-permute-start.9 = (f32[3,2,4,16,128]{4,3,2,1,0:T(8,128)}, f32[3,2,4,16,128]{4,3,2,1,0:T(8,128)}, u32[]{:S(2)}, u32[]{:S(2)}) collective-permute-start(f32[3,2,4,16,128]{4,3,2,1,0:T(8,128)} %get-tuple-element.52), channel_id=1, source_target_pairs={{0,3},{1,2},{2,1},{3,0},{4,7},{5,6},{6,5},{7,4},{8,11},{9,10},{10,... | collective-permute-start | bytes 589832 | tf_op jit(solution)/shard_map/ppermute | solution.py:338
  81.1 17.5 %copy-start.5 = (f32[3,2,4,16,128]{4,3,2,1,0:T(8,128)}, f32[3,2,4,16,128]{4,3,2,1,0:T(8,128)S(1)}, u32[]{:S(2)}) copy-start(f32[3,2,4,16,128]{4,3,2,1,0:T(8,128)S(1)} %collective-permute-done.12.refs_6_) | copy-start | bytes 589828
  81.1 12.2 %collective-permute-start.21 = (f32[3,2,4,16,128]{4,3,2,1,0:T(8,128)}, f32[3,2,4,16,128]{4,3,2,1,0:T(8,128)}, u32[]{:S(2)}, u32[]{:S(2)}) collective-permute-start(f32[3,2,4,16,128]{4,3,2,1,0:T(8,128)} %get-tuple-element.65), channel_id=1, source_target_pairs={{0,1},{1,0},{2,3},{3,2},{4,5},{5,4},{6,7},{7,6},{8,9},{9,8},{10,11... | collective-permute-start | bytes 589832 | tf_op jit(solution)/shard_map/ppermute | solution.py:338
  81.1 17.5 %copy-start.6 = (f32[3,2,4,16,128]{4,3,2,1,0:T(8,128)}, f32[3,2,4,16,128]{4,3,2,1,0:T(8,128)S(1)}, u32[]{:S(2)}) copy-start(f32[3,2,4,16,128]{4,3,2,1,0:T(8,128)S(1)} %collective-permute-done.13.refs_7_) | copy-start | bytes 589828
  81.1 12.7 %collective-permute-start.22 = (f32[3,2,4,16,128]{4,3,2,1,0:T(8,128)}, f32[3,2,4,16,128]{4,3,2,1,0:T(8,128)}, u32[]{:S(2)}, u32[]{:S(2)}) collective-permute-start(f32[3,2,4,16,128]{4,3,2,1,0:T(8,128)} %get-tuple-element.66), channel_id=1, source_target_pairs={{0,2},{1,3},{2,0},{3,1},{4,6},{5,7},{6,4},{7,5},{8,10},{9,11},{10,... | collective-permute-start | bytes 589832 | tf_op jit(solution)/shard_map/ppermute | solution.py:338
  81.3 17.3 %copy-start.7 = (f32[3,2,4,16,128]{4,3,2,1,0:T(8,128)}, f32[3,2,4,16,128]{4,3,2,1,0:T(8,128)S(1)}, u32[]{:S(2)}) copy-start(f32[3,2,4,16,128]{4,3,2,1,0:T(8,128)S(1)} %collective-permute-done.7.refs_1_) | copy-start | bytes 589828
  81.3 24.1 %collective-permute-start.23 = (f32[3,2,4,16,128]{4,3,2,1,0:T(8,128)}, f32[3,2,4,16,128]{4,3,2,1,0:T(8,128)}, u32[]{:S(2)}, u32[]{:S(2)}) collective-permute-start(f32[3,2,4,16,128]{4,3,2,1,0:T(8,128)} %get-tuple-element.67), channel_id=1, source_target_pairs={{0,3},{1,2},{2,1},{3,0},{4,7},{5,6},{6,5},{7,4},{8,11},{9,10},{10,... | collective-permute-start | bytes 589832 | tf_op jit(solution)/shard_map/ppermute | solution.py:338
  85.2 20.2 %collective-permute-start.24 = (f32[3,2,4,16,128]{4,3,2,1,0:T(8,128)}, f32[3,2,4,16,128]{4,3,2,1,0:T(8,128)}, u32[]{:S(2)}, u32[]{:S(2)}) collective-permute-start(f32[3,2,4,16,128]{4,3,2,1,0:T(8,128)} %get-tuple-element.68), channel_id=1, source_target_pairs={{0,4},{1,5},{2,6},{3,7},{4,0},{5,1},{6,2},{7,3},{8,12},{9,13},{10,... | collective-permute-start | bytes 589832 | tf_op jit(solution)/shard_map/ppermute | solution.py:338
  91.1 18.4 %collective-permute-start.25 = (f32[3,2,4,16,128]{4,3,2,1,0:T(8,128)}, f32[3,2,4,16,128]{4,3,2,1,0:T(8,128)}, u32[]{:S(2)}, u32[]{:S(2)}) collective-permute-start(f32[3,2,4,16,128]{4,3,2,1,0:T(8,128)} %get-tuple-element.69), channel_id=1, source_target_pairs={{0,5},{1,4},{2,7},{3,6},{4,1},{5,0},{6,3},{7,2},{8,13},{9,12},{10,... | collective-permute-start | bytes 589832 | tf_op jit(solution)/shard_map/ppermute | solution.py:338
  93.3 16.2 %collective-permute-start.26 = (f32[3,2,4,16,128]{4,3,2,1,0:T(8,128)}, f32[3,2,4,16,128]{4,3,2,1,0:T(8,128)}, u32[]{:S(2)}, u32[]{:S(2)}) collective-permute-start(f32[3,2,4,16,128]{4,3,2,1,0:T(8,128)} %get-tuple-element.70), channel_id=1, source_target_pairs={{0,6},{1,7},{2,4},{3,5},{4,2},{5,3},{6,0},{7,1},{8,14},{9,15},{10,... | collective-permute-start | bytes 589832 | tf_op jit(solution)/shard_map/ppermute | solution.py:338
  93.8 20.3 %collective-permute-start.27 = (f32[3,2,4,16,128]{4,3,2,1,0:T(8,128)}, f32[3,2,4,16,128]{4,3,2,1,0:T(8,128)}, u32[]{:S(2)}, u32[]{:S(2)}) collective-permute-start(f32[3,2,4,16,128]{4,3,2,1,0:T(8,128)} %get-tuple-element.71), channel_id=1, source_target_pairs={{0,7},{1,6},{2,5},{3,4},{4,3},{5,2},{6,1},{7,0},{8,15},{9,14},{10,... | collective-permute-start | bytes 589832 | tf_op jit(solution)/shard_map/ppermute | solution.py:338
  118.9 37.8 %all-to-all-start.3 = ((f32[16,3,2,2,8,128]{5,4,3,2,1,0:T(8,128)}), f32[16,3,2,2,8,128]{5,4,3,2,1,0:T(8,128)S(1)}, u32[]{:S(2)}, u32[]{:S(2)}) async-start(f32[16,3,2,2,8,128]{5,4,3,2,1,0:T(8,128)} %shard_map.137), calls=%async_computation.3 | async-start | bytes 1572864 | tf_op jit(solution)/shard_map/all_to_all | solution.py:343
  125.9 5.3 %collective-permute-start.14 = (f32[3,2,4,16,128]{4,3,2,1,0:T(8,128)}, f32[3,2,4,16,128]{4,3,2,1,0:T(8,128)S(1)}, u32[]{:S(2)}, u32[]{:S(2)}) collective-permute-start(f32[3,2,4,16,128]{4,3,2,1,0:T(8,128)} %get-tuple-element.58), channel_id=1, source_target_pairs={{0,1},{1,0},{2,3},{3,2},{4,5},{5,4},{6,7},{7,6},{8,9},{9,8},{10,11... | collective-permute-start | bytes 589832 | tf_op jit(solution)/shard_map/ppermute | solution.py:338
  126.2 6.5 %collective-permute-start.15 = (f32[3,2,4,16,128]{4,3,2,1,0:T(8,128)}, f32[3,2,4,16,128]{4,3,2,1,0:T(8,128)}, u32[]{:S(2)}, u32[]{:S(2)}) collective-permute-start(f32[3,2,4,16,128]{4,3,2,1,0:T(8,128)} %get-tuple-element.59), channel_id=1, source_target_pairs={{0,2},{1,3},{2,0},{3,1},{4,6},{5,7},{6,4},{7,5},{8,10},{9,11},{10,... | collective-permute-start | bytes 589832 | tf_op jit(solution)/shard_map/ppermute | solution.py:338
  126.2 12.2 %collective-permute-start.16 = (f32[3,2,4,16,128]{4,3,2,1,0:T(8,128)}, f32[3,2,4,16,128]{4,3,2,1,0:T(8,128)}, u32[]{:S(2)}, u32[]{:S(2)}) collective-permute-start(f32[3,2,4,16,128]{4,3,2,1,0:T(8,128)} %get-tuple-element.60), channel_id=1, source_target_pairs={{0,3},{1,2},{2,1},{3,0},{4,7},{5,6},{6,5},{7,4},{8,11},{9,10},{10,... | collective-permute-start | bytes 589832 | tf_op jit(solution)/shard_map/ppermute | solution.py:338
  128.1 13.5 %collective-permute-start.17 = (f32[3,2,4,16,128]{4,3,2,1,0:T(8,128)}, f32[3,2,4,16,128]{4,3,2,1,0:T(8,128)}, u32[]{:S(2)}, u32[]{:S(2)}) collective-permute-start(f32[3,2,4,16,128]{4,3,2,1,0:T(8,128)} %get-tuple-element.61), channel_id=1, source_target_pairs={{0,4},{1,5},{2,6},{3,7},{4,0},{5,1},{6,2},{7,3},{8,12},{9,13},{10,... | collective-permute-start | bytes 589832 | tf_op jit(solution)/shard_map/ppermute | solution.py:338
  128.1 18.1 %collective-permute-start.18 = (f32[3,2,4,16,128]{4,3,2,1,0:T(8,128)}, f32[3,2,4,16,128]{4,3,2,1,0:T(8,128)}, u32[]{:S(2)}, u32[]{:S(2)}) collective-permute-start(f32[3,2,4,16,128]{4,3,2,1,0:T(8,128)} %get-tuple-element.62), channel_id=1, source_target_pairs={{0,5},{1,4},{2,7},{3,6},{4,1},{5,0},{6,3},{7,2},{8,13},{9,12},{10,... | collective-permute-start | bytes 589832 | tf_op jit(solution)/shard_map/ppermute | solution.py:338
  131.2 20.8 %copy-start.11 = (f32[3,2,4,16,128]{4,3,2,1,0:T(8,128)}, f32[3,2,4,16,128]{4,3,2,1,0:T(8,128)S(1)}, u32[]{:S(2)}) copy-start(f32[3,2,4,16,128]{4,3,2,1,0:T(8,128)S(1)} %collective-permute-done.14.refs_1_) | copy-start | bytes 589828
  131.2 16.1 %collective-permute-start.19 = (f32[3,2,4,16,128]{4,3,2,1,0:T(8,128)}, f32[3,2,4,16,128]{4,3,2,1,0:T(8,128)}, u32[]{:S(2)}, u32[]{:S(2)}) collective-permute-start(f32[3,2,4,16,128]{4,3,2,1,0:T(8,128)} %get-tuple-element.63), channel_id=1, source_target_pairs={{0,6},{1,7},{2,4},{3,5},{4,2},{5,3},{6,0},{7,1},{8,14},{9,15},{10,... | collective-permute-start | bytes 589832 | tf_op jit(solution)/shard_map/ppermute | solution.py:338
  132.7 19.3 %collective-permute-start.20 = (f32[3,2,4,16,128]{4,3,2,1,0:T(8,128)}, f32[3,2,4,16,128]{4,3,2,1,0:T(8,128)}, u32[]{:S(2)}, u32[]{:S(2)}) collective-permute-start(f32[3,2,4,16,128]{4,3,2,1,0:T(8,128)} %get-tuple-element.64), channel_id=1, source_target_pairs={{0,7},{1,6},{2,5},{3,4},{4,3},{5,2},{6,1},{7,0},{8,15},{9,14},{10,... | collective-permute-start | bytes 589832 | tf_op jit(solution)/shard_map/ppermute | solution.py:338
  156.8 0.9 copy-start.2
  157.7 19.5 %all-to-all-start.2 = ((f32[16,3,2,2,8,128]{5,4,3,2,1,0:T(8,128)}), f32[16,3,2,2,8,128]{5,4,3,2,1,0:T(8,128)S(1)}, u32[]{:S(2)}, u32[]{:S(2)}) async-start(f32[16,3,2,2,8,128]{5,4,3,2,1,0:T(8,128)} %shard_map.136), calls=%async_computation.2 | async-start | bytes 1572864 | tf_op jit(solution)/shard_map/all_to_all | solution.py:343
  177.2 0.9 copy-start
where the time goes:
time: 207 us; the launch traced here: 206 us
  starting transfers between devices  69 us (33%)
  Pallas kernels  60 us (29%)
  waiting for transfers between devices  48.8 us (24%)
  blocking collectives  16.9 us (8%)
  local copies, waits for them, and re-layouts  10.2 us (5%)
    ppermute x28, waiting for transfers between devices, exchange_cols(): lax.ppermute(blocks[d], COL, [(i, i ^ d) for i in range(NCOL)])  42.7 us
    ppermute x28, starting transfers between devices, exchange_cols(): lax.ppermute(blocks[d], COL, [(i, i ^ d) for i in range(NCOL)])  41.9 us
    all_to_all x4, starting transfers between devices, exchange_rows(): return lax.all_to_all(x, ROW, split_axis=0, concat_axis=0, tiled=True)  27.1 us
    all_to_all x1, blocking collectives, per_device(): lax.all_to_all(everyone, ROW_COL, split_axis=0, concat_axis=0, tiled=True)  16.9 us
    pallas_call x2, Pallas kernels, per_device(): call(z_both, (4 // nk,), [after, smem, pl.BlockSpec((6, 2 * GZ, nk * 128)...  13.7 us
    pallas_call x2, Pallas kernels, per_device(): sent.append(kernel(mixed[1 - half][0], me, *back, *cols[half]))  9.61 us
    pallas_call x2, Pallas kernels, per_device(): call(y_forward, (3,), [smem, row_spec, whole(side[0].shape), whole(side[1...  9.14 us
    pallas_call x2, Pallas kernels, per_device(): sent.append(kernel(*earlier, krylov_basis, *x_tables))  8.47 us
  transfers between devices with their start and end apart: 32, of which 16 were waited for; matrix products, arithmetic and copies ran while one was open for 3% of the time, Pallas kernels for 20%

commit v1 on v0

--- a/solution.py
+++ b/solution.py
@@ -26,11 +26,12 @@
 PY = 2 * GY // NCOL
 F32 = jnp.float32
 BF16 = jnp.bfloat16
-tensor_pairs = ((0, 3, 4), (3, 1, 5), (4, 5, 2))
 ENTRY = 3.0 * GX * GY * GZ
 SCALING = 1.0 / (8 * GX * GY * GZ)
 PAIRS = [(i, k) for i in range(2 * NB) for k in range(i, 2 * NB)]
-VMEM = 63 * 1024 * 1024
+VMEM = 65024 * 1024
+HELD = 57344 * 1024
+SMALL = 16 * 1024 * 1024
 
 
 def split_np(table):
@@ -46,7 +47,7 @@
     x_tables = split_np(np.cos(angle)) + split_np(np.sin(angle))
     angle = (np.outer(np.arange(2 * GY), np.arange(GY)) % (2 * GY)) * (2.0 * math.pi / (2 * GY))
     side = np.concatenate([np.cos(angle), np.sin(angle)], axis=0)
-    return x_tables, split_np(side), split_np(side.T.copy())
+    return x_tables, split_np(side)
 
 
 def split(x):
@@ -135,32 +136,38 @@
 
 
 def z_both(_, me_ref, g_ref, th_ref, tl_ref, bh_ref, bl_ref, *refs):
-    x_refs, o_refs, s_ref = refs[:NCOL], refs[NCOL : 2 * NCOL], refs[2 * NCOL]
+    x_refs, o_refs, s_ref, f_ref = refs[:NCOL], refs[NCOL : 2 * NCOL], refs[2 * NCOL], refs[2 * NCOL + 1]
     nk = x_refs[0].shape[2]
-    th, tl = ahead(th_ref), ahead(tl_ref)
-    bh, bl = behind(bh_ref), behind(bl_ref)
-    spectra = []
-    for c in range(3):
+
+    def place(d, r):
+        return pl.ds(pl.multiple_of(r * GZ + (me_ref[0] ^ d) * LZ, LZ), LZ)
+
+    def there(c, carry):
         for d in range(NCOL):
             for r in range(2):
-                row = pl.multiple_of(r * GZ + (me_ref[0] ^ d) * LZ, LZ)
                 for k in range(nk):
-                    s_ref[c, pl.ds(row, LZ), k * 128 : (k + 1) * 128] = x_refs[d][c, r, k]
-        spectra.append(left(th, tl, s_ref[c], 0))
-    for c in range(3):
+                    s_ref[c, place(d, r), k * 128 : (k + 1) * 128] = x_refs[d][c, r, k]
+        f_ref[c] = left(ahead(th_ref), ahead(tl_ref), s_ref[c], 0)
+        return carry
+
+    def again(c, carry):
         pieces = []
         for r in range(2):
             total = None
             for j in range(3):
-                term = g_ref[tensor_pairs[c][j]].astype(F32) * spectra[j][r * 256 : (r + 1) * 256]
+                entry = jnp.where(c == j, c, c + j + 2)
+                term = g_ref[entry].astype(F32) * f_ref[j, r * 256 : (r + 1) * 256]
                 total = term if total is None else total + term
             pieces.append(total)
-        s_ref[c] = left(bh, bl, jnp.concatenate(pieces, axis=0), 0)
+        s_ref[c] = left(behind(bh_ref), behind(bl_ref), jnp.concatenate(pieces, axis=0), 0)
         for d in range(NCOL):
             for r in range(2):
-                row = pl.multiple_of(r * GZ + (me_ref[0] ^ d) * LZ, LZ)
                 for k in range(nk):
-                    o_refs[d][c, r, k] = s_ref[c, pl.ds(row, LZ), k * 128 : (k + 1) * 128]
+                    o_refs[d][c, r, k] = s_ref[c, place(d, r), k * 128 : (k + 1) * 128]
+        return carry
+
+    lax.fori_loop(0, 3, there, 0)
+    lax.fori_loop(0, 3, again, 0)
 
 
 def y_back(_, me_ref, bh_ref, bl_ref, *refs):
@@ -316,7 +323,7 @@
     lax.fori_loop(0, LZ, body, 0)
 
 
-def call(body, grid, ins, outs, shapes, scratch=()):
+def call(body, grid, ins, outs, shapes, scratch=(), grant=VMEM):
     return pl.pallas_call(
         body,
         grid=grid,
@@ -324,7 +331,7 @@
         out_specs=outs,
         out_shape=shapes,
         scratch_shapes=list(scratch),
-        compiler_params=pltpu.CompilerParams(vmem_limit_bytes=VMEM, dimension_semantics=("arbitrary",) * len(grid)),
+        compiler_params=pltpu.CompilerParams(vmem_limit_bytes=grant, dimension_semantics=("arbitrary",) * len(grid)),
     )
 
 
@@ -344,7 +351,7 @@
 
 
 def per_device(krylov_basis, susceptibility, green_spectra):
-    x_tables, side, back = ([jnp.asarray(t) for t in group] for group in tables())
+    x_tables, side = ([jnp.asarray(t) for t in group] for group in tables())
     me = lax.axis_index(COL).astype(jnp.int32).reshape(1)
     row_spec = pl.BlockSpec((NROW, 1, 2, 2, LY, 128), lambda c: (0, c, 0, 0, 0, 0))
     row_shape = jax.ShapeDtypeStruct((NROW, 3, 2, 2, LY, 128), F32)
@@ -369,6 +376,7 @@
         kernel = call(x_forward, (3,), [after] * len(earlier) + [latest_spec] + table_specs[half], row_spec, row_shape)
         sent.append(kernel(*earlier, krylov_basis, *x_tables))
     rows = [exchange_rows(x) for x in sent]
+    back = [t.T for t in lax.optimization_barrier((*side, sent[0]))[:2]]
     own = [
         call(
             y_forward,
@@ -399,7 +407,7 @@
                 + [z_spec] * NCOL,
                 [z_spec] * NCOL,
                 [col_shape] * NCOL,
-                [pltpu.VMEM((3, 2 * GZ, nk * 128), F32)],
+                [pltpu.VMEM((3, 2 * GZ, nk * 128), F32), pltpu.VMEM((3, 4 * GZ, nk * 128), F32)],
             )(own[1 - half][0], me, green, *side, *back, *cols[half])
         )
     cols = [exchange_cols(blocks) for blocks in mixed]
@@ -427,6 +435,7 @@
         [image_spec, whole((NROW * NCOL, 128))],
         [image_shape, jax.ShapeDtypeStruct((NROW * NCOL, 128), F32)],
         [pltpu.VMEM((1, 128), F32)],
+        HELD,
     )(arrived[1], *x_tables, first, krylov_basis, susceptibility, gram_part)
     everyone = everyone.reshape(NROW * NCOL, 1, 128)
     everyone = lax.all_to_all(everyone, ROW_COL, split_axis=0, concat_axis=0, tiled=True)
@@ -437,6 +446,7 @@
         [image_spec, smem, smem],
         [image_shape, jax.ShapeDtypeStruct((2, 2, NB), F32), jax.ShapeDtypeStruct((2, 2), F32)],
         [pltpu.VMEM((1, 128), F32), pltpu.SMEM((1, 128), F32), pltpu.VMEM((3, 8, 128), F32)],
+        SMALL,
     )(everyone.reshape(NROW * NCOL, 128), image, krylov_basis)
     return (jnp.transpose(coefficients, (2, 0, 1)), next_block, factor)
 

time: 207 us -> 205 us (level)
    pallas_call x2, Pallas kernels: 13.7 us -> 16 us  [per_device(): call(z_both, (4 // nk,), [after, smem, pl.BlockSpec((6, 2 * GZ, nk * 128)...]
    unnamed x25 -> x17, local copies, waits for them, and re-layouts: 7.13 us -> 6.3 us
  transfers between devices with their start and end apart: 32 -> 32, of which waited for: 16 -> 16; matrix products, arithmetic and copies ran while one was open for 3% -> 3% of each run, Pallas kernels for 20% -> 21%
where the time goes in v1:
time: 205 us; the launch traced here: 204 us
  starting transfers between devices  69.5 us (34%)
  Pallas kernels  60.4 us (29%)
  waiting for transfers between devices  47.8 us (23%)
  blocking collectives  16.1 us (8%)
  local copies, waits for them, and re-layouts  9.37 us (5%)
    ppermute x28, starting transfers between devices, exchange_cols(): lax.ppermute(blocks[d], COL, [(i, i ^ d) for i in range(NCOL)])  42.5 us
    ppermute x28, waiting for transfers between devices, exchange_cols(): lax.ppermute(blocks[d], COL, [(i, i ^ d) for i in range(NCOL)])  41.7 us
    all_to_all x4, starting transfers between devices, exchange_rows(): return lax.all_to_all(x, ROW, split_axis=0, concat_axis=0, tiled=True)  27.1 us
    all_to_all x1, blocking collectives, per_device(): lax.all_to_all(everyone, ROW_COL, split_axis=0, concat_axis=0, tiled=True)  16.1 us
    pallas_call x2, Pallas kernels, per_device(): call(z_both, (4 // nk,), [after, smem, pl.BlockSpec((6, 2 * GZ, nk * 128)...  16 us
    pallas_call x2, Pallas kernels, per_device(): sent.append(kernel(mixed[1 - half][0], me, *back, *cols[half]))  9.6 us
    pallas_call x2, Pallas kernels, per_device(): call(y_forward, (3,), [smem, row_spec, whole(side[0].shape), whole(side[1...  9.16 us
    pallas_call x2, Pallas kernels, per_device(): sent.append(kernel(*earlier, krylov_basis, *x_tables))  8.48 us
  transfers between devices with their start and end apart: 32, of which 16 were waited for; matrix products, arithmetic and copies ran while one was open for 3% of the time, Pallas kernels for 21%

profile of v1, /device:TPU:1, one launch (start us, length us, event | category | flops | bytes accessed | tf_op | source)
XLA Modules:
  0.0 204.1 jit_solution(9350772443627020024)
XLA Ops:
  0.6 4.2 %shard_map.112.refs_1_ = f32[16,3,2,2,8,128]{5,4,3,2,1,0:T(8,128)} custom-call(f32[4,2,3,16,8,256]{5,4,3,2,1,0:T(8,128)} %b_ref.5, bf16[256,512]{1,0:T(8,128)(2,1)} %constant.22.clone.refs_1_.refs_3_.ch_ref, bf16[256,512]{1,0:T(8,128)(2,1)} %constant.23.clone.refs_2_.refs_4_.cl_ref, bf16[256,512]{1,0:T(8,128)(2,1)} %constant.24.clone.refs_3_.refs_5_.sh_ref, ...), custom_call_target="tpu_custom_call" | custom-call | tf_op jit(solution)/shard_map/pallas_call | solution.py:377
  4.9 8.5 %all-to-all-start.1 = ((f32[16,3,2,2,8,128]{5,4,3,2,1,0:T(8,128)}), f32[16,3,2,2,8,128]{5,4,3,2,1,0:T(8,128)}, u32[]{:S(2)}, u32[]{:S(2)}) async-start(f32[16,3,2,2,8,128]{5,4,3,2,1,0:T(8,128)} %shard_map.112.refs_1_), calls=%async_computation.1 | async-start | bytes 1572864 | tf_op jit(solution)/shard_map/all_to_all | solution.py:350
  13.3 3.8 %copy.33 = bf16[6,256,32,32]{1,2,3,0:T(8,128)(2,1)S(1)} copy(bf16[6,256,32,32]{1,3,2,0:T(8,128)(2,1)} %param.11) | data formatting | bytes 6291456 | tf_op args[2]
  17.1 3.1 %copy.34.refs_0_.g_ref = bf16[6,256,1024]{2,1,0:T(8,128)(2,1)} copy(bf16[6,256,1024]{1,2,0:T(8,128)(2,1)S(1)} %bitcast.12) | data formatting | bytes 6291456 | tf_op jit(solution)/shard_map/reshape | solution.py:369
  20.2 4.2 %shard_map.113 = f32[16,3,2,2,8,128]{5,4,3,2,1,0:T(8,128)} custom-call(bf16[6,256,1024]{2,1,0:T(8,128)(2,1)} %copy.34.refs_0_.g_ref, f32[16,3,2,2,8,128]{5,4,3,2,1,0:T(8,128)} %shard_map.112.refs_1_, f32[4,2,3,16,8,256]{5,4,3,2,1,0:T(8,128)} %b_ref.5, bf16[256,512]{1,0:T(8,128)(2,1)} %constant.22.clone.refs_1_.refs_3_.ch_ref, ...), custom_call_target="tpu_custom_call" | custom-call | tf_op jit(solution)/shard_map/pallas_call | solution.py:377
  24.4 1.8 all-to-all-done.1.x_ref
  26.2 4.9 %all-to-all-start = ((f32[16,3,2,2,8,128]{5,4,3,2,1,0:T(8,128)}), f32[16,3,2,2,8,128]{5,4,3,2,1,0:T(8,128)}, u32[]{:S(2)}, u32[]{:S(2)}) async-start(f32[16,3,2,2,8,128]{5,4,3,2,1,0:T(8,128)} %shard_map.113), calls=%async_computation | async-start | bytes 1572864 | tf_op jit(solution)/shard_map/all_to_all | solution.py:350
  31.1 4.6 %shard_map.115 = (f32[3,2,4,16,128]{4,3,2,1,0:T(8,128)}, f32[3,2,4,16,128]{4,3,2,1,0:T(8,128)}, f32[3,2,4,16,128]{4,3,2,1,0:T(8,128)}, f32[3,2,4,16,128]{4,3,2,1...) custom-call(s32[1]{0:T(128)} %bitcast.me_ref, ...), custom_call_target="tpu_custom_call" | custom-call | tf_op jit(solution)/shard_map/pallas_call | solution.py:381
  35.7 2.0 collective-permute-start
  37.7 1.3 collective-permute-start.1
  39.4 2.9 %collective-permute-start.3 = (f32[3,2,4,16,128]{4,3,2,1,0:T(8,128)}, f32[3,2,4,16,128]{4,3,2,1,0:T(8,128)S(1)}, u32[]{:S(2)}, u32[]{:S(2)}) collective-permute-start(f32[3,2,4,16,128]{4,3,2,1,0:T(8,128)} %get-tuple-element.49), channel_id=1, source_target_pairs={{0,4},{1,5},{2,6},{3,7},{4,0},{5,1},{6,2},{7,3},{8,12},{9,13},{10,... | collective-permute-start | bytes 589832 | tf_op jit(solution)/shard_map/ppermute | solution.py:345
  42.7 2.7 %collective-permute-start.5 = (f32[3,2,4,16,128]{4,3,2,1,0:T(8,128)}, f32[3,2,4,16,128]{4,3,2,1,0:T(8,128)}, u32[]{:S(2)}, u32[]{:S(2)}) collective-permute-start(f32[3,2,4,16,128]{4,3,2,1,0:T(8,128)} %get-tuple-element.51), channel_id=1, source_target_pairs={{0,6},{1,7},{2,4},{3,5},{4,2},{5,3},{6,0},{7,1},{8,14},{9,15},{10,... | collective-permute-start | bytes 589832 | tf_op jit(solution)/shard_map/ppermute | solution.py:345
  45.5 3.1 %collective-permute-start.6 = (f32[3,2,4,16,128]{4,3,2,1,0:T(8,128)}, f32[3,2,4,16,128]{4,3,2,1,0:T(8,128)}, u32[]{:S(2)}, u32[]{:S(2)}) collective-permute-start(f32[3,2,4,16,128]{4,3,2,1,0:T(8,128)} %get-tuple-element.52), channel_id=1, source_target_pairs={{0,7},{1,6},{2,5},{3,4},{4,3},{5,2},{6,1},{7,0},{8,15},{9,14},{10,... | collective-permute-start | bytes 589832 | tf_op jit(solution)/shard_map/ppermute | solution.py:345
  48.5 4.6 %shard_map.114 = (f32[3,2,4,16,128]{4,3,2,1,0:T(8,128)}, f32[3,2,4,16,128]{4,3,2,1,0:T(8,128)}, f32[3,2,4,16,128]{4,3,2,1,0:T(8,128)}, f32[3,2,4,16,128]{4,3,2,1...) custom-call(s32[1]{0:T(128)} %bitcast.me_ref, ...), custom_call_target="tpu_custom_call" | custom-call | tf_op jit(solution)/shard_map/pallas_call | solution.py:381
  55.9 1.8 collective-permute-start.11
  57.7 2.7 %collective-permute-done.4.refs_5_ = f32[3,2,4,16,128]{4,3,2,1,0:T(8,128)} collective-permute-done((f32[3,2,4,16,128]{4,3,2,1,0:T(8,128)}, f32[3,2,4,16,128]{4,3,2,1,0:T(8,128)}, u32[]{:S(2)}, u32[]{:S(2)}) %collective-permute-start.4) | collective-permute-done | bytes 196640 | tf_op jit(solution)/shard_map/ppermute | solution.py:345
  60.4 6.4 %collective-permute-done.5.refs_6_ = f32[3,2,4,16,128]{4,3,2,1,0:T(8,128)} collective-permute-done((f32[3,2,4,16,128]{4,3,2,1,0:T(8,128)}, f32[3,2,4,16,128]{4,3,2,1,0:T(8,128)}, u32[]{:S(2)}, u32[]{:S(2)}) %collective-permute-start.5) | collective-permute-done | bytes 196640 | tf_op jit(solution)/shard_map/ppermute | solution.py:345
  66.8 4.8 %collective-permute-start.13 = (f32[3,2,4,16,128]{4,3,2,1,0:T(8,128)}, f32[3,2,4,16,128]{4,3,2,1,0:T(8,128)}, u32[]{:S(2)}, u32[]{:S(2)}) collective-permute-start(f32[3,2,4,16,128]{4,3,2,1,0:T(8,128)} %get-tuple-element.60), channel_id=1, source_target_pairs={{0,7},{1,6},{2,5},{3,4},{4,3},{5,2},{6,1},{7,0},{8,15},{9,14},{10,... | collective-permute-start | bytes 589832 | tf_op jit(solution)/shard_map/ppermute | solution.py:345
  72.5 8.0 %shard_map.116 = (f32[3,2,4,16,128]{4,3,2,1,0:T(8,128)}, f32[3,2,4,16,128]{4,3,2,1,0:T(8,128)}, f32[3,2,4,16,128]{4,3,2,1,0:T(8,128)}, f32[3,2,4,16,128]{4,3,2,1...) custom-call(f32[3,2,4,16,128]{4,3,2,1,0:T(8,128)} %get-tuple-element, ...), custom_call_target="tpu_custom_call" | custom-call | tf_op jit(solution)/shard_map/pallas_call | solution.py:395
  80.7 2.0 collective-permute-start.9
  83.0 1.9 collective-permute-start.23
  84.9 2.0 collective-permute-done.8.refs_2_
  86.9 2.7 %collective-permute-start.24 = (f32[3,2,4,16,128]{4,3,2,1,0:T(8,128)}, f32[3,2,4,16,128]{4,3,2,1,0:T(8,128)}, u32[]{:S(2)}, u32[]{:S(2)}) collective-permute-start(f32[3,2,4,16,128]{4,3,2,1,0:T(8,128)} %get-tuple-element.72), channel_id=1, source_target_pairs={{0,4},{1,5},{2,6},{3,7},{4,0},{5,1},{6,2},{7,3},{8,12},{9,13},{10,... | collective-permute-start | bytes 589832 | tf_op jit(solution)/shard_map/ppermute | solution.py:345
  89.7 3.1 %collective-permute-done.9.refs_3_ = f32[3,2,4,16,128]{4,3,2,1,0:T(8,128)} collective-permute-done((f32[3,2,4,16,128]{4,3,2,1,0:T(8,128)}, f32[3,2,4,16,128]{4,3,2,1,0:T(8,128)}, u32[]{:S(2)}, u32[]{:S(2)}) %collective-permute-start.9) | collective-permute-done | bytes 196640 | tf_op jit(solution)/shard_map/ppermute | solution.py:345
  92.7 2.3 %collective-permute-start.25 = (f32[3,2,4,16,128]{4,3,2,1,0:T(8,128)}, f32[3,2,4,16,128]{4,3,2,1,0:T(8,128)}, u32[]{:S(2)}, u32[]{:S(2)}) collective-permute-start(f32[3,2,4,16,128]{4,3,2,1,0:T(8,128)} %get-tuple-element.73), channel_id=1, source_target_pairs={{0,5},{1,4},{2,7},{3,6},{4,1},{5,0},{6,3},{7,2},{8,13},{9,12},{10,... | collective-permute-start | bytes 589832 | tf_op jit(solution)/shard_map/ppermute | solution.py:345
  95.5 4.8 %collective-permute-start.27 = (f32[3,2,4,16,128]{4,3,2,1,0:T(8,128)}, f32[3,2,4,16,128]{4,3,2,1,0:T(8,128)}, u32[]{:S(2)}, u32[]{:S(2)}) collective-permute-start(f32[3,2,4,16,128]{4,3,2,1,0:T(8,128)} %get-tuple-element.75), channel_id=1, source_target_pairs={{0,7},{1,6},{2,5},{3,4},{4,3},{5,2},{6,1},{7,0},{8,15},{9,14},{10,... | collective-permute-start | bytes 589832 | tf_op jit(solution)/shard_map/ppermute | solution.py:345
  100.3 8.0 %shard_map.117 = (f32[3,2,4,16,128]{4,3,2,1,0:T(8,128)}, f32[3,2,4,16,128]{4,3,2,1,0:T(8,128)}, f32[3,2,4,16,128]{4,3,2,1,0:T(8,128)}, f32[3,2,4,16,128]{4,3,2,1...) custom-call(f32[3,2,4,16,128]{4,3,2,1,0:T(8,128)} %get-tuple-element, ...), custom_call_target="tpu_custom_call" | custom-call | tf_op jit(solution)/shard_map/pallas_call | solution.py:395
  108.3 2.9 %collective-permute-done.25.refs_5_ = f32[3,2,4,16,128]{4,3,2,1,0:T(8,128)} collective-permute-done((f32[3,2,4,16,128]{4,3,2,1,0:T(8,128)}, f32[3,2,4,16,128]{4,3,2,1,0:T(8,128)}, u32[]{:S(2)}, u32[]{:S(2)}) %collective-permute-start.25) | collective-permute-done | bytes 196640 | tf_op jit(solution)/shard_map/ppermute | solution.py:345
  111.2 4.6 %collective-permute-done.27.refs_7_ = f32[3,2,4,16,128]{4,3,2,1,0:T(8,128)} collective-permute-done((f32[3,2,4,16,128]{4,3,2,1,0:T(8,128)}, f32[3,2,4,16,128]{4,3,2,1,0:T(8,128)}, u32[]{:S(2)}, u32[]{:S(2)}) %collective-permute-start.27) | collective-permute-done | bytes 196640 | tf_op jit(solution)/shard_map/ppermute | solution.py:345
  115.8 4.8 %shard_map.119 = f32[16,3,2,2,8,128]{5,4,3,2,1,0:T(8,128)} custom-call(f32[3,2,4,16,128]{4,3,2,1,0:T(8,128)} %get-tuple-element.61.refs_0_._, s32[1]{0:T(128)} %bitcast.me_ref, bf16[128,512]{1,0:T(8,128)(2,1)} %bitcast.15, bf16[128,512]{1,0:T(8,128)(2,1)} %bitcast.19, f32[3,2,4,16,128]{4,3,2,1,0:T(8,128)} %get-tuple-element.53._.refs_0_, ...), custom_call_target="tpu_custom_call" | custom-call | tf_op jit(solution)/shard_map/pallas_call | solution.py:424
  120.7 6.8 %all-to-all-start.3 = ((f32[16,3,2,2,8,128]{5,4,3,2,1,0:T(8,128)}), f32[16,3,2,2,8,128]{5,4,3,2,1,0:T(8,128)}, u32[]{:S(2)}, u32[]{:S(2)}) async-start(f32[16,3,2,2,8,128]{5,4,3,2,1,0:T(8,128)} %shard_map.119), calls=%async_computation.3 | async-start | bytes 1572864 | tf_op jit(solution)/shard_map/all_to_all | solution.py:350
  127.8 1.9 collective-permute-start.16
  129.7 3.1 %collective-permute-start.18 = (f32[3,2,4,16,128]{4,3,2,1,0:T(8,128)}, f32[3,2,4,16,128]{4,3,2,1,0:T(8,128)}, u32[]{:S(2)}, u32[]{:S(2)}) collective-permute-start(f32[3,2,4,16,128]{4,3,2,1,0:T(8,128)} %get-tuple-element.66), channel_id=1, source_target_pairs={{0,5},{1,4},{2,7},{3,6},{4,1},{5,0},{6,3},{7,2},{8,13},{9,12},{10,... | collective-permute-start | bytes 589832 | tf_op jit(solution)/shard_map/ppermute | solution.py:345
  134.3 2.1 %collective-permute-start.20 = (f32[3,2,4,16,128]{4,3,2,1,0:T(8,128)}, f32[3,2,4,16,128]{4,3,2,1,0:T(8,128)}, u32[]{:S(2)}, u32[]{:S(2)}) collective-permute-start(f32[3,2,4,16,128]{4,3,2,1,0:T(8,128)} %get-tuple-element.68), channel_id=1, source_target_pairs={{0,7},{1,6},{2,5},{3,4},{4,3},{5,2},{6,1},{7,0},{8,15},{9,14},{10,... | collective-permute-start | bytes 589832 | tf_op jit(solution)/shard_map/ppermute | solution.py:345
  136.4 3.6 %collective-permute-done.16.refs_3_ = f32[3,2,4,16,128]{4,3,2,1,0:T(8,128)} collective-permute-done((f32[3,2,4,16,128]{4,3,2,1,0:T(8,128)}, f32[3,2,4,16,128]{4,3,2,1,0:T(8,128)}, u32[]{:S(2)}, u32[]{:S(2)}) %collective-permute-start.16) | collective-permute-done | bytes 196640 | tf_op jit(solution)/shard_map/ppermute | solution.py:345
  140.0 3.2 %collective-permute-done.17.refs_4_ = f32[3,2,4,16,128]{4,3,2,1,0:T(8,128)} collective-permute-done((f32[3,2,4,16,128]{4,3,2,1,0:T(8,128)}, f32[3,2,4,16,128]{4,3,2,1,0:T(8,128)}, u32[]{:S(2)}, u32[]{:S(2)}) %collective-permute-start.17) | collective-permute-done | bytes 196640 | tf_op jit(solution)/shard_map/ppermute | solution.py:345
  143.2 4.6 %collective-permute-done.18.refs_5_ = f32[3,2,4,16,128]{4,3,2,1,0:T(8,128)} collective-permute-done((f32[3,2,4,16,128]{4,3,2,1,0:T(8,128)}, f32[3,2,4,16,128]{4,3,2,1,0:T(8,128)}, u32[]{:S(2)}, u32[]{:S(2)}) %collective-permute-start.18) | collective-permute-done | bytes 196640 | tf_op jit(solution)/shard_map/ppermute | solution.py:345
  147.8 1.1 collective-permute-done.19.refs_6_
  148.9 4.7 %collective-permute-done.20.refs_7_ = f32[3,2,4,16,128]{4,3,2,1,0:T(8,128)} collective-permute-done((f32[3,2,4,16,128]{4,3,2,1,0:T(8,128)}, f32[3,2,4,16,128]{4,3,2,1,0:T(8,128)}, u32[]{:S(2)}, u32[]{:S(2)}) %collective-permute-start.20) | collective-permute-done | bytes 196640 | tf_op jit(solution)/shard_map/ppermute | solution.py:345
  153.6 4.8 %shard_map.118 = f32[16,3,2,2,8,128]{5,4,3,2,1,0:T(8,128)} custom-call(f32[3,2,4,16,128]{4,3,2,1,0:T(8,128)} %get-tuple-element.53._.refs_0_, s32[1]{0:T(128)} %bitcast.me_ref, bf16[128,512]{1,0:T(8,128)(2,1)} %bitcast.16, bf16[128,512]{1,0:T(8,128)(2,1)} %bitcast.20, f32[3,2,4,16,128]{4,3,2,1,0:T(8,128)} %get-tuple-element.61.refs_0_._, ...), custom_call_target="tpu_custom_call" | custom-call | tf_op jit(solution)/shard_map/pallas_call | solution.py:424
  158.4 6.9 %all-to-all-start.2 = ((f32[16,3,2,2,8,128]{5,4,3,2,1,0:T(8,128)}), f32[16,3,2,2,8,128]{5,4,3,2,1,0:T(8,128)}, u32[]{:S(2)}, u32[]{:S(2)}) async-start(f32[16,3,2,2,8,128]{5,4,3,2,1,0:T(8,128)} %shard_map.118), calls=%async_computation.2 | async-start | bytes 1572864 | tf_op jit(solution)/shard_map/all_to_all | solution.py:350
  165.3 4.2 %shard_map.121.g_ref = f32[1,128]{1,0:T(1,128)} custom-call(f32[4,2,3,16,8,256]{5,4,3,2,1,0:T(8,128)} %b_ref.5), custom_call_target="tpu_custom_call" | custom-call | tf_op jit(solution)/shard_map/pallas_call | solution.py:426
  169.5 4.2 %shard_map.120.p_ref = f32[2,3,16,8,256]{4,3,2,1,0:T(8,128)} custom-call(f32[16,3,2,2,8,128]{5,4,3,2,1,0:T(8,128)} %all-to-all-done.3.x_ref, bf16[256,512]{1,0:T(8,128)(2,1)} %constant.22.clone.refs_1_.refs_3_.ch_ref, bf16[256,512]{1,0:T(8,128)(2,1)} %constant.23.clone.refs_2_.refs_4_.cl_ref, bf16[256,512]{1,0:T(8,128)(2,1)} %constant.24.clone.refs_3_.refs_5_.sh_ref, ...), custom_call_target="tpu_custom_call" | custom-call | tf_op jit(solution)/shard_map/pallas_call | solution.py:428
  173.7 4.3 %all-to-all-done.2.x_ref = f32[16,3,2,2,8,128]{5,4,3,2,1,0:T(8,128)} async-done(((f32[16,3,2,2,8,128]{5,4,3,2,1,0:T(8,128)}), f32[16,3,2,2,8,128]{5,4,3,2,1,0:T(8,128)}, u32[]{:S(2)}, u32[]{:S(2)}) %all-to-all-start.2) | async-done | bytes 786464 | tf_op jit(solution)/shard_map/all_to_all | solution.py:350
  178.0 5.7 %shard_map.122 = (f32[2,3,16,8,256]{4,3,2,1,0:T(8,128)}, f32[128,128]{1,0:T(8,128)}) custom-call(f32[16,3,2,2,8,128]{5,4,3,2,1,0:T(8,128)} %all-to-all-done.2.x_ref, bf16[256,512]{1,0:T(8,128)(2,1)} %constant.22.clone.refs_1_.refs_3_.ch_ref, bf16[256,512]{1,0:T(8,128)(2,1)} %constant.23.clone.refs_2_.refs_4_.cl_ref, ...), custom_call_target="tpu_custom_call" | custom-call | tf_op jit(solution)/shard_map/pallas_call | solution.py:431
  183.7 16.1 %all_to_all.25 = f32[128,1,128]{2,1,0:T(1,128)S(1)} all-to-all(f32[128,1,128]{2,1,0:T(1,128)} %bitcast.21), channel_id=1, replica_groups=mesh['row_0'=4,'row_1'=4,'col_0'=4,'col_1'=2] {'row_0','row_1','col_0','..., dimensions={0} | all-to-all | bytes 131072 | tf_op jit(solution)/shard_map/all_to_all | solution.py:441
  199.8 1.1 copy-done.1
  200.9 3.1 %shard_map.123 = (f32[2,3,16,8,256]{4,3,2,1,0:T(8,128)}, f32[2,2,4]{2,1,0:T(2,128)}, f32[2,2]{1,0:T(2,128)}) custom-call(f32[128,128]{1,0:T(8,128)S(1)} %bitcast.11, f32[2,3,16,8,256]{4,3,2,1,0:T(8,128)S(1)} %copy-done.1, f32[4,2,3,16,8,256]{5,4,3,2,1,0:T(8,128)S(1)} %copy-done), custom_call_target="tpu_custom_call" | custom-call | tf_op jit(solution)/shard_map/pallas_call | solution.py:442
  (47 shorter events, 7.1 us)
Async XLA Ops:
  4.9 21.3 %all-to-all-start.1 = ((f32[16,3,2,2,8,128]{5,4,3,2,1,0:T(8,128)}), f32[16,3,2,2,8,128]{5,4,3,2,1,0:T(8,128)}, u32[]{:S(2)}, u32[]{:S(2)}) async-start(f32[16,3,2,2,8,128]{5,4,3,2,1,0:T(8,128)} %shard_map.112.refs_1_), calls=%async_computation.1 | async-start | bytes 1572864 | tf_op jit(solution)/shard_map/all_to_all | solution.py:350
  26.2 22.3 %all-to-all-start = ((f32[16,3,2,2,8,128]{5,4,3,2,1,0:T(8,128)}), f32[16,3,2,2,8,128]{5,4,3,2,1,0:T(8,128)}, u32[]{:S(2)}, u32[]{:S(2)}) async-start(f32[16,3,2,2,8,128]{5,4,3,2,1,0:T(8,128)} %shard_map.113), calls=%async_computation | async-start | bytes 1572864 | tf_op jit(solution)/shard_map/all_to_all | solution.py:350
  35.7 7.0 %collective-permute-start = (f32[3,2,4,16,128]{4,3,2,1,0:T(8,128)}, f32[3,2,4,16,128]{4,3,2,1,0:T(8,128)}, u32[]{:S(2)}, u32[]{:S(2)}) collective-permute-start(f32[3,2,4,16,128]{4,3,2,1,0:T(8,128)} %get-tuple-element.46), channel_id=1, source_target_pairs={{0,1},{1,0},{2,3},{3,2},{4,5},{5,4},{6,7},{7,6},{8,9},{9,8},{10,11... | collective-permute-start | bytes 589832 | tf_op jit(solution)/shard_map/ppermute | solution.py:345
  37.7 7.7 %collective-permute-start.1 = (f32[3,2,4,16,128]{4,3,2,1,0:T(8,128)}, f32[3,2,4,16,128]{4,3,2,1,0:T(8,128)}, u32[]{:S(2)}, u32[]{:S(2)}) collective-permute-start(f32[3,2,4,16,128]{4,3,2,1,0:T(8,128)} %get-tuple-element.47), channel_id=1, source_target_pairs={{0,2},{1,3},{2,0},{3,1},{4,6},{5,7},{6,4},{7,5},{8,10},{9,11},{10,... | collective-permute-start | bytes 589832 | tf_op jit(solution)/shard_map/ppermute | solution.py:345
  39.0 14.1 %collective-permute-start.2 = (f32[3,2,4,16,128]{4,3,2,1,0:T(8,128)}, f32[3,2,4,16,128]{4,3,2,1,0:T(8,128)S(1)}, u32[]{:S(2)}, u32[]{:S(2)}) collective-permute-start(f32[3,2,4,16,128]{4,3,2,1,0:T(8,128)} %get-tuple-element.48), channel_id=1, source_target_pairs={{0,3},{1,2},{2,1},{3,0},{4,7},{5,6},{6,5},{7,4},{8,11},{9,10},{10,... | collective-permute-start | bytes 589832 | tf_op jit(solution)/shard_map/ppermute | solution.py:345
  39.4 15.8 %collective-permute-start.3 = (f32[3,2,4,16,128]{4,3,2,1,0:T(8,128)}, f32[3,2,4,16,128]{4,3,2,1,0:T(8,128)S(1)}, u32[]{:S(2)}, u32[]{:S(2)}) collective-permute-start(f32[3,2,4,16,128]{4,3,2,1,0:T(8,128)} %get-tuple-element.49), channel_id=1, source_target_pairs={{0,4},{1,5},{2,6},{3,7},{4,0},{5,1},{6,2},{7,3},{8,12},{9,13},{10,... | collective-permute-start | bytes 589832 | tf_op jit(solution)/shard_map/ppermute | solution.py:345
  42.4 18.1 %collective-permute-start.4 = (f32[3,2,4,16,128]{4,3,2,1,0:T(8,128)}, f32[3,2,4,16,128]{4,3,2,1,0:T(8,128)}, u32[]{:S(2)}, u32[]{:S(2)}) collective-permute-start(f32[3,2,4,16,128]{4,3,2,1,0:T(8,128)} %get-tuple-element.50), channel_id=1, source_target_pairs={{0,5},{1,4},{2,7},{3,6},{4,1},{5,0},{6,3},{7,2},{8,13},{9,12},{10,... | collective-permute-start | bytes 589832 | tf_op jit(solution)/shard_map/ppermute | solution.py:345
  42.7 24.1 %collective-permute-start.5 = (f32[3,2,4,16,128]{4,3,2,1,0:T(8,128)}, f32[3,2,4,16,128]{4,3,2,1,0:T(8,128)}, u32[]{:S(2)}, u32[]{:S(2)}) collective-permute-start(f32[3,2,4,16,128]{4,3,2,1,0:T(8,128)} %get-tuple-element.51), channel_id=1, source_target_pairs={{0,6},{1,7},{2,4},{3,5},{4,2},{5,3},{6,0},{7,1},{8,14},{9,15},{10,... | collective-permute-start | bytes 589832 | tf_op jit(solution)/shard_map/ppermute | solution.py:345
  45.5 27.0 %collective-permute-start.6 = (f32[3,2,4,16,128]{4,3,2,1,0:T(8,128)}, f32[3,2,4,16,128]{4,3,2,1,0:T(8,128)}, u32[]{:S(2)}, u32[]{:S(2)}) collective-permute-start(f32[3,2,4,16,128]{4,3,2,1,0:T(8,128)} %get-tuple-element.52), channel_id=1, source_target_pairs={{0,7},{1,6},{2,5},{3,4},{4,3},{5,2},{6,1},{7,0},{8,15},{9,14},{10,... | collective-permute-start | bytes 589832 | tf_op jit(solution)/shard_map/ppermute | solution.py:345
  53.1 0.7 copy-start.4
  53.8 26.7 %collective-permute-start.10 = (f32[3,2,4,16,128]{4,3,2,1,0:T(8,128)}, f32[3,2,4,16,128]{4,3,2,1,0:T(8,128)S(1)}, u32[]{:S(2)}, u32[]{:S(2)}) collective-permute-start(f32[3,2,4,16,128]{4,3,2,1,0:T(8,128)} %get-tuple-element.57), channel_id=1, source_target_pairs={{0,4},{1,5},{2,6},{3,7},{4,0},{5,1},{6,2},{7,3},{8,12},{9,13},{10,... | collective-permute-start | bytes 589832 | tf_op jit(solution)/shard_map/ppermute | solution.py:345
  55.2 0.7 copy-start.5
  55.9 24.8 %collective-permute-start.11 = (f32[3,2,4,16,128]{4,3,2,1,0:T(8,128)}, f32[3,2,4,16,128]{4,3,2,1,0:T(8,128)S(1)}, u32[]{:S(2)}, u32[]{:S(2)}) collective-permute-start(f32[3,2,4,16,128]{4,3,2,1,0:T(8,128)} %get-tuple-element.58), channel_id=1, source_target_pairs={{0,5},{1,4},{2,7},{3,6},{4,1},{5,0},{6,3},{7,2},{8,13},{9,12},{10,... | collective-permute-start | bytes 589832 | tf_op jit(solution)/shard_map/ppermute | solution.py:345
  60.4 22.3 %collective-permute-start.12 = (f32[3,2,4,16,128]{4,3,2,1,0:T(8,128)}, f32[3,2,4,16,128]{4,3,2,1,0:T(8,128)}, u32[]{:S(2)}, u32[]{:S(2)}) collective-permute-start(f32[3,2,4,16,128]{4,3,2,1,0:T(8,128)} %get-tuple-element.59), channel_id=1, source_target_pairs={{0,6},{1,7},{2,4},{3,5},{4,2},{5,3},{6,0},{7,1},{8,14},{9,15},{10,... | collective-permute-start | bytes 589832 | tf_op jit(solution)/shard_map/ppermute | solution.py:345
  66.8 16.0 %collective-permute-start.13 = (f32[3,2,4,16,128]{4,3,2,1,0:T(8,128)}, f32[3,2,4,16,128]{4,3,2,1,0:T(8,128)}, u32[]{:S(2)}, u32[]{:S(2)}) collective-permute-start(f32[3,2,4,16,128]{4,3,2,1,0:T(8,128)} %get-tuple-element.60), channel_id=1, source_target_pairs={{0,7},{1,6},{2,5},{3,4},{4,3},{5,2},{6,1},{7,0},{8,15},{9,14},{10,... | collective-permute-start | bytes 589832 | tf_op jit(solution)/shard_map/ppermute | solution.py:345
  72.5 10.5 %collective-permute-start.7 = (f32[3,2,4,16,128]{4,3,2,1,0:T(8,128)}, f32[3,2,4,16,128]{4,3,2,1,0:T(8,128)}, u32[]{:S(2)}, u32[]{:S(2)}) collective-permute-start(f32[3,2,4,16,128]{4,3,2,1,0:T(8,128)} %get-tuple-element.54), channel_id=1, source_target_pairs={{0,1},{1,0},{2,3},{3,2},{4,5},{5,4},{6,7},{7,6},{8,9},{9,8},{10,11... | collective-permute-start | bytes 589832 | tf_op jit(solution)/shard_map/ppermute | solution.py:345
  80.5 19.7 %copy-start.2 = (f32[3,2,4,16,128]{4,3,2,1,0:T(8,128)}, f32[3,2,4,16,128]{4,3,2,1,0:T(8,128)S(1)}, u32[]{:S(2)}) copy-start(f32[3,2,4,16,128]{4,3,2,1,0:T(8,128)S(1)} %collective-permute-done.10.refs_4_) | copy-start | bytes 589828
  80.5 6.4 %collective-permute-start.8 = (f32[3,2,4,16,128]{4,3,2,1,0:T(8,128)}, f32[3,2,4,16,128]{4,3,2,1,0:T(8,128)}, u32[]{:S(2)}, u32[]{:S(2)}) collective-permute-start(f32[3,2,4,16,128]{4,3,2,1,0:T(8,128)} %get-tuple-element.55), channel_id=1, source_target_pairs={{0,2},{1,3},{2,0},{3,1},{4,6},{5,7},{6,4},{7,5},{8,10},{9,11},{10,... | collective-permute-start | bytes 589832 | tf_op jit(solution)/shard_map/ppermute | solution.py:345
  80.7 19.6 %copy-start.3 = (f32[3,2,4,16,128]{4,3,2,1,0:T(8,128)}, f32[3,2,4,16,128]{4,3,2,1,0:T(8,128)S(1)}, u32[]{:S(2)}) copy-start(f32[3,2,4,16,128]{4,3,2,1,0:T(8,128)S(1)} %collective-permute-done.11.refs_5_) | copy-start | bytes 589828
  80.7 12.0 %collective-permute-start.9 = (f32[3,2,4,16,128]{4,3,2,1,0:T(8,128)}, f32[3,2,4,16,128]{4,3,2,1,0:T(8,128)}, u32[]{:S(2)}, u32[]{:S(2)}) collective-permute-start(f32[3,2,4,16,128]{4,3,2,1,0:T(8,128)} %get-tuple-element.56), channel_id=1, source_target_pairs={{0,3},{1,2},{2,1},{3,0},{4,7},{5,6},{6,5},{7,4},{8,11},{9,10},{10,... | collective-permute-start | bytes 589832 | tf_op jit(solution)/shard_map/ppermute | solution.py:345
  82.8 12.3 %collective-permute-start.21 = (f32[3,2,4,16,128]{4,3,2,1,0:T(8,128)}, f32[3,2,4,16,128]{4,3,2,1,0:T(8,128)}, u32[]{:S(2)}, u32[]{:S(2)}) collective-permute-start(f32[3,2,4,16,128]{4,3,2,1,0:T(8,128)} %get-tuple-element.69), channel_id=1, source_target_pairs={{0,1},{1,0},{2,3},{3,2},{4,5},{5,4},{6,7},{7,6},{8,9},{9,8},{10,11... | collective-permute-start | bytes 589832 | tf_op jit(solution)/shard_map/ppermute | solution.py:345
  82.8 12.7 %collective-permute-start.22 = (f32[3,2,4,16,128]{4,3,2,1,0:T(8,128)}, f32[3,2,4,16,128]{4,3,2,1,0:T(8,128)}, u32[]{:S(2)}, u32[]{:S(2)}) collective-permute-start(f32[3,2,4,16,128]{4,3,2,1,0:T(8,128)} %get-tuple-element.70), channel_id=1, source_target_pairs={{0,2},{1,3},{2,0},{3,1},{4,6},{5,7},{6,4},{7,5},{8,10},{9,11},{10,... | collective-permute-start | bytes 589832 | tf_op jit(solution)/shard_map/ppermute | solution.py:345
  83.0 25.3 %collective-permute-start.23 = (f32[3,2,4,16,128]{4,3,2,1,0:T(8,128)}, f32[3,2,4,16,128]{4,3,2,1,0:T(8,128)}, u32[]{:S(2)}, u32[]{:S(2)}) collective-permute-start(f32[3,2,4,16,128]{4,3,2,1,0:T(8,128)} %get-tuple-element.71), channel_id=1, source_target_pairs={{0,3},{1,2},{2,1},{3,0},{4,7},{5,6},{6,5},{7,4},{8,11},{9,10},{10,... | collective-permute-start | bytes 589832 | tf_op jit(solution)/shard_map/ppermute | solution.py:345
  86.9 21.4 %collective-permute-start.24 = (f32[3,2,4,16,128]{4,3,2,1,0:T(8,128)}, f32[3,2,4,16,128]{4,3,2,1,0:T(8,128)}, u32[]{:S(2)}, u32[]{:S(2)}) collective-permute-start(f32[3,2,4,16,128]{4,3,2,1,0:T(8,128)} %get-tuple-element.72), channel_id=1, source_target_pairs={{0,4},{1,5},{2,6},{3,7},{4,0},{5,1},{6,2},{7,3},{8,12},{9,13},{10,... | collective-permute-start | bytes 589832 | tf_op jit(solution)/shard_map/ppermute | solution.py:345
  92.7 18.5 %collective-permute-start.25 = (f32[3,2,4,16,128]{4,3,2,1,0:T(8,128)}, f32[3,2,4,16,128]{4,3,2,1,0:T(8,128)}, u32[]{:S(2)}, u32[]{:S(2)}) collective-permute-start(f32[3,2,4,16,128]{4,3,2,1,0:T(8,128)} %get-tuple-element.73), channel_id=1, source_target_pairs={{0,5},{1,4},{2,7},{3,6},{4,1},{5,0},{6,3},{7,2},{8,13},{9,12},{10,... | collective-permute-start | bytes 589832 | tf_op jit(solution)/shard_map/ppermute | solution.py:345
  95.0 16.2 %collective-permute-start.26 = (f32[3,2,4,16,128]{4,3,2,1,0:T(8,128)}, f32[3,2,4,16,128]{4,3,2,1,0:T(8,128)}, u32[]{:S(2)}, u32[]{:S(2)}) collective-permute-start(f32[3,2,4,16,128]{4,3,2,1,0:T(8,128)} %get-tuple-element.74), channel_id=1, source_target_pairs={{0,6},{1,7},{2,4},{3,5},{4,2},{5,3},{6,0},{7,1},{8,14},{9,15},{10,... | collective-permute-start | bytes 589832 | tf_op jit(solution)/shard_map/ppermute | solution.py:345
  95.5 20.3 %collective-permute-start.27 = (f32[3,2,4,16,128]{4,3,2,1,0:T(8,128)}, f32[3,2,4,16,128]{4,3,2,1,0:T(8,128)}, u32[]{:S(2)}, u32[]{:S(2)}) collective-permute-start(f32[3,2,4,16,128]{4,3,2,1,0:T(8,128)} %get-tuple-element.75), channel_id=1, source_target_pairs={{0,7},{1,6},{2,5},{3,4},{4,3},{5,2},{6,1},{7,0},{8,15},{9,14},{10,... | collective-permute-start | bytes 589832 | tf_op jit(solution)/shard_map/ppermute | solution.py:345
  120.7 37.8 %all-to-all-start.3 = ((f32[16,3,2,2,8,128]{5,4,3,2,1,0:T(8,128)}), f32[16,3,2,2,8,128]{5,4,3,2,1,0:T(8,128)}, u32[]{:S(2)}, u32[]{:S(2)}) async-start(f32[16,3,2,2,8,128]{5,4,3,2,1,0:T(8,128)} %shard_map.119), calls=%async_computation.3 | async-start | bytes 1572864 | tf_op jit(solution)/shard_map/all_to_all | solution.py:350
  127.5 5.3 %collective-permute-start.14 = (f32[3,2,4,16,128]{4,3,2,1,0:T(8,128)}, f32[3,2,4,16,128]{4,3,2,1,0:T(8,128)S(1)}, u32[]{:S(2)}, u32[]{:S(2)}) collective-permute-start(f32[3,2,4,16,128]{4,3,2,1,0:T(8,128)} %get-tuple-element.62), channel_id=1, source_target_pairs={{0,1},{1,0},{2,3},{3,2},{4,5},{5,4},{6,7},{7,6},{8,9},{9,8},{10,11... | collective-permute-start | bytes 589832 | tf_op jit(solution)/shard_map/ppermute | solution.py:345
  127.8 6.5 %collective-permute-start.15 = (f32[3,2,4,16,128]{4,3,2,1,0:T(8,128)}, f32[3,2,4,16,128]{4,3,2,1,0:T(8,128)S(1)}, u32[]{:S(2)}, u32[]{:S(2)}) collective-permute-start(f32[3,2,4,16,128]{4,3,2,1,0:T(8,128)} %get-tuple-element.63), channel_id=1, source_target_pairs={{0,2},{1,3},{2,0},{3,1},{4,6},{5,7},{6,4},{7,5},{8,10},{9,11},{10,... | collective-permute-start | bytes 589832 | tf_op jit(solution)/shard_map/ppermute | solution.py:345
  127.8 12.2 %collective-permute-start.16 = (f32[3,2,4,16,128]{4,3,2,1,0:T(8,128)}, f32[3,2,4,16,128]{4,3,2,1,0:T(8,128)}, u32[]{:S(2)}, u32[]{:S(2)}) collective-permute-start(f32[3,2,4,16,128]{4,3,2,1,0:T(8,128)} %get-tuple-element.64), channel_id=1, source_target_pairs={{0,3},{1,2},{2,1},{3,0},{4,7},{5,6},{6,5},{7,4},{8,11},{9,10},{10,... | collective-permute-start | bytes 589832 | tf_op jit(solution)/shard_map/ppermute | solution.py:345
  129.7 13.5 %collective-permute-start.17 = (f32[3,2,4,16,128]{4,3,2,1,0:T(8,128)}, f32[3,2,4,16,128]{4,3,2,1,0:T(8,128)}, u32[]{:S(2)}, u32[]{:S(2)}) collective-permute-start(f32[3,2,4,16,128]{4,3,2,1,0:T(8,128)} %get-tuple-element.65), channel_id=1, source_target_pairs={{0,4},{1,5},{2,6},{3,7},{4,0},{5,1},{6,2},{7,3},{8,12},{9,13},{10,... | collective-permute-start | bytes 589832 | tf_op jit(solution)/shard_map/ppermute | solution.py:345
  129.7 18.1 %collective-permute-start.18 = (f32[3,2,4,16,128]{4,3,2,1,0:T(8,128)}, f32[3,2,4,16,128]{4,3,2,1,0:T(8,128)}, u32[]{:S(2)}, u32[]{:S(2)}) collective-permute-start(f32[3,2,4,16,128]{4,3,2,1,0:T(8,128)} %get-tuple-element.66), channel_id=1, source_target_pairs={{0,5},{1,4},{2,7},{3,6},{4,1},{5,0},{6,3},{7,2},{8,13},{9,12},{10,... | collective-permute-start | bytes 589832 | tf_op jit(solution)/shard_map/ppermute | solution.py:345
  132.8 20.8 %copy-start.6 = (f32[3,2,4,16,128]{4,3,2,1,0:T(8,128)}, f32[3,2,4,16,128]{4,3,2,1,0:T(8,128)S(1)}, u32[]{:S(2)}) copy-start(f32[3,2,4,16,128]{4,3,2,1,0:T(8,128)S(1)} %collective-permute-done.14.refs_1_) | copy-start | bytes 589828
  132.8 16.1 %collective-permute-start.19 = (f32[3,2,4,16,128]{4,3,2,1,0:T(8,128)}, f32[3,2,4,16,128]{4,3,2,1,0:T(8,128)}, u32[]{:S(2)}, u32[]{:S(2)}) collective-permute-start(f32[3,2,4,16,128]{4,3,2,1,0:T(8,128)} %get-tuple-element.67), channel_id=1, source_target_pairs={{0,6},{1,7},{2,4},{3,5},{4,2},{5,3},{6,0},{7,1},{8,14},{9,15},{10,... | collective-permute-start | bytes 589832 | tf_op jit(solution)/shard_map/ppermute | solution.py:345
  134.3 19.3 %copy-start.7 = (f32[3,2,4,16,128]{4,3,2,1,0:T(8,128)}, f32[3,2,4,16,128]{4,3,2,1,0:T(8,128)S(1)}, u32[]{:S(2)}) copy-start(f32[3,2,4,16,128]{4,3,2,1,0:T(8,128)S(1)} %collective-permute-done.15.refs_2_) | copy-start | bytes 589828
  134.3 19.3 %collective-permute-start.20 = (f32[3,2,4,16,128]{4,3,2,1,0:T(8,128)}, f32[3,2,4,16,128]{4,3,2,1,0:T(8,128)}, u32[]{:S(2)}, u32[]{:S(2)}) collective-permute-start(f32[3,2,4,16,128]{4,3,2,1,0:T(8,128)} %get-tuple-element.68), channel_id=1, source_target_pairs={{0,7},{1,6},{2,5},{3,4},{4,3},{5,2},{6,1},{7,0},{8,15},{9,14},{10,... | collective-permute-start | bytes 589832 | tf_op jit(solution)/shard_map/ppermute | solution.py:345
  158.4 19.6 %all-to-all-start.2 = ((f32[16,3,2,2,8,128]{5,4,3,2,1,0:T(8,128)}), f32[16,3,2,2,8,128]{5,4,3,2,1,0:T(8,128)}, u32[]{:S(2)}, u32[]{:S(2)}) async-start(f32[16,3,2,2,8,128]{5,4,3,2,1,0:T(8,128)} %shard_map.118), calls=%async_computation.2 | async-start | bytes 1572864 | tf_op jit(solution)/shard_map/all_to_all | solution.py:350
  173.7 26.1 %copy-start = (f32[4,2,3,16,8,256]{5,4,3,2,1,0:T(8,128)S(1)}, f32[4,2,3,16,8,256]{5,4,3,2,1,0:T(8,128)}, u32[]{:S(2)}) copy-start(f32[4,2,3,16,8,256]{5,4,3,2,1,0:T(8,128)} %b_ref.5) | copy-start | bytes 9437188
  199.8 1.1 copy-start.1

commit v2 on v1

--- a/solution.py
+++ b/solution.py
@@ -30,7 +30,8 @@
 SCALING = 1.0 / (8 * GX * GY * GZ)
 PAIRS = [(i, k) for i in range(2 * NB) for k in range(i, 2 * NB)]
 VMEM = 65024 * 1024
-HELD = 57344 * 1024
+HELD = 40 * 1024 * 1024
+ROOMY = 36
 SMALL = 16 * 1024 * 1024
 
 
@@ -233,16 +234,19 @@
     return [(cos[:n] - sin[n:]).reshape(LZ, LY, GX), (cos[n:] + sin[:n]).reshape(LZ, LY, GX)]
 
 
-def x_back_first(x_ref, ch_ref, cl_ref, sh_ref, sl_ref, u_ref, chi_ref, o_ref):
+def x_back_first(x_ref, ch_ref, cl_ref, sh_ref, sl_ref, *refs):
+    others, (u_ref, chi_ref, o_ref, t_ref) = refs[:4], refs[4:]
+    for place, other in enumerate(others):
+        t_ref[place] = other[...]
     chi = chi_ref[...] * SCALING
     for j, part in enumerate(x_part(x_ref, ch_ref, cl_ref, sh_ref, sl_ref)):
         o_ref[j, 0] = u_ref[0, j, 0] - chi * part
 
 
-def x_back(x_ref, ch_ref, cl_ref, sh_ref, sl_ref, p_ref, b_ref, chi_ref, g_ref, img_ref, all_ref, o_ref):
+def x_back(x_ref, t_ref, p_ref, b_ref, chi_ref, g_ref, img_ref, all_ref, o_ref):
     c = pl.program_id(0)
     chi = chi_ref[...] * SCALING
-    for j, part in enumerate(x_part(x_ref, ch_ref, cl_ref, sh_ref, sl_ref)):
+    for j, part in enumerate(x_part(x_ref, *(t_ref.at[place] for place in range(4)))):
         img_ref[j, 0] = p_ref[j, 0] - chi * part
 
     def body(z, sums):
@@ -423,20 +427,27 @@
         )
         sent.append(kernel(mixed[1 - half][0], me, *back, *cols[half]))
     arrived = [exchange_rows(x) for x in sent]
-    gram_part = call(basis_gram, (3,), [basis_spec], whole((1, 128)), line)(krylov_basis)
+    gram_part = call(basis_gram, (3,), [basis_spec], whole((1, 128)), line, (), HELD)(krylov_basis)
     chi_spec = whole((LZ, LY, GX))
-    first = call(
-        x_back_first, (3,), [row_spec] + table_specs[0] + [latest_spec, chi_spec], image_spec, image_shape
-    )(arrived[0], *x_tables, krylov_basis, susceptibility)
+    table_spec = pl.BlockSpec((4, GX, GX), lambda c: (0, 0, 0))
+    first, table = call(
+        x_back_first,
+        (3,),
+        [row_spec] + table_specs[0] + table_specs[1] + [latest_spec, chi_spec],
+        [image_spec, table_spec],
+        [jax.ShapeDtypeStruct((2, 3, ROOMY * LZ, LY, GX), F32), jax.ShapeDtypeStruct((6 * ROOMY, GX, GX), BF16)],
+        (),
+        HELD,
+    )(arrived[0], *x_tables, *x_tables, krylov_basis, susceptibility)
     image, everyone = call(
         x_back,
         (3,),
-        [row_spec] + table_specs[1] + [image_spec, basis_spec, chi_spec, whole((1, 128))],
+        [row_spec, table_spec, image_spec, basis_spec, chi_spec, whole((1, 128))],
         [image_spec, whole((NROW * NCOL, 128))],
         [image_shape, jax.ShapeDtypeStruct((NROW * NCOL, 128), F32)],
         [pltpu.VMEM((1, 128), F32)],
         HELD,
-    )(arrived[1], *x_tables, first, krylov_basis, susceptibility, gram_part)
+    )(arrived[1], table, first, krylov_basis, susceptibility, gram_part)
     everyone = everyone.reshape(NROW * NCOL, 1, 128)
     everyone = lax.all_to_all(everyone, ROW_COL, split_axis=0, concat_axis=0, tiled=True)
     next_block, coefficients, factor = call(

time: 205 us -> 194 us (0.946)
  starting transfers between devices: 69.5 us -> 64 us
  waiting for transfers between devices: 47.8 us -> 43.1 us
  Pallas kernels: 60.4 us -> 57 us
    ppermute x28, starting transfers between devices: 42.5 us -> 36.8 us  [exchange_cols(): lax.ppermute(blocks[d], COL, [(i, i ^ d) for i in range(NCOL)])]
    ppermute x28, waiting for transfers between devices: 41.7 us -> 36.9 us  [exchange_cols(): lax.ppermute(blocks[d], COL, [(i, i ^ d) for i in range(NCOL)])]
    pallas_call x3, Pallas kernels: 14.1 us -> 10.7 us  [the longest x1 4.35 us: per_device(): call(x_back, (3,), [row_spec, table_spec, image_spec, basis_spec, chi_spe...]
    unnamed x17 -> x31, local copies, waits for them, and re-layouts: 6.3 us -> 7.74 us
  transfers between devices with their start and end apart: 32 -> 32, of which waited for: 16 -> 13; matrix products, arithmetic and copies ran while one was open for 3% -> 4% of each run, Pallas kernels for 21% -> 21%
where the time goes in v2:
time: 194 us; the launch traced here: 193 us
  starting transfers between devices  64 us (33%)
  Pallas kernels  57 us (29%)
  waiting for transfers between devices  43.1 us (22%)
  blocking collectives  16.9 us (9%)
  local copies, waits for them, and re-layouts  10.8 us (6%)
    ppermute x28, waiting for transfers between devices, exchange_cols(): lax.ppermute(blocks[d], COL, [(i, i ^ d) for i in range(NCOL)])  36.9 us
    ppermute x28, starting transfers between devices, exchange_cols(): lax.ppermute(blocks[d], COL, [(i, i ^ d) for i in range(NCOL)])  36.8 us
    all_to_all x4, starting transfers between devices, exchange_rows(): return lax.all_to_all(x, ROW, split_axis=0, concat_axis=0, tiled=True)  27.1 us
    all_to_all x1, blocking collectives, per_device(): lax.all_to_all(everyone, ROW_COL, split_axis=0, concat_axis=0, tiled=True)  16.9 us
    pallas_call x2, Pallas kernels, per_device(): call(z_both, (4 // nk,), [after, smem, pl.BlockSpec((6, 2 * GZ, nk * 128)...  16 us
    pallas_call x2, Pallas kernels, per_device(): sent.append(kernel(mixed[1 - half][0], me, *back, *cols[half]))  9.59 us
    pallas_call x2, Pallas kernels, per_device(): call(y_forward, (3,), [smem, row_spec, whole(side[0].shape), whole(side[1...  9.14 us
    pallas_call x2, Pallas kernels, per_device(): sent.append(kernel(*earlier, krylov_basis, *x_tables))  8.48 us
  transfers between devices with their start and end apart: 32, of which 13 were waited for; matrix products, arithmetic and copies ran while one was open for 4% of the time, Pallas kernels for 21%

profile of v2, /device:TPU:1, one launch (start us, length us, event | category | flops | bytes accessed | tf_op | source)
XLA Modules:
  0.0 192.8 jit_solution(6960826807234746915)
XLA Ops:
  0.6 4.2 %shard_map.112.refs_1_ = f32[16,3,2,2,8,128]{5,4,3,2,1,0:T(8,128)} custom-call(f32[4,2,3,16,8,256]{5,4,3,2,1,0:T(8,128)} %b_ref.5, bf16[256,512]{1,0:T(8,128)(2,1)} %constant.22.clone.refs_1_.refs_3_.ch_ref.refs_0_, bf16[256,512]{1,0:T(8,128)(2,1)} %constant.23.clone.refs_2_.refs_4_.cl_ref.refs_1_, ...), custom_call_target="tpu_custom_call" | custom-call | tf_op jit(solution)/shard_map/pallas_call | solution.py:381
  4.9 8.5 %all-to-all-start.1 = ((f32[16,3,2,2,8,128]{5,4,3,2,1,0:T(8,128)}), f32[16,3,2,2,8,128]{5,4,3,2,1,0:T(8,128)}, u32[]{:S(2)}, u32[]{:S(2)}) async-start(f32[16,3,2,2,8,128]{5,4,3,2,1,0:T(8,128)} %shard_map.112.refs_1_), calls=%async_computation.1 | async-start | bytes 1572864 | tf_op jit(solution)/shard_map/all_to_all | solution.py:354
  13.3 3.8 %copy.33 = bf16[6,256,32,32]{1,2,3,0:T(8,128)(2,1)S(1)} copy(bf16[6,256,32,32]{1,3,2,0:T(8,128)(2,1)} %param.11) | data formatting | bytes 6291456 | tf_op args[2]
  17.1 3.1 %copy.34.refs_0_.g_ref = bf16[6,256,1024]{2,1,0:T(8,128)(2,1)} copy(bf16[6,256,1024]{1,2,0:T(8,128)(2,1)S(1)} %bitcast.13) | data formatting | bytes 6291456 | tf_op jit(solution)/shard_map/reshape | solution.py:373
  20.2 4.2 %shard_map.113 = f32[16,3,2,2,8,128]{5,4,3,2,1,0:T(8,128)} custom-call(bf16[6,256,1024]{2,1,0:T(8,128)(2,1)} %copy.34.refs_0_.g_ref, f32[16,3,2,2,8,128]{5,4,3,2,1,0:T(8,128)} %shard_map.112.refs_1_, f32[4,2,3,16,8,256]{5,4,3,2,1,0:T(8,128)} %b_ref.5, bf16[256,512]{1,0:T(8,128)(2,1)} %constant.22.clone.refs_1_.refs_3_.ch_ref.refs_0_, ...), custom_call_target="tpu_custom_call" | custom-call | tf_op jit(solution)/shard_map/pallas_call | solution.py:381
  24.4 1.8 all-to-all-done.1.x_ref
  26.2 4.9 %all-to-all-start = ((f32[16,3,2,2,8,128]{5,4,3,2,1,0:T(8,128)}), f32[16,3,2,2,8,128]{5,4,3,2,1,0:T(8,128)}, u32[]{:S(2)}, u32[]{:S(2)}) async-start(f32[16,3,2,2,8,128]{5,4,3,2,1,0:T(8,128)} %shard_map.113), calls=%async_computation | async-start | bytes 1572864 | tf_op jit(solution)/shard_map/all_to_all | solution.py:354
  31.1 4.6 %shard_map.115 = (f32[3,2,4,16,128]{4,3,2,1,0:T(8,128)}, f32[3,2,4,16,128]{4,3,2,1,0:T(8,128)}, f32[3,2,4,16,128]{4,3,2,1,0:T(8,128)}, f32[3,2,4,16,128]{4,3,2,1...) custom-call(s32[1]{0:T(128)} %bitcast.me_ref, ...), custom_call_target="tpu_custom_call" | custom-call | tf_op jit(solution)/shard_map/pallas_call | solution.py:385
  35.7 2.0 %collective-permute-start = (f32[3,2,4,16,128]{4,3,2,1,0:T(8,128)}, f32[3,2,4,16,128]{4,3,2,1,0:T(8,128)}, u32[]{:S(2)}, u32[]{:S(2)}) collective-permute-start(f32[3,2,4,16,128]{4,3,2,1,0:T(8,128)} %get-tuple-element.48), channel_id=1, source_target_pairs={{0,1},{1,0},{2,3},{3,2},{4,5},{5,4},{6,7},{7,6},{8,9},{9,8},{10,11... | collective-permute-start | bytes 589832 | tf_op jit(solution)/shard_map/ppermute | solution.py:349
  39.4 2.9 %collective-permute-start.3 = (f32[3,2,4,16,128]{4,3,2,1,0:T(8,128)}, f32[3,2,4,16,128]{4,3,2,1,0:T(8,128)S(1)}, u32[]{:S(2)}, u32[]{:S(2)}) collective-permute-start(f32[3,2,4,16,128]{4,3,2,1,0:T(8,128)} %get-tuple-element.51), channel_id=1, source_target_pairs={{0,4},{1,5},{2,6},{3,7},{4,0},{5,1},{6,2},{7,3},{8,12},{9,13},{10,... | collective-permute-start | bytes 589832 | tf_op jit(solution)/shard_map/ppermute | solution.py:349
  42.7 2.7 %collective-permute-start.5 = (f32[3,2,4,16,128]{4,3,2,1,0:T(8,128)}, f32[3,2,4,16,128]{4,3,2,1,0:T(8,128)}, u32[]{:S(2)}, u32[]{:S(2)}) collective-permute-start(f32[3,2,4,16,128]{4,3,2,1,0:T(8,128)} %get-tuple-element.53), channel_id=1, source_target_pairs={{0,6},{1,7},{2,4},{3,5},{4,2},{5,3},{6,0},{7,1},{8,14},{9,15},{10,... | collective-permute-start | bytes 589832 | tf_op jit(solution)/shard_map/ppermute | solution.py:349
  45.5 3.1 %collective-permute-start.6 = (f32[3,2,4,16,128]{4,3,2,1,0:T(8,128)}, f32[3,2,4,16,128]{4,3,2,1,0:T(8,128)}, u32[]{:S(2)}, u32[]{:S(2)}) collective-permute-start(f32[3,2,4,16,128]{4,3,2,1,0:T(8,128)} %get-tuple-element.54), channel_id=1, source_target_pairs={{0,7},{1,6},{2,5},{3,4},{4,3},{5,2},{6,1},{7,0},{8,15},{9,14},{10,... | collective-permute-start | bytes 589832 | tf_op jit(solution)/shard_map/ppermute | solution.py:349
  48.5 4.6 %shard_map.114 = (f32[3,2,4,16,128]{4,3,2,1,0:T(8,128)}, f32[3,2,4,16,128]{4,3,2,1,0:T(8,128)}, f32[3,2,4,16,128]{4,3,2,1,0:T(8,128)}, f32[3,2,4,16,128]{4,3,2,1...) custom-call(s32[1]{0:T(128)} %bitcast.me_ref, ...), custom_call_target="tpu_custom_call" | custom-call | tf_op jit(solution)/shard_map/pallas_call | solution.py:385
  53.8 1.4 collective-permute-done.3.refs_4_
  55.9 4.4 %collective-permute-done.4.refs_5_ = f32[3,2,4,16,128]{4,3,2,1,0:T(8,128)} collective-permute-done((f32[3,2,4,16,128]{4,3,2,1,0:T(8,128)}, f32[3,2,4,16,128]{4,3,2,1,0:T(8,128)}, u32[]{:S(2)}, u32[]{:S(2)}) %collective-permute-start.4) | collective-permute-done | bytes 196640 | tf_op jit(solution)/shard_map/ppermute | solution.py:349
  61.0 2.6 %collective-permute-done.6.refs_7_ = f32[3,2,4,16,128]{4,3,2,1,0:T(8,128)} collective-permute-done((f32[3,2,4,16,128]{4,3,2,1,0:T(8,128)}, f32[3,2,4,16,128]{4,3,2,1,0:T(8,128)}, u32[]{:S(2)}, u32[]{:S(2)}) %collective-permute-start.6) | collective-permute-done | bytes 196640 | tf_op jit(solution)/shard_map/ppermute | solution.py:349
  63.6 1.7 collective-permute-start.11
  65.2 8.0 %shard_map.116 = (f32[3,2,4,16,128]{4,3,2,1,0:T(8,128)}, f32[3,2,4,16,128]{4,3,2,1,0:T(8,128)}, f32[3,2,4,16,128]{4,3,2,1,0:T(8,128)}, f32[3,2,4,16,128]{4,3,2,1...) custom-call(f32[3,2,4,16,128]{4,3,2,1,0:T(8,128)} %get-tuple-element, ...), custom_call_target="tpu_custom_call" | custom-call | tf_op jit(solution)/shard_map/pallas_call | solution.py:399
  74.6 2.3 %collective-permute-start.13 = (f32[3,2,4,16,128]{4,3,2,1,0:T(8,128)}, f32[3,2,4,16,128]{4,3,2,1,0:T(8,128)}, u32[]{:S(2)}, u32[]{:S(2)}) collective-permute-start(f32[3,2,4,16,128]{4,3,2,1,0:T(8,128)} %get-tuple-element.62), channel_id=1, source_target_pairs={{0,7},{1,6},{2,5},{3,4},{4,3},{5,2},{6,1},{7,0},{8,15},{9,14},{10,... | collective-permute-start | bytes 589832 | tf_op jit(solution)/shard_map/ppermute | solution.py:349
  77.1 1.9 %collective-permute-start.23 = (f32[3,2,4,16,128]{4,3,2,1,0:T(8,128)}, f32[3,2,4,16,128]{4,3,2,1,0:T(8,128)}, u32[]{:S(2)}, u32[]{:S(2)}) collective-permute-start(f32[3,2,4,16,128]{4,3,2,1,0:T(8,128)} %get-tuple-element.73), channel_id=1, source_target_pairs={{0,3},{1,2},{2,1},{3,0},{4,7},{5,6},{6,5},{7,4},{8,11},{9,10},{10,... | collective-permute-start | bytes 589832 | tf_op jit(solution)/shard_map/ppermute | solution.py:349
  79.0 1.6 collective-permute-done.12.refs_6_
  80.7 1.3 collective-permute-start.24
  82.0 3.7 %collective-permute-done.13.refs_7_ = f32[3,2,4,16,128]{4,3,2,1,0:T(8,128)} collective-permute-done((f32[3,2,4,16,128]{4,3,2,1,0:T(8,128)}, f32[3,2,4,16,128]{4,3,2,1,0:T(8,128)}, u32[]{:S(2)}, u32[]{:S(2)}) %collective-permute-start.13) | collective-permute-done | bytes 196640 | tf_op jit(solution)/shard_map/ppermute | solution.py:349
  86.5 1.8 collective-permute-start.26
  88.3 1.7 collective-permute-start.27
  90.0 8.0 %shard_map.117 = (f32[3,2,4,16,128]{4,3,2,1,0:T(8,128)}, f32[3,2,4,16,128]{4,3,2,1,0:T(8,128)}, f32[3,2,4,16,128]{4,3,2,1,0:T(8,128)}, f32[3,2,4,16,128]{4,3,2,1...) custom-call(f32[3,2,4,16,128]{4,3,2,1,0:T(8,128)} %get-tuple-element, ...), custom_call_target="tpu_custom_call" | custom-call | tf_op jit(solution)/shard_map/pallas_call | solution.py:399
  98.1 3.4 %collective-permute-done.26.refs_6_ = f32[3,2,4,16,128]{4,3,2,1,0:T(8,128)} collective-permute-done((f32[3,2,4,16,128]{4,3,2,1,0:T(8,128)}, f32[3,2,4,16,128]{4,3,2,1,0:T(8,128)}, u32[]{:S(2)}, u32[]{:S(2)}) %collective-permute-start.26) | collective-permute-done | bytes 196640 | tf_op jit(solution)/shard_map/ppermute | solution.py:349
  101.5 4.2 %collective-permute-done.27.refs_7_ = f32[3,2,4,16,128]{4,3,2,1,0:T(8,128)} collective-permute-done((f32[3,2,4,16,128]{4,3,2,1,0:T(8,128)}, f32[3,2,4,16,128]{4,3,2,1,0:T(8,128)}, u32[]{:S(2)}, u32[]{:S(2)}) %collective-permute-start.27) | collective-permute-done | bytes 196640 | tf_op jit(solution)/shard_map/ppermute | solution.py:349
  105.7 4.8 %shard_map.119 = f32[16,3,2,2,8,128]{5,4,3,2,1,0:T(8,128)} custom-call(f32[3,2,4,16,128]{4,3,2,1,0:T(8,128)} %get-tuple-element.63.refs_0_._, s32[1]{0:T(128)} %bitcast.me_ref, bf16[128,512]{1,0:T(8,128)(2,1)} %bitcast.16, bf16[128,512]{1,0:T(8,128)(2,1)} %bitcast.20, f32[3,2,4,16,128]{4,3,2,1,0:T(8,128)} %get-tuple-element.55._.refs_0_, ...), custom_call_target="tpu_custom_call" | custom-call | tf_op jit(solution)/shard_map/pallas_call | solution.py:428
  110.5 6.8 %all-to-all-start.3 = ((f32[16,3,2,2,8,128]{5,4,3,2,1,0:T(8,128)}), f32[16,3,2,2,8,128]{5,4,3,2,1,0:T(8,128)}, u32[]{:S(2)}, u32[]{:S(2)}) async-start(f32[16,3,2,2,8,128]{5,4,3,2,1,0:T(8,128)} %shard_map.119), calls=%async_computation.3 | async-start | bytes 1572864 | tf_op jit(solution)/shard_map/all_to_all | solution.py:354
  118.1 1.7 collective-permute-start.16
  119.8 1.4 collective-permute-start.17
  121.2 1.8 collective-permute-start.18
  123.1 1.9 collective-permute-start.19
  125.7 2.8 %collective-permute-start.20 = (f32[3,2,4,16,128]{4,3,2,1,0:T(8,128)}, f32[3,2,4,16,128]{4,3,2,1,0:T(8,128)}, u32[]{:S(2)}, u32[]{:S(2)}) collective-permute-start(f32[3,2,4,16,128]{4,3,2,1,0:T(8,128)} %get-tuple-element.70), channel_id=1, source_target_pairs={{0,7},{1,6},{2,5},{3,4},{4,3},{5,2},{6,1},{7,0},{8,15},{9,14},{10,... | collective-permute-start | bytes 589832 | tf_op jit(solution)/shard_map/ppermute | solution.py:349
  128.4 1.5 collective-permute-done.16.refs_3_
  129.9 4.7 %collective-permute-done.17.refs_4_ = f32[3,2,4,16,128]{4,3,2,1,0:T(8,128)} collective-permute-done((f32[3,2,4,16,128]{4,3,2,1,0:T(8,128)}, f32[3,2,4,16,128]{4,3,2,1,0:T(8,128)}, u32[]{:S(2)}, u32[]{:S(2)}) %collective-permute-start.17) | collective-permute-done | bytes 196640 | tf_op jit(solution)/shard_map/ppermute | solution.py:349
  134.6 4.5 %collective-permute-done.18.refs_5_ = f32[3,2,4,16,128]{4,3,2,1,0:T(8,128)} collective-permute-done((f32[3,2,4,16,128]{4,3,2,1,0:T(8,128)}, f32[3,2,4,16,128]{4,3,2,1,0:T(8,128)}, u32[]{:S(2)}, u32[]{:S(2)}) %collective-permute-start.18) | collective-permute-done | bytes 196640 | tf_op jit(solution)/shard_map/ppermute | solution.py:349
  139.2 4.7 %collective-permute-done.20.refs_7_ = f32[3,2,4,16,128]{4,3,2,1,0:T(8,128)} collective-permute-done((f32[3,2,4,16,128]{4,3,2,1,0:T(8,128)}, f32[3,2,4,16,128]{4,3,2,1,0:T(8,128)}, u32[]{:S(2)}, u32[]{:S(2)}) %collective-permute-start.20) | collective-permute-done | bytes 196640 | tf_op jit(solution)/shard_map/ppermute | solution.py:349
  143.9 4.8 %shard_map.118 = f32[16,3,2,2,8,128]{5,4,3,2,1,0:T(8,128)} custom-call(f32[3,2,4,16,128]{4,3,2,1,0:T(8,128)} %get-tuple-element.55._.refs_0_, s32[1]{0:T(128)} %bitcast.me_ref, bf16[128,512]{1,0:T(8,128)(2,1)} %bitcast.17, bf16[128,512]{1,0:T(8,128)(2,1)} %bitcast.21, f32[3,2,4,16,128]{4,3,2,1,0:T(8,128)} %get-tuple-element.63.refs_0_._, ...), custom_call_target="tpu_custom_call" | custom-call | tf_op jit(solution)/shard_map/pallas_call | solution.py:428
  148.7 6.9 %all-to-all-start.2 = ((f32[16,3,2,2,8,128]{5,4,3,2,1,0:T(8,128)}), f32[16,3,2,2,8,128]{5,4,3,2,1,0:T(8,128)}, u32[]{:S(2)}, u32[]{:S(2)}) async-start(f32[16,3,2,2,8,128]{5,4,3,2,1,0:T(8,128)} %shard_map.118), calls=%async_computation.2 | async-start | bytes 1572864 | tf_op jit(solution)/shard_map/all_to_all | solution.py:354
  155.7 1.9 copy-done
  157.5 2.0 %shard_map.121.g_ref = f32[1,128]{1,0:T(1,128)S(1)} custom-call(f32[4,2,3,16,8,256]{5,4,3,2,1,0:T(8,128)S(1)} %copy-done), custom_call_target="tpu_custom_call" | custom-call | tf_op jit(solution)/shard_map/pallas_call | solution.py:430
  159.6 4.3 %shard_map.120 = (f32[2,3,576,8,256]{4,3,2,1,0:T(8,128)}, bf16[216,256,256]{2,1,0:T(8,128)(2,1)}) custom-call(f32[16,3,2,2,8,128]{5,4,3,2,1,0:T(8,128)} %all-to-all-done.3.x_ref, bf16[256,512]{1,0:T(8,128)(2,1)S(1)} %copy-done.5, bf16[256,512]{1,0:T(8,128)(2,1)S(1)} %copy-done.4, bf16[256,512]{1,0:T(8,128)(2,1)S(1)} %copy-done.3, ...), custom_call_target="tpu_custom_call" | custom-call | tf_op jit(solution)/shard_map/pallas_call | solution.py:433
  164.0 4.4 %all-to-all-done.2.x_ref = f32[16,3,2,2,8,128]{5,4,3,2,1,0:T(8,128)} async-done(((f32[16,3,2,2,8,128]{5,4,3,2,1,0:T(8,128)}), f32[16,3,2,2,8,128]{5,4,3,2,1,0:T(8,128)}, u32[]{:S(2)}, u32[]{:S(2)}) %all-to-all-start.2) | async-done | bytes 786464 | tf_op jit(solution)/shard_map/all_to_all | solution.py:354
  168.4 4.4 %shard_map.122 = (f32[2,3,16,8,256]{4,3,2,1,0:T(8,128)S(1)}, f32[128,128]{1,0:T(8,128)S(1)}) custom-call(f32[16,3,2,2,8,128]{5,4,3,2,1,0:T(8,128)} %all-to-all-done.2.x_ref, bf16[216,256,256]{2,1,0:T(8,128)(2,1)} %get-tuple-element.78.t_ref, f32[2,3,576,8,256]{4,3,2,1,0:T(8,128)} %get-tuple-element.79.p_ref, f32[4,2,3,16,8,256]{5,4,3,2,1,0:T(8,128)S(1)} %copy-done.1, ...), custom_call_target="tpu_custom_call" | custom-call | tf_op jit(solution)/shard_map/pallas_call | solution.py:442
  172.7 16.9 %all_to_all.25 = f32[128,1,128]{2,1,0:T(1,128)S(1)} all-to-all(f32[128,1,128]{2,1,0:T(1,128)S(1)} %bitcast.12), channel_id=1, replica_groups=mesh['row_0'=4,'row_1'=4,'col_0'=4,'col_1'=2] {'row_0','row_1','col_0','..., dimensions={0} | all-to-all | bytes 131072 | tf_op jit(solution)/shard_map/all_to_all | solution.py:452
  189.6 3.1 %shard_map.123 = (f32[2,3,16,8,256]{4,3,2,1,0:T(8,128)}, f32[2,2,4]{2,1,0:T(2,128)}, f32[2,2]{1,0:T(2,128)}) custom-call(f32[128,128]{1,0:T(8,128)S(1)} %bitcast.11, f32[2,3,16,8,256]{4,3,2,1,0:T(8,128)S(1)} %get-tuple-element.81.img_ref, f32[4,2,3,16,8,256]{5,4,3,2,1,0:T(8,128)S(1)} %copy-done.1), custom_call_target="tpu_custom_call" | custom-call | tf_op jit(solution)/shard_map/pallas_call | solution.py:453
  (61 shorter events, 7.9 us)
Async XLA Ops:
  4.9 21.3 %all-to-all-start.1 = ((f32[16,3,2,2,8,128]{5,4,3,2,1,0:T(8,128)}), f32[16,3,2,2,8,128]{5,4,3,2,1,0:T(8,128)}, u32[]{:S(2)}, u32[]{:S(2)}) async-start(f32[16,3,2,2,8,128]{5,4,3,2,1,0:T(8,128)} %shard_map.112.refs_1_), calls=%async_computation.1 | async-start | bytes 1572864 | tf_op jit(solution)/shard_map/all_to_all | solution.py:354
  26.2 22.3 %all-to-all-start = ((f32[16,3,2,2,8,128]{5,4,3,2,1,0:T(8,128)}), f32[16,3,2,2,8,128]{5,4,3,2,1,0:T(8,128)}, u32[]{:S(2)}, u32[]{:S(2)}) async-start(f32[16,3,2,2,8,128]{5,4,3,2,1,0:T(8,128)} %shard_map.113), calls=%async_computation | async-start | bytes 1572864 | tf_op jit(solution)/shard_map/all_to_all | solution.py:354
  35.7 7.0 %collective-permute-start = (f32[3,2,4,16,128]{4,3,2,1,0:T(8,128)}, f32[3,2,4,16,128]{4,3,2,1,0:T(8,128)}, u32[]{:S(2)}, u32[]{:S(2)}) collective-permute-start(f32[3,2,4,16,128]{4,3,2,1,0:T(8,128)} %get-tuple-element.48), channel_id=1, source_target_pairs={{0,1},{1,0},{2,3},{3,2},{4,5},{5,4},{6,7},{7,6},{8,9},{9,8},{10,11... | collective-permute-start | bytes 589832 | tf_op jit(solution)/shard_map/ppermute | solution.py:349
  37.7 7.7 %collective-permute-start.1 = (f32[3,2,4,16,128]{4,3,2,1,0:T(8,128)}, f32[3,2,4,16,128]{4,3,2,1,0:T(8,128)}, u32[]{:S(2)}, u32[]{:S(2)}) collective-permute-start(f32[3,2,4,16,128]{4,3,2,1,0:T(8,128)} %get-tuple-element.49), channel_id=1, source_target_pairs={{0,2},{1,3},{2,0},{3,1},{4,6},{5,7},{6,4},{7,5},{8,10},{9,11},{10,... | collective-permute-start | bytes 589832 | tf_op jit(solution)/shard_map/ppermute | solution.py:349
  39.0 14.1 %collective-permute-start.2 = (f32[3,2,4,16,128]{4,3,2,1,0:T(8,128)}, f32[3,2,4,16,128]{4,3,2,1,0:T(8,128)S(1)}, u32[]{:S(2)}, u32[]{:S(2)}) collective-permute-start(f32[3,2,4,16,128]{4,3,2,1,0:T(8,128)} %get-tuple-element.50), channel_id=1, source_target_pairs={{0,3},{1,2},{2,1},{3,0},{4,7},{5,6},{6,5},{7,4},{8,11},{9,10},{10,... | collective-permute-start | bytes 589832 | tf_op jit(solution)/shard_map/ppermute | solution.py:349
  39.4 15.8 %collective-permute-start.3 = (f32[3,2,4,16,128]{4,3,2,1,0:T(8,128)}, f32[3,2,4,16,128]{4,3,2,1,0:T(8,128)S(1)}, u32[]{:S(2)}, u32[]{:S(2)}) collective-permute-start(f32[3,2,4,16,128]{4,3,2,1,0:T(8,128)} %get-tuple-element.51), channel_id=1, source_target_pairs={{0,4},{1,5},{2,6},{3,7},{4,0},{5,1},{6,2},{7,3},{8,12},{9,13},{10,... | collective-permute-start | bytes 589832 | tf_op jit(solution)/shard_map/ppermute | solution.py:349
  42.4 18.0 %collective-permute-start.4 = (f32[3,2,4,16,128]{4,3,2,1,0:T(8,128)}, f32[3,2,4,16,128]{4,3,2,1,0:T(8,128)}, u32[]{:S(2)}, u32[]{:S(2)}) collective-permute-start(f32[3,2,4,16,128]{4,3,2,1,0:T(8,128)} %get-tuple-element.52), channel_id=1, source_target_pairs={{0,5},{1,4},{2,7},{3,6},{4,1},{5,0},{6,3},{7,2},{8,13},{9,12},{10,... | collective-permute-start | bytes 589832 | tf_op jit(solution)/shard_map/ppermute | solution.py:349
  42.7 17.6 %collective-permute-start.5 = (f32[3,2,4,16,128]{4,3,2,1,0:T(8,128)}, f32[3,2,4,16,128]{4,3,2,1,0:T(8,128)}, u32[]{:S(2)}, u32[]{:S(2)}) collective-permute-start(f32[3,2,4,16,128]{4,3,2,1,0:T(8,128)} %get-tuple-element.53), channel_id=1, source_target_pairs={{0,6},{1,7},{2,4},{3,5},{4,2},{5,3},{6,0},{7,1},{8,14},{9,15},{10,... | collective-permute-start | bytes 589832 | tf_op jit(solution)/shard_map/ppermute | solution.py:349
  45.5 18.1 %collective-permute-start.6 = (f32[3,2,4,16,128]{4,3,2,1,0:T(8,128)}, f32[3,2,4,16,128]{4,3,2,1,0:T(8,128)}, u32[]{:S(2)}, u32[]{:S(2)}) collective-permute-start(f32[3,2,4,16,128]{4,3,2,1,0:T(8,128)} %get-tuple-element.54), channel_id=1, source_target_pairs={{0,7},{1,6},{2,5},{3,4},{4,3},{5,2},{6,1},{7,0},{8,15},{9,14},{10,... | collective-permute-start | bytes 589832 | tf_op jit(solution)/shard_map/ppermute | solution.py:349
  53.1 0.7 copy-start.9
  53.8 19.5 %collective-permute-start.7 = (f32[3,2,4,16,128]{4,3,2,1,0:T(8,128)}, f32[3,2,4,16,128]{4,3,2,1,0:T(8,128)S(1)}, u32[]{:S(2)}, u32[]{:S(2)}) collective-permute-start(f32[3,2,4,16,128]{4,3,2,1,0:T(8,128)} %get-tuple-element.56), channel_id=1, source_target_pairs={{0,1},{1,0},{2,3},{3,2},{4,5},{5,4},{6,7},{7,6},{8,9},{9,8},{10,11... | collective-permute-start | bytes 589832 | tf_op jit(solution)/shard_map/ppermute | solution.py:349
  55.2 0.7 copy-start.10
  55.9 18.7 %collective-permute-start.8 = (f32[3,2,4,16,128]{4,3,2,1,0:T(8,128)}, f32[3,2,4,16,128]{4,3,2,1,0:T(8,128)S(1)}, u32[]{:S(2)}, u32[]{:S(2)}) collective-permute-start(f32[3,2,4,16,128]{4,3,2,1,0:T(8,128)} %get-tuple-element.57), channel_id=1, source_target_pairs={{0,2},{1,3},{2,0},{3,1},{4,6},{5,7},{6,4},{7,5},{8,10},{9,11},{10,... | collective-permute-start | bytes 589832 | tf_op jit(solution)/shard_map/ppermute | solution.py:349
  60.4 16.5 %collective-permute-start.9 = (f32[3,2,4,16,128]{4,3,2,1,0:T(8,128)}, f32[3,2,4,16,128]{4,3,2,1,0:T(8,128)}, u32[]{:S(2)}, u32[]{:S(2)}) collective-permute-start(f32[3,2,4,16,128]{4,3,2,1,0:T(8,128)} %get-tuple-element.58), channel_id=1, source_target_pairs={{0,3},{1,2},{2,1},{3,0},{4,7},{5,6},{6,5},{7,4},{8,11},{9,10},{10,... | collective-permute-start | bytes 589832 | tf_op jit(solution)/shard_map/ppermute | solution.py:349
  60.4 16.5 %collective-permute-start.10 = (f32[3,2,4,16,128]{4,3,2,1,0:T(8,128)}, f32[3,2,4,16,128]{4,3,2,1,0:T(8,128)}, u32[]{:S(2)}, u32[]{:S(2)}) collective-permute-start(f32[3,2,4,16,128]{4,3,2,1,0:T(8,128)} %get-tuple-element.59), channel_id=1, source_target_pairs={{0,4},{1,5},{2,6},{3,7},{4,0},{5,1},{6,2},{7,3},{8,12},{9,13},{10,... | collective-permute-start | bytes 589832 | tf_op jit(solution)/shard_map/ppermute | solution.py:349
  63.6 13.5 %collective-permute-start.11 = (f32[3,2,4,16,128]{4,3,2,1,0:T(8,128)}, f32[3,2,4,16,128]{4,3,2,1,0:T(8,128)}, u32[]{:S(2)}, u32[]{:S(2)}) collective-permute-start(f32[3,2,4,16,128]{4,3,2,1,0:T(8,128)} %get-tuple-element.60), channel_id=1, source_target_pairs={{0,5},{1,4},{2,7},{3,6},{4,1},{5,0},{6,3},{7,2},{8,13},{9,12},{10,... | collective-permute-start | bytes 589832 | tf_op jit(solution)/shard_map/ppermute | solution.py:349
  73.3 16.7 %copy-start.7 = (f32[3,2,4,16,128]{4,3,2,1,0:T(8,128)}, f32[3,2,4,16,128]{4,3,2,1,0:T(8,128)S(1)}, u32[]{:S(2)}) copy-start(f32[3,2,4,16,128]{4,3,2,1,0:T(8,128)S(1)} %collective-permute-done.7.refs_1_) | copy-start | bytes 589828
  73.3 7.4 %collective-permute-start.12 = (f32[3,2,4,16,128]{4,3,2,1,0:T(8,128)}, f32[3,2,4,16,128]{4,3,2,1,0:T(8,128)}, u32[]{:S(2)}, u32[]{:S(2)}) collective-permute-start(f32[3,2,4,16,128]{4,3,2,1,0:T(8,128)} %get-tuple-element.61), channel_id=1, source_target_pairs={{0,6},{1,7},{2,4},{3,5},{4,2},{5,3},{6,0},{7,1},{8,14},{9,15},{10,... | collective-permute-start | bytes 589832 | tf_op jit(solution)/shard_map/ppermute | solution.py:349
  74.6 15.4 %copy-start.8 = (f32[3,2,4,16,128]{4,3,2,1,0:T(8,128)}, f32[3,2,4,16,128]{4,3,2,1,0:T(8,128)S(1)}, u32[]{:S(2)}) copy-start(f32[3,2,4,16,128]{4,3,2,1,0:T(8,128)S(1)} %collective-permute-done.8.refs_2_) | copy-start | bytes 589828
  74.6 11.1 %collective-permute-start.13 = (f32[3,2,4,16,128]{4,3,2,1,0:T(8,128)}, f32[3,2,4,16,128]{4,3,2,1,0:T(8,128)}, u32[]{:S(2)}, u32[]{:S(2)}) collective-permute-start(f32[3,2,4,16,128]{4,3,2,1,0:T(8,128)} %get-tuple-element.62), channel_id=1, source_target_pairs={{0,7},{1,6},{2,5},{3,4},{4,3},{5,2},{6,1},{7,0},{8,15},{9,14},{10,... | collective-permute-start | bytes 589832 | tf_op jit(solution)/shard_map/ppermute | solution.py:349
  76.9 9.6 %collective-permute-start.21 = (f32[3,2,4,16,128]{4,3,2,1,0:T(8,128)}, f32[3,2,4,16,128]{4,3,2,1,0:T(8,128)}, u32[]{:S(2)}, u32[]{:S(2)}) collective-permute-start(f32[3,2,4,16,128]{4,3,2,1,0:T(8,128)} %get-tuple-element.71), channel_id=1, source_target_pairs={{0,1},{1,0},{2,3},{3,2},{4,5},{5,4},{6,7},{7,6},{8,9},{9,8},{10,11... | collective-permute-start | bytes 589832 | tf_op jit(solution)/shard_map/ppermute | solution.py:349
  76.9 11.4 %collective-permute-start.22 = (f32[3,2,4,16,128]{4,3,2,1,0:T(8,128)}, f32[3,2,4,16,128]{4,3,2,1,0:T(8,128)}, u32[]{:S(2)}, u32[]{:S(2)}) collective-permute-start(f32[3,2,4,16,128]{4,3,2,1,0:T(8,128)} %get-tuple-element.72), channel_id=1, source_target_pairs={{0,2},{1,3},{2,0},{3,1},{4,6},{5,7},{6,4},{7,5},{8,10},{9,11},{10,... | collective-permute-start | bytes 589832 | tf_op jit(solution)/shard_map/ppermute | solution.py:349
  77.1 21.0 %collective-permute-start.23 = (f32[3,2,4,16,128]{4,3,2,1,0:T(8,128)}, f32[3,2,4,16,128]{4,3,2,1,0:T(8,128)}, u32[]{:S(2)}, u32[]{:S(2)}) collective-permute-start(f32[3,2,4,16,128]{4,3,2,1,0:T(8,128)} %get-tuple-element.73), channel_id=1, source_target_pairs={{0,3},{1,2},{2,1},{3,0},{4,7},{5,6},{6,5},{7,4},{8,11},{9,10},{10,... | collective-permute-start | bytes 589832 | tf_op jit(solution)/shard_map/ppermute | solution.py:349
  80.7 17.4 %collective-permute-start.24 = (f32[3,2,4,16,128]{4,3,2,1,0:T(8,128)}, f32[3,2,4,16,128]{4,3,2,1,0:T(8,128)}, u32[]{:S(2)}, u32[]{:S(2)}) collective-permute-start(f32[3,2,4,16,128]{4,3,2,1,0:T(8,128)} %get-tuple-element.74), channel_id=1, source_target_pairs={{0,4},{1,5},{2,6},{3,7},{4,0},{5,1},{6,2},{7,3},{8,12},{9,13},{10,... | collective-permute-start | bytes 589832 | tf_op jit(solution)/shard_map/ppermute | solution.py:349
  85.7 12.3 %collective-permute-start.25 = (f32[3,2,4,16,128]{4,3,2,1,0:T(8,128)}, f32[3,2,4,16,128]{4,3,2,1,0:T(8,128)}, u32[]{:S(2)}, u32[]{:S(2)}) collective-permute-start(f32[3,2,4,16,128]{4,3,2,1,0:T(8,128)} %get-tuple-element.75), channel_id=1, source_target_pairs={{0,5},{1,4},{2,7},{3,6},{4,1},{5,0},{6,3},{7,2},{8,13},{9,12},{10,... | collective-permute-start | bytes 589832 | tf_op jit(solution)/shard_map/ppermute | solution.py:349
  86.5 15.0 %collective-permute-start.26 = (f32[3,2,4,16,128]{4,3,2,1,0:T(8,128)}, f32[3,2,4,16,128]{4,3,2,1,0:T(8,128)}, u32[]{:S(2)}, u32[]{:S(2)}) collective-permute-start(f32[3,2,4,16,128]{4,3,2,1,0:T(8,128)} %get-tuple-element.76), channel_id=1, source_target_pairs={{0,6},{1,7},{2,4},{3,5},{4,2},{5,3},{6,0},{7,1},{8,14},{9,15},{10,... | collective-permute-start | bytes 589832 | tf_op jit(solution)/shard_map/ppermute | solution.py:349
  88.3 17.4 %collective-permute-start.27 = (f32[3,2,4,16,128]{4,3,2,1,0:T(8,128)}, f32[3,2,4,16,128]{4,3,2,1,0:T(8,128)}, u32[]{:S(2)}, u32[]{:S(2)}) collective-permute-start(f32[3,2,4,16,128]{4,3,2,1,0:T(8,128)} %get-tuple-element.77), channel_id=1, source_target_pairs={{0,7},{1,6},{2,5},{3,4},{4,3},{5,2},{6,1},{7,0},{8,15},{9,14},{10,... | collective-permute-start | bytes 589832 | tf_op jit(solution)/shard_map/ppermute | solution.py:349
  98.0 19.3 %copy-start.14 = (f32[3,2,4,16,128]{4,3,2,1,0:T(8,128)S(1)}, f32[3,2,4,16,128]{4,3,2,1,0:T(8,128)}, u32[]{:S(2)}) copy-start(f32[3,2,4,16,128]{4,3,2,1,0:T(8,128)} %get-tuple-element.64) | copy-start | bytes 589828
  98.0 20.1 %copy-start.13 = (f32[3,2,4,16,128]{4,3,2,1,0:T(8,128)S(1)}, f32[3,2,4,16,128]{4,3,2,1,0:T(8,128)}, u32[]{:S(2)}) copy-start(f32[3,2,4,16,128]{4,3,2,1,0:T(8,128)} %get-tuple-element.65) | copy-start | bytes 589828
  110.5 38.2 %all-to-all-start.3 = ((f32[16,3,2,2,8,128]{5,4,3,2,1,0:T(8,128)}), f32[16,3,2,2,8,128]{5,4,3,2,1,0:T(8,128)}, u32[]{:S(2)}, u32[]{:S(2)}) async-start(f32[16,3,2,2,8,128]{5,4,3,2,1,0:T(8,128)} %shard_map.119), calls=%async_computation.3 | async-start | bytes 1572864 | tf_op jit(solution)/shard_map/all_to_all | solution.py:354
  117.3 5.8 %collective-permute-start.14 = (f32[3,2,4,16,128]{4,3,2,1,0:T(8,128)S(1)}, f32[3,2,4,16,128]{4,3,2,1,0:T(8,128)S(1)}, u32[]{:S(2)}, u32[]{:S(2)}) collective-permute-start(f32[3,2,4,16,128]{4,3,2,1,0:T(8,128)S(1)} %copy-done.14), channel_id=1, source_target_pairs={{0,1},{1,0},{2,3},{3,2},{4,5},{5,4},{6,7},{7,6},{8,9},{9,8},{10,11... | collective-permute-start | bytes 589832 | tf_op jit(solution)/shard_map/ppermute | solution.py:349
  118.1 6.9 %collective-permute-start.15 = (f32[3,2,4,16,128]{4,3,2,1,0:T(8,128)S(1)}, f32[3,2,4,16,128]{4,3,2,1,0:T(8,128)S(1)}, u32[]{:S(2)}, u32[]{:S(2)}) collective-permute-start(f32[3,2,4,16,128]{4,3,2,1,0:T(8,128)S(1)} %copy-done.13), channel_id=1, source_target_pairs={{0,2},{1,3},{2,0},{3,1},{4,6},{5,7},{6,4},{7,5},{8,10},{9,11},{10,... | collective-permute-start | bytes 589832 | tf_op jit(solution)/shard_map/ppermute | solution.py:349
  118.1 11.8 %collective-permute-start.16 = (f32[3,2,4,16,128]{4,3,2,1,0:T(8,128)}, f32[3,2,4,16,128]{4,3,2,1,0:T(8,128)}, u32[]{:S(2)}, u32[]{:S(2)}) collective-permute-start(f32[3,2,4,16,128]{4,3,2,1,0:T(8,128)} %get-tuple-element.66), channel_id=1, source_target_pairs={{0,3},{1,2},{2,1},{3,0},{4,7},{5,6},{6,5},{7,4},{8,11},{9,10},{10,... | collective-permute-start | bytes 589832 | tf_op jit(solution)/shard_map/ppermute | solution.py:349
  119.8 14.8 %collective-permute-start.17 = (f32[3,2,4,16,128]{4,3,2,1,0:T(8,128)}, f32[3,2,4,16,128]{4,3,2,1,0:T(8,128)}, u32[]{:S(2)}, u32[]{:S(2)}) collective-permute-start(f32[3,2,4,16,128]{4,3,2,1,0:T(8,128)} %get-tuple-element.67), channel_id=1, source_target_pairs={{0,4},{1,5},{2,6},{3,7},{4,0},{5,1},{6,2},{7,3},{8,12},{9,13},{10,... | collective-permute-start | bytes 589832 | tf_op jit(solution)/shard_map/ppermute | solution.py:349
  121.2 17.9 %collective-permute-start.18 = (f32[3,2,4,16,128]{4,3,2,1,0:T(8,128)}, f32[3,2,4,16,128]{4,3,2,1,0:T(8,128)}, u32[]{:S(2)}, u32[]{:S(2)}) collective-permute-start(f32[3,2,4,16,128]{4,3,2,1,0:T(8,128)} %get-tuple-element.68), channel_id=1, source_target_pairs={{0,5},{1,4},{2,7},{3,6},{4,1},{5,0},{6,3},{7,2},{8,13},{9,12},{10,... | collective-permute-start | bytes 589832 | tf_op jit(solution)/shard_map/ppermute | solution.py:349
  123.1 1.9 copy-start.11
  123.1 16.1 %collective-permute-start.19 = (f32[3,2,4,16,128]{4,3,2,1,0:T(8,128)}, f32[3,2,4,16,128]{4,3,2,1,0:T(8,128)}, u32[]{:S(2)}, u32[]{:S(2)}) collective-permute-start(f32[3,2,4,16,128]{4,3,2,1,0:T(8,128)} %get-tuple-element.69), channel_id=1, source_target_pairs={{0,6},{1,7},{2,4},{3,5},{4,2},{5,3},{6,0},{7,1},{8,14},{9,15},{10,... | collective-permute-start | bytes 589832 | tf_op jit(solution)/shard_map/ppermute | solution.py:349
  125.0 0.7 copy-start.12
  125.7 33.9 %copy-start.2 = (bf16[256,512]{1,0:T(8,128)(2,1)S(1)}, bf16[256,512]{1,0:T(8,128)(2,1)}, u32[]{:S(2)}) copy-start(bf16[256,512]{1,0:T(8,128)(2,1)} %constant.25.clone.refs_4_.refs_6_.sl_ref.refs_3_) | copy-start | bytes 786436
  125.7 33.9 %copy-start.6 = (f32[16,8,256]{2,1,0:T(8,128)S(1)}, f32[16,8,256]{2,1,0:T(8,128)}, u32[]{:S(2)}) copy-start(f32[16,8,256]{2,1,0:T(8,128)} %chi_ref.1) | copy-start | bytes 393220
  125.7 18.2 %collective-permute-start.20 = (f32[3,2,4,16,128]{4,3,2,1,0:T(8,128)}, f32[3,2,4,16,128]{4,3,2,1,0:T(8,128)}, u32[]{:S(2)}, u32[]{:S(2)}) collective-permute-start(f32[3,2,4,16,128]{4,3,2,1,0:T(8,128)} %get-tuple-element.70), channel_id=1, source_target_pairs={{0,7},{1,6},{2,5},{3,4},{4,3},{5,2},{6,1},{7,0},{8,15},{9,14},{10,... | collective-permute-start | bytes 589832 | tf_op jit(solution)/shard_map/ppermute | solution.py:349
  148.7 19.7 %all-to-all-start.2 = ((f32[16,3,2,2,8,128]{5,4,3,2,1,0:T(8,128)}), f32[16,3,2,2,8,128]{5,4,3,2,1,0:T(8,128)}, u32[]{:S(2)}, u32[]{:S(2)}) async-start(f32[16,3,2,2,8,128]{5,4,3,2,1,0:T(8,128)} %shard_map.118), calls=%async_computation.2 | async-start | bytes 1572864 | tf_op jit(solution)/shard_map/all_to_all | solution.py:354
  155.6 1.9 copy-start
  157.5 2.1 %copy-start.3 = (bf16[256,512]{1,0:T(8,128)(2,1)S(1)}, bf16[256,512]{1,0:T(8,128)(2,1)}, u32[]{:S(2)}) copy-start(bf16[256,512]{1,0:T(8,128)(2,1)} %constant.24.clone.refs_3_.refs_5_.sh_ref.refs_2_) | copy-start | bytes 786436
  157.5 2.1 %copy-start.4 = (bf16[256,512]{1,0:T(8,128)(2,1)S(1)}, bf16[256,512]{1,0:T(8,128)(2,1)}, u32[]{:S(2)}) copy-start(bf16[256,512]{1,0:T(8,128)(2,1)} %constant.23.clone.refs_2_.refs_4_.cl_ref.refs_1_) | copy-start | bytes 786436
  157.5 2.1 %copy-start.5 = (bf16[256,512]{1,0:T(8,128)(2,1)S(1)}, bf16[256,512]{1,0:T(8,128)(2,1)}, u32[]{:S(2)}) copy-start(bf16[256,512]{1,0:T(8,128)(2,1)} %constant.22.clone.refs_1_.refs_3_.ch_ref.refs_0_) | copy-start | bytes 786436
  159.6 8.7 %copy-start.1 = (f32[4,2,3,16,8,256]{5,4,3,2,1,0:T(8,128)S(1)}, f32[4,2,3,16,8,256]{5,4,3,2,1,0:T(8,128)}, u32[]{:S(2)}) copy-start(f32[4,2,3,16,8,256]{5,4,3,2,1,0:T(8,128)} %b_ref.5) | copy-start | bytes 9437188

commit v3 on v2

--- a/solution.py
+++ b/solution.py
@@ -1,3 +1,4 @@
+import functools
 import math
 
 import jax
@@ -100,19 +101,42 @@
     return v
 
 
-def x_forward(*refs):
-    u_ref, ch_ref, cl_ref, sh_ref, sl_ref, o_ref = refs[-6:]
+def x_forward(half, *refs):
+    u_hbm, *t_hbm = refs[-14:-9]
+    o_hbm, u_ref, *t_ref = refs[-9:-3]
+    o_ref, sem_in, sem_out = refs[-3:]
     n = LZ * LY
-    u = jnp.concatenate([u_ref[0, 0, 0].reshape(n, GX), u_ref[0, 1, 0].reshape(n, GX)], axis=0)
-    c = right(u, ch_ref[...], cl_ref[...], 0)
-    s = right(u, sh_ref[...], sl_ref[...], 0)
-    acc = jnp.concatenate([c[:n] + s[n:], c[n:] - s[:n]], axis=0)
-    acc = acc.reshape(2, 2, 8, LY, GX)
-    for t in range(2):
-        part = acc[..., t * 128 : (t + 1) * 128]
-        v = [part[:, :, zi].reshape(4 * LY, 128) for zi in range(8)]
-        for di, w in enumerate(swap_blocks(v, HX)):
-            o_ref[8 * t + di, 0] = w.reshape(2, 2, LY, 128)
+    tables = [
+        pltpu.make_async_copy(t_hbm[i].at[:, pl.ds(half * GX, GX)], t_ref[i], sem_in.at[3 + i]) for i in range(4)
+    ]
+    fetch = lambda c: pltpu.make_async_copy(u_hbm.at[NB - 1, :, c], u_ref.at[c], sem_in.at[c])
+    store = lambda c: pltpu.make_async_copy(o_ref.at[:, c], o_hbm.at[:, c], sem_out.at[c])
+    fetch(0).start()
+    for table in tables:
+        table.start()
+    fetch(1).start()
+    fetch(2).start()
+    for table in tables:
+        table.wait()
+
+    def body(c, carry):
+        fetch(c).wait()
+        u = u_ref[c].reshape(2 * n, GX)
+        cos = right(u, t_ref[0][...], t_ref[1][...], 0)
+        sin = right(u, t_ref[2][...], t_ref[3][...], 0)
+        acc = jnp.concatenate([cos[:n] + sin[n:], cos[n:] - sin[:n]], axis=0)
+        acc = acc.reshape(2, 2, 8, LY, GX)
+        for t in range(2):
+            part = acc[..., t * 128 : (t + 1) * 128]
+            v = [part[:, :, zi].reshape(4 * LY, 128) for zi in range(8)]
+            for di, w in enumerate(swap_blocks(v, HX)):
+                o_ref[8 * t + di, c] = w.reshape(2, 2, LY, 128)
+        store(c).start()
+        return carry
+
+    lax.fori_loop(0, 3, body, 0)
+    for c in range(3):
+        store(c).wait()
 
 
 def y_forward(me_ref, x_ref, th_ref, tl_ref, *refs):
@@ -335,7 +359,7 @@
         out_specs=outs,
         out_shape=shapes,
         scratch_shapes=list(scratch),
-        compiler_params=pltpu.CompilerParams(vmem_limit_bytes=grant, dimension_semantics=("arbitrary",) * len(grid)),
+        compiler_params=pltpu.CompilerParams(vmem_limit_bytes=grant, dimension_semantics=("arbitrary",) * len(grid) or None),
     )
 
 
@@ -377,7 +401,17 @@
     sent = []
     for half in range(2):
         earlier = [green, sent[0]] if half else []
-        kernel = call(x_forward, (3,), [after] * len(earlier) + [latest_spec] + table_specs[half], row_spec, row_shape)
+        kernel = call(
+            functools.partial(x_forward, half),
+            (),
+            [after] * (len(earlier) + 5),
+            after,
+            row_shape,
+            [pltpu.VMEM((3, 2, LZ, LY, GX), F32)]
+            + [pltpu.VMEM((GX, GX), BF16)] * 4
+            + [pltpu.VMEM((NROW, 3, 2, 2, LY, 128), F32)]
+            + [pltpu.SemaphoreType.DMA((7,)), pltpu.SemaphoreType.DMA((3,))],
+        )
         sent.append(kernel(*earlier, krylov_basis, *x_tables))
     rows = [exchange_rows(x) for x in sent]
     back = [t.T for t in lax.optimization_barrier((*side, sent[0]))[:2]]

time: 194 us -> 193 us (level)
  no operation moved by 1% of the time
where the time goes in v3:
time: 193 us; the launch traced here: 192 us
  starting transfers between devices  64 us (33%)
  Pallas kernels  56.3 us (29%)
  waiting for transfers between devices  43.4 us (22%)
  blocking collectives  16.9 us (9%)
  local copies, waits for them, and re-layouts  10.8 us (6%)
    ppermute x28, starting transfers between devices, exchange_cols(): lax.ppermute(blocks[d], COL, [(i, i ^ d) for i in range(NCOL)])  37.2 us
    ppermute x28, waiting for transfers between devices, exchange_cols(): lax.ppermute(blocks[d], COL, [(i, i ^ d) for i in range(NCOL)])  36.9 us
    all_to_all x4, starting transfers between devices, exchange_rows(): return lax.all_to_all(x, ROW, split_axis=0, concat_axis=0, tiled=True)  26.8 us
    all_to_all x1, blocking collectives, per_device(): lax.all_to_all(everyone, ROW_COL, split_axis=0, concat_axis=0, tiled=True)  16.9 us
    pallas_call x2, Pallas kernels, per_device(): call(z_both, (4 // nk,), [after, smem, pl.BlockSpec((6, 2 * GZ, nk * 128)...  16 us
    pallas_call x2, Pallas kernels, per_device(): sent.append(kernel(mixed[1 - half][0], me, *back, *cols[half]))  9.59 us
    pallas_call x2, Pallas kernels, per_device(): call(y_forward, (3,), [smem, row_spec, whole(side[0].shape), whole(side[1...  9.14 us
    pallas_call x2, Pallas kernels, per_device(): sent.append(kernel(*earlier, krylov_basis, *x_tables))  7.8 us
  transfers between devices with their start and end apart: 32, of which 13 were waited for; matrix products, arithmetic and copies ran while one was open for 4% of the time, Pallas kernels for 21%

profile of v3, /device:TPU:1, one launch (start us, length us, event | category | flops | bytes accessed | tf_op | source)
XLA Modules:
  0.0 192.5 jit_solution(2387407513176626125)
XLA Ops:
  0.6 3.9 %shard_map.112.refs_1_ = f32[16,3,2,2,8,128]{5,4,3,2,1,0:T(8,128)} custom-call(f32[4,2,3,16,8,256]{5,4,3,2,1,0:T(8,128)} %b_ref.5, bf16[256,512]{1,0:T(8,128)(2,1)} %constant.22.clone.refs_1_.refs_3_.ch_ref.refs_0_, bf16[256,512]{1,0:T(8,128)(2,1)} %constant.23.clone.refs_2_.refs_4_.cl_ref.refs_1_, ...), custom_call_target="tpu_custom_call" | custom-call | tf_op jit(solution)/shard_map/pallas_call | solution.py:415
  4.5 8.5 %all-to-all-start.1 = ((f32[16,3,2,2,8,128]{5,4,3,2,1,0:T(8,128)}), f32[16,3,2,2,8,128]{5,4,3,2,1,0:T(8,128)}, u32[]{:S(2)}, u32[]{:S(2)}) async-start(f32[16,3,2,2,8,128]{5,4,3,2,1,0:T(8,128)} %shard_map.112.refs_1_), calls=%async_computation.1 | async-start | bytes 1572864 | tf_op jit(solution)/shard_map/all_to_all | solution.py:378
  13.0 3.8 %copy.33 = bf16[6,256,32,32]{1,2,3,0:T(8,128)(2,1)S(1)} copy(bf16[6,256,32,32]{1,3,2,0:T(8,128)(2,1)} %param.11) | data formatting | bytes 6291456 | tf_op args[2]
  16.8 3.1 %copy.34.refs_0_.g_ref = bf16[6,256,1024]{2,1,0:T(8,128)(2,1)} copy(bf16[6,256,1024]{1,2,0:T(8,128)(2,1)S(1)} %bitcast.13) | data formatting | bytes 6291456 | tf_op jit(solution)/shard_map/reshape | solution.py:397
  19.9 3.9 %shard_map.113 = f32[16,3,2,2,8,128]{5,4,3,2,1,0:T(8,128)} custom-call(bf16[6,256,1024]{2,1,0:T(8,128)(2,1)} %copy.34.refs_0_.g_ref, f32[16,3,2,2,8,128]{5,4,3,2,1,0:T(8,128)} %shard_map.112.refs_1_, f32[4,2,3,16,8,256]{5,4,3,2,1,0:T(8,128)} %b_ref.5, bf16[256,512]{1,0:T(8,128)(2,1)} %constant.22.clone.refs_1_.refs_3_.ch_ref.refs_0_, ...), custom_call_target="tpu_custom_call" | custom-call | tf_op jit(solution)/shard_map/pallas_call | solution.py:415
  23.8 2.1 %all-to-all-done.1.x_ref = f32[16,3,2,2,8,128]{5,4,3,2,1,0:T(8,128)} async-done(((f32[16,3,2,2,8,128]{5,4,3,2,1,0:T(8,128)}), f32[16,3,2,2,8,128]{5,4,3,2,1,0:T(8,128)}, u32[]{:S(2)}, u32[]{:S(2)}) %all-to-all-start.1) | async-done | bytes 786464 | tf_op jit(solution)/shard_map/all_to_all | solution.py:378
  25.9 4.6 %all-to-all-start = ((f32[16,3,2,2,8,128]{5,4,3,2,1,0:T(8,128)}), f32[16,3,2,2,8,128]{5,4,3,2,1,0:T(8,128)}, u32[]{:S(2)}, u32[]{:S(2)}) async-start(f32[16,3,2,2,8,128]{5,4,3,2,1,0:T(8,128)} %shard_map.113), calls=%async_computation | async-start | bytes 1572864 | tf_op jit(solution)/shard_map/all_to_all | solution.py:378
  30.5 4.6 %shard_map.115 = (f32[3,2,4,16,128]{4,3,2,1,0:T(8,128)}, f32[3,2,4,16,128]{4,3,2,1,0:T(8,128)}, f32[3,2,4,16,128]{4,3,2,1,0:T(8,128)}, f32[3,2,4,16,128]{4,3,2,1...) custom-call(s32[1]{0:T(128)} %bitcast.me_ref, ...), custom_call_target="tpu_custom_call" | custom-call | tf_op jit(solution)/shard_map/pallas_call | solution.py:419
  35.0 2.4 %collective-permute-start = (f32[3,2,4,16,128]{4,3,2,1,0:T(8,128)}, f32[3,2,4,16,128]{4,3,2,1,0:T(8,128)}, u32[]{:S(2)}, u32[]{:S(2)}) collective-permute-start(f32[3,2,4,16,128]{4,3,2,1,0:T(8,128)} %get-tuple-element.48), channel_id=1, source_target_pairs={{0,1},{1,0},{2,3},{3,2},{4,5},{5,4},{6,7},{7,6},{8,9},{9,8},{10,11... | collective-permute-start | bytes 589832 | tf_op jit(solution)/shard_map/ppermute | solution.py:373
  39.1 2.9 %collective-permute-start.3 = (f32[3,2,4,16,128]{4,3,2,1,0:T(8,128)}, f32[3,2,4,16,128]{4,3,2,1,0:T(8,128)S(1)}, u32[]{:S(2)}, u32[]{:S(2)}) collective-permute-start(f32[3,2,4,16,128]{4,3,2,1,0:T(8,128)} %get-tuple-element.51), channel_id=1, source_target_pairs={{0,4},{1,5},{2,6},{3,7},{4,0},{5,1},{6,2},{7,3},{8,12},{9,13},{10,... | collective-permute-start | bytes 589832 | tf_op jit(solution)/shard_map/ppermute | solution.py:373
  42.4 2.7 %collective-permute-start.5 = (f32[3,2,4,16,128]{4,3,2,1,0:T(8,128)}, f32[3,2,4,16,128]{4,3,2,1,0:T(8,128)}, u32[]{:S(2)}, u32[]{:S(2)}) collective-permute-start(f32[3,2,4,16,128]{4,3,2,1,0:T(8,128)} %get-tuple-element.53), channel_id=1, source_target_pairs={{0,6},{1,7},{2,4},{3,5},{4,2},{5,3},{6,0},{7,1},{8,14},{9,15},{10,... | collective-permute-start | bytes 589832 | tf_op jit(solution)/shard_map/ppermute | solution.py:373
  45.1 3.1 %collective-permute-start.6 = (f32[3,2,4,16,128]{4,3,2,1,0:T(8,128)}, f32[3,2,4,16,128]{4,3,2,1,0:T(8,128)}, u32[]{:S(2)}, u32[]{:S(2)}) collective-permute-start(f32[3,2,4,16,128]{4,3,2,1,0:T(8,128)} %get-tuple-element.54), channel_id=1, source_target_pairs={{0,7},{1,6},{2,5},{3,4},{4,3},{5,2},{6,1},{7,0},{8,15},{9,14},{10,... | collective-permute-start | bytes 589832 | tf_op jit(solution)/shard_map/ppermute | solution.py:373
  48.2 4.6 %shard_map.114 = (f32[3,2,4,16,128]{4,3,2,1,0:T(8,128)}, f32[3,2,4,16,128]{4,3,2,1,0:T(8,128)}, f32[3,2,4,16,128]{4,3,2,1,0:T(8,128)}, f32[3,2,4,16,128]{4,3,2,1...) custom-call(s32[1]{0:T(128)} %bitcast.me_ref, ...), custom_call_target="tpu_custom_call" | custom-call | tf_op jit(solution)/shard_map/pallas_call | solution.py:419
  53.5 1.4 collective-permute-done.3.refs_4_
  55.6 4.4 %collective-permute-done.4.refs_5_ = f32[3,2,4,16,128]{4,3,2,1,0:T(8,128)} collective-permute-done((f32[3,2,4,16,128]{4,3,2,1,0:T(8,128)}, f32[3,2,4,16,128]{4,3,2,1,0:T(8,128)}, u32[]{:S(2)}, u32[]{:S(2)}) %collective-permute-start.4) | collective-permute-done | bytes 196640 | tf_op jit(solution)/shard_map/ppermute | solution.py:373
  60.7 2.6 %collective-permute-done.6.refs_7_ = f32[3,2,4,16,128]{4,3,2,1,0:T(8,128)} collective-permute-done((f32[3,2,4,16,128]{4,3,2,1,0:T(8,128)}, f32[3,2,4,16,128]{4,3,2,1,0:T(8,128)}, u32[]{:S(2)}, u32[]{:S(2)}) %collective-permute-start.6) | collective-permute-done | bytes 196640 | tf_op jit(solution)/shard_map/ppermute | solution.py:373
  63.2 1.7 collective-permute-start.11
  64.9 8.0 %shard_map.116 = (f32[3,2,4,16,128]{4,3,2,1,0:T(8,128)}, f32[3,2,4,16,128]{4,3,2,1,0:T(8,128)}, f32[3,2,4,16,128]{4,3,2,1,0:T(8,128)}, f32[3,2,4,16,128]{4,3,2,1...) custom-call(f32[3,2,4,16,128]{4,3,2,1,0:T(8,128)} %get-tuple-element, ...), custom_call_target="tpu_custom_call" | custom-call | tf_op jit(solution)/shard_map/pallas_call | solution.py:433
  74.2 2.3 %collective-permute-start.13 = (f32[3,2,4,16,128]{4,3,2,1,0:T(8,128)}, f32[3,2,4,16,128]{4,3,2,1,0:T(8,128)}, u32[]{:S(2)}, u32[]{:S(2)}) collective-permute-start(f32[3,2,4,16,128]{4,3,2,1,0:T(8,128)} %get-tuple-element.62), channel_id=1, source_target_pairs={{0,7},{1,6},{2,5},{3,4},{4,3},{5,2},{6,1},{7,0},{8,15},{9,14},{10,... | collective-permute-start | bytes 589832 | tf_op jit(solution)/shard_map/ppermute | solution.py:373
  76.7 2.0 %collective-permute-start.23 = (f32[3,2,4,16,128]{4,3,2,1,0:T(8,128)}, f32[3,2,4,16,128]{4,3,2,1,0:T(8,128)}, u32[]{:S(2)}, u32[]{:S(2)}) collective-permute-start(f32[3,2,4,16,128]{4,3,2,1,0:T(8,128)} %get-tuple-element.73), channel_id=1, source_target_pairs={{0,3},{1,2},{2,1},{3,0},{4,7},{5,6},{6,5},{7,4},{8,11},{9,10},{10,... | collective-permute-start | bytes 589832 | tf_op jit(solution)/shard_map/ppermute | solution.py:373
  78.7 1.6 collective-permute-done.12.refs_6_
  80.3 1.3 collective-permute-start.24
  81.6 3.8 %collective-permute-done.13.refs_7_ = f32[3,2,4,16,128]{4,3,2,1,0:T(8,128)} collective-permute-done((f32[3,2,4,16,128]{4,3,2,1,0:T(8,128)}, f32[3,2,4,16,128]{4,3,2,1,0:T(8,128)}, u32[]{:S(2)}, u32[]{:S(2)}) %collective-permute-start.13) | collective-permute-done | bytes 196640 | tf_op jit(solution)/shard_map/ppermute | solution.py:373
  86.1 1.8 collective-permute-start.26
  87.9 1.7 collective-permute-start.27
  89.7 8.0 %shard_map.117 = (f32[3,2,4,16,128]{4,3,2,1,0:T(8,128)}, f32[3,2,4,16,128]{4,3,2,1,0:T(8,128)}, f32[3,2,4,16,128]{4,3,2,1,0:T(8,128)}, f32[3,2,4,16,128]{4,3,2,1...) custom-call(f32[3,2,4,16,128]{4,3,2,1,0:T(8,128)} %get-tuple-element, ...), custom_call_target="tpu_custom_call" | custom-call | tf_op jit(solution)/shard_map/pallas_call | solution.py:433
  97.7 3.4 %collective-permute-done.26.refs_6_ = f32[3,2,4,16,128]{4,3,2,1,0:T(8,128)} collective-permute-done((f32[3,2,4,16,128]{4,3,2,1,0:T(8,128)}, f32[3,2,4,16,128]{4,3,2,1,0:T(8,128)}, u32[]{:S(2)}, u32[]{:S(2)}) %collective-permute-start.26) | collective-permute-done | bytes 196640 | tf_op jit(solution)/shard_map/ppermute | solution.py:373
  101.1 4.2 %collective-permute-done.27.refs_7_ = f32[3,2,4,16,128]{4,3,2,1,0:T(8,128)} collective-permute-done((f32[3,2,4,16,128]{4,3,2,1,0:T(8,128)}, f32[3,2,4,16,128]{4,3,2,1,0:T(8,128)}, u32[]{:S(2)}, u32[]{:S(2)}) %collective-permute-start.27) | collective-permute-done | bytes 196640 | tf_op jit(solution)/shard_map/ppermute | solution.py:373
  105.3 4.8 %shard_map.119 = f32[16,3,2,2,8,128]{5,4,3,2,1,0:T(8,128)} custom-call(f32[3,2,4,16,128]{4,3,2,1,0:T(8,128)} %get-tuple-element.63.refs_0_._, s32[1]{0:T(128)} %bitcast.me_ref, bf16[128,512]{1,0:T(8,128)(2,1)} %bitcast.16, bf16[128,512]{1,0:T(8,128)(2,1)} %bitcast.20, f32[3,2,4,16,128]{4,3,2,1,0:T(8,128)} %get-tuple-element.55._.refs_0_, ...), custom_call_target="tpu_custom_call" | custom-call | tf_op jit(solution)/shard_map/pallas_call | solution.py:462
  110.1 6.8 %all-to-all-start.3 = ((f32[16,3,2,2,8,128]{5,4,3,2,1,0:T(8,128)}), f32[16,3,2,2,8,128]{5,4,3,2,1,0:T(8,128)}, u32[]{:S(2)}, u32[]{:S(2)}) async-start(f32[16,3,2,2,8,128]{5,4,3,2,1,0:T(8,128)} %shard_map.119), calls=%async_computation.3 | async-start | bytes 1572864 | tf_op jit(solution)/shard_map/all_to_all | solution.py:378
  117.8 1.7 collective-permute-start.16
  119.5 1.4 collective-permute-start.17
  120.9 1.8 collective-permute-start.18
  122.8 1.9 collective-permute-start.19
  125.3 2.8 %collective-permute-start.20 = (f32[3,2,4,16,128]{4,3,2,1,0:T(8,128)}, f32[3,2,4,16,128]{4,3,2,1,0:T(8,128)}, u32[]{:S(2)}, u32[]{:S(2)}) collective-permute-start(f32[3,2,4,16,128]{4,3,2,1,0:T(8,128)} %get-tuple-element.70), channel_id=1, source_target_pairs={{0,7},{1,6},{2,5},{3,4},{4,3},{5,2},{6,1},{7,0},{8,15},{9,14},{10,... | collective-permute-start | bytes 589832 | tf_op jit(solution)/shard_map/ppermute | solution.py:373
  128.1 1.5 collective-permute-done.16.refs_3_
  129.6 4.8 %collective-permute-done.17.refs_4_ = f32[3,2,4,16,128]{4,3,2,1,0:T(8,128)} collective-permute-done((f32[3,2,4,16,128]{4,3,2,1,0:T(8,128)}, f32[3,2,4,16,128]{4,3,2,1,0:T(8,128)}, u32[]{:S(2)}, u32[]{:S(2)}) %collective-permute-start.17) | collective-permute-done | bytes 196640 | tf_op jit(solution)/shard_map/ppermute | solution.py:373
  134.3 4.5 %collective-permute-done.18.refs_5_ = f32[3,2,4,16,128]{4,3,2,1,0:T(8,128)} collective-permute-done((f32[3,2,4,16,128]{4,3,2,1,0:T(8,128)}, f32[3,2,4,16,128]{4,3,2,1,0:T(8,128)}, u32[]{:S(2)}, u32[]{:S(2)}) %collective-permute-start.18) | collective-permute-done | bytes 196640 | tf_op jit(solution)/shard_map/ppermute | solution.py:373
  138.8 4.7 %collective-permute-done.20.refs_7_ = f32[3,2,4,16,128]{4,3,2,1,0:T(8,128)} collective-permute-done((f32[3,2,4,16,128]{4,3,2,1,0:T(8,128)}, f32[3,2,4,16,128]{4,3,2,1,0:T(8,128)}, u32[]{:S(2)}, u32[]{:S(2)}) %collective-permute-start.20) | collective-permute-done | bytes 196640 | tf_op jit(solution)/shard_map/ppermute | solution.py:373
  143.6 4.8 %shard_map.118 = f32[16,3,2,2,8,128]{5,4,3,2,1,0:T(8,128)} custom-call(f32[3,2,4,16,128]{4,3,2,1,0:T(8,128)} %get-tuple-element.55._.refs_0_, s32[1]{0:T(128)} %bitcast.me_ref, bf16[128,512]{1,0:T(8,128)(2,1)} %bitcast.17, bf16[128,512]{1,0:T(8,128)(2,1)} %bitcast.21, f32[3,2,4,16,128]{4,3,2,1,0:T(8,128)} %get-tuple-element.63.refs_0_._, ...), custom_call_target="tpu_custom_call" | custom-call | tf_op jit(solution)/shard_map/pallas_call | solution.py:462
  148.3 6.9 %all-to-all-start.2 = ((f32[16,3,2,2,8,128]{5,4,3,2,1,0:T(8,128)}), f32[16,3,2,2,8,128]{5,4,3,2,1,0:T(8,128)}, u32[]{:S(2)}, u32[]{:S(2)}) async-start(f32[16,3,2,2,8,128]{5,4,3,2,1,0:T(8,128)} %shard_map.118), calls=%async_computation.2 | async-start | bytes 1572864 | tf_op jit(solution)/shard_map/all_to_all | solution.py:378
  155.3 1.9 copy-done
  157.2 2.0 %shard_map.121.g_ref = f32[1,128]{1,0:T(1,128)S(1)} custom-call(f32[4,2,3,16,8,256]{5,4,3,2,1,0:T(8,128)S(1)} %copy-done), custom_call_target="tpu_custom_call" | custom-call | tf_op jit(solution)/shard_map/pallas_call | solution.py:464
  159.3 4.3 %shard_map.120 = (f32[2,3,576,8,256]{4,3,2,1,0:T(8,128)}, bf16[216,256,256]{2,1,0:T(8,128)(2,1)}) custom-call(f32[16,3,2,2,8,128]{5,4,3,2,1,0:T(8,128)} %all-to-all-done.3.x_ref, bf16[256,512]{1,0:T(8,128)(2,1)S(1)} %copy-done.5, bf16[256,512]{1,0:T(8,128)(2,1)S(1)} %copy-done.4, bf16[256,512]{1,0:T(8,128)(2,1)S(1)} %copy-done.3, ...), custom_call_target="tpu_custom_call" | custom-call | tf_op jit(solution)/shard_map/pallas_call | solution.py:467
  163.6 4.4 %all-to-all-done.2.x_ref = f32[16,3,2,2,8,128]{5,4,3,2,1,0:T(8,128)} async-done(((f32[16,3,2,2,8,128]{5,4,3,2,1,0:T(8,128)}), f32[16,3,2,2,8,128]{5,4,3,2,1,0:T(8,128)}, u32[]{:S(2)}, u32[]{:S(2)}) %all-to-all-start.2) | async-done | bytes 786464 | tf_op jit(solution)/shard_map/all_to_all | solution.py:378
  168.0 4.4 %shard_map.122 = (f32[2,3,16,8,256]{4,3,2,1,0:T(8,128)S(1)}, f32[128,128]{1,0:T(8,128)S(1)}) custom-call(f32[16,3,2,2,8,128]{5,4,3,2,1,0:T(8,128)} %all-to-all-done.2.x_ref, bf16[216,256,256]{2,1,0:T(8,128)(2,1)} %get-tuple-element.78.t_ref, f32[2,3,576,8,256]{4,3,2,1,0:T(8,128)} %get-tuple-element.79.p_ref, f32[4,2,3,16,8,256]{5,4,3,2,1,0:T(8,128)S(1)} %copy-done.1, ...), custom_call_target="tpu_custom_call" | custom-call | tf_op jit(solution)/shard_map/pallas_call | solution.py:476
  172.4 16.9 %all_to_all.25 = f32[128,1,128]{2,1,0:T(1,128)S(1)} all-to-all(f32[128,1,128]{2,1,0:T(1,128)S(1)} %bitcast.12), channel_id=1, replica_groups=mesh['row_0'=4,'row_1'=4,'col_0'=4,'col_1'=2] {'row_0','row_1','col_0','..., dimensions={0} | all-to-all | bytes 131072 | tf_op jit(solution)/shard_map/all_to_all | solution.py:486
  189.3 3.1 %shard_map.123 = (f32[2,3,16,8,256]{4,3,2,1,0:T(8,128)}, f32[2,2,4]{2,1,0:T(2,128)}, f32[2,2]{1,0:T(2,128)}) custom-call(f32[128,128]{1,0:T(8,128)S(1)} %bitcast.11, f32[2,3,16,8,256]{4,3,2,1,0:T(8,128)S(1)} %get-tuple-element.81.img_ref, f32[4,2,3,16,8,256]{5,4,3,2,1,0:T(8,128)S(1)} %copy-done.1), custom_call_target="tpu_custom_call" | custom-call | tf_op jit(solution)/shard_map/pallas_call | solution.py:487
  (61 shorter events, 7.9 us)
Async XLA Ops:
  4.5 21.3 %all-to-all-start.1 = ((f32[16,3,2,2,8,128]{5,4,3,2,1,0:T(8,128)}), f32[16,3,2,2,8,128]{5,4,3,2,1,0:T(8,128)}, u32[]{:S(2)}, u32[]{:S(2)}) async-start(f32[16,3,2,2,8,128]{5,4,3,2,1,0:T(8,128)} %shard_map.112.refs_1_), calls=%async_computation.1 | async-start | bytes 1572864 | tf_op jit(solution)/shard_map/all_to_all | solution.py:378
  25.9 22.3 %all-to-all-start = ((f32[16,3,2,2,8,128]{5,4,3,2,1,0:T(8,128)}), f32[16,3,2,2,8,128]{5,4,3,2,1,0:T(8,128)}, u32[]{:S(2)}, u32[]{:S(2)}) async-start(f32[16,3,2,2,8,128]{5,4,3,2,1,0:T(8,128)} %shard_map.113), calls=%async_computation | async-start | bytes 1572864 | tf_op jit(solution)/shard_map/all_to_all | solution.py:378
  35.0 7.4 %collective-permute-start = (f32[3,2,4,16,128]{4,3,2,1,0:T(8,128)}, f32[3,2,4,16,128]{4,3,2,1,0:T(8,128)}, u32[]{:S(2)}, u32[]{:S(2)}) collective-permute-start(f32[3,2,4,16,128]{4,3,2,1,0:T(8,128)} %get-tuple-element.48), channel_id=1, source_target_pairs={{0,1},{1,0},{2,3},{3,2},{4,5},{5,4},{6,7},{7,6},{8,9},{9,8},{10,11... | collective-permute-start | bytes 589832 | tf_op jit(solution)/shard_map/ppermute | solution.py:373
  37.4 7.7 %collective-permute-start.1 = (f32[3,2,4,16,128]{4,3,2,1,0:T(8,128)}, f32[3,2,4,16,128]{4,3,2,1,0:T(8,128)}, u32[]{:S(2)}, u32[]{:S(2)}) collective-permute-start(f32[3,2,4,16,128]{4,3,2,1,0:T(8,128)} %get-tuple-element.49), channel_id=1, source_target_pairs={{0,2},{1,3},{2,0},{3,1},{4,6},{5,7},{6,4},{7,5},{8,10},{9,11},{10,... | collective-permute-start | bytes 589832 | tf_op jit(solution)/shard_map/ppermute | solution.py:373
  38.7 14.1 %collective-permute-start.2 = (f32[3,2,4,16,128]{4,3,2,1,0:T(8,128)}, f32[3,2,4,16,128]{4,3,2,1,0:T(8,128)S(1)}, u32[]{:S(2)}, u32[]{:S(2)}) collective-permute-start(f32[3,2,4,16,128]{4,3,2,1,0:T(8,128)} %get-tuple-element.50), channel_id=1, source_target_pairs={{0,3},{1,2},{2,1},{3,0},{4,7},{5,6},{6,5},{7,4},{8,11},{9,10},{10,... | collective-permute-start | bytes 589832 | tf_op jit(solution)/shard_map/ppermute | solution.py:373
  39.1 15.8 %collective-permute-start.3 = (f32[3,2,4,16,128]{4,3,2,1,0:T(8,128)}, f32[3,2,4,16,128]{4,3,2,1,0:T(8,128)S(1)}, u32[]{:S(2)}, u32[]{:S(2)}) collective-permute-start(f32[3,2,4,16,128]{4,3,2,1,0:T(8,128)} %get-tuple-element.51), channel_id=1, source_target_pairs={{0,4},{1,5},{2,6},{3,7},{4,0},{5,1},{6,2},{7,3},{8,12},{9,13},{10,... | collective-permute-start | bytes 589832 | tf_op jit(solution)/shard_map/ppermute | solution.py:373
  42.0 18.0 %collective-permute-start.4 = (f32[3,2,4,16,128]{4,3,2,1,0:T(8,128)}, f32[3,2,4,16,128]{4,3,2,1,0:T(8,128)}, u32[]{:S(2)}, u32[]{:S(2)}) collective-permute-start(f32[3,2,4,16,128]{4,3,2,1,0:T(8,128)} %get-tuple-element.52), channel_id=1, source_target_pairs={{0,5},{1,4},{2,7},{3,6},{4,1},{5,0},{6,3},{7,2},{8,13},{9,12},{10,... | collective-permute-start | bytes 589832 | tf_op jit(solution)/shard_map/ppermute | solution.py:373
  42.4 17.6 %collective-permute-start.5 = (f32[3,2,4,16,128]{4,3,2,1,0:T(8,128)}, f32[3,2,4,16,128]{4,3,2,1,0:T(8,128)}, u32[]{:S(2)}, u32[]{:S(2)}) collective-permute-start(f32[3,2,4,16,128]{4,3,2,1,0:T(8,128)} %get-tuple-element.53), channel_id=1, source_target_pairs={{0,6},{1,7},{2,4},{3,5},{4,2},{5,3},{6,0},{7,1},{8,14},{9,15},{10,... | collective-permute-start | bytes 589832 | tf_op jit(solution)/shard_map/ppermute | solution.py:373
  45.1 18.1 %collective-permute-start.6 = (f32[3,2,4,16,128]{4,3,2,1,0:T(8,128)}, f32[3,2,4,16,128]{4,3,2,1,0:T(8,128)}, u32[]{:S(2)}, u32[]{:S(2)}) collective-permute-start(f32[3,2,4,16,128]{4,3,2,1,0:T(8,128)} %get-tuple-element.54), channel_id=1, source_target_pairs={{0,7},{1,6},{2,5},{3,4},{4,3},{5,2},{6,1},{7,0},{8,15},{9,14},{10,... | collective-permute-start | bytes 589832 | tf_op jit(solution)/shard_map/ppermute | solution.py:373
  52.8 0.7 copy-start.9
  53.5 19.5 %collective-permute-start.7 = (f32[3,2,4,16,128]{4,3,2,1,0:T(8,128)}, f32[3,2,4,16,128]{4,3,2,1,0:T(8,128)S(1)}, u32[]{:S(2)}, u32[]{:S(2)}) collective-permute-start(f32[3,2,4,16,128]{4,3,2,1,0:T(8,128)} %get-tuple-element.56), channel_id=1, source_target_pairs={{0,1},{1,0},{2,3},{3,2},{4,5},{5,4},{6,7},{7,6},{8,9},{9,8},{10,11... | collective-permute-start | bytes 589832 | tf_op jit(solution)/shard_map/ppermute | solution.py:373
  54.9 0.7 copy-start.10
  55.6 18.7 %collective-permute-start.8 = (f32[3,2,4,16,128]{4,3,2,1,0:T(8,128)}, f32[3,2,4,16,128]{4,3,2,1,0:T(8,128)S(1)}, u32[]{:S(2)}, u32[]{:S(2)}) collective-permute-start(f32[3,2,4,16,128]{4,3,2,1,0:T(8,128)} %get-tuple-element.57), channel_id=1, source_target_pairs={{0,2},{1,3},{2,0},{3,1},{4,6},{5,7},{6,4},{7,5},{8,10},{9,11},{10,... | collective-permute-start | bytes 589832 | tf_op jit(solution)/shard_map/ppermute | solution.py:373
  60.0 16.5 %collective-permute-start.9 = (f32[3,2,4,16,128]{4,3,2,1,0:T(8,128)}, f32[3,2,4,16,128]{4,3,2,1,0:T(8,128)}, u32[]{:S(2)}, u32[]{:S(2)}) collective-permute-start(f32[3,2,4,16,128]{4,3,2,1,0:T(8,128)} %get-tuple-element.58), channel_id=1, source_target_pairs={{0,3},{1,2},{2,1},{3,0},{4,7},{5,6},{6,5},{7,4},{8,11},{9,10},{10,... | collective-permute-start | bytes 589832 | tf_op jit(solution)/shard_map/ppermute | solution.py:373
  60.0 16.5 %collective-permute-start.10 = (f32[3,2,4,16,128]{4,3,2,1,0:T(8,128)}, f32[3,2,4,16,128]{4,3,2,1,0:T(8,128)}, u32[]{:S(2)}, u32[]{:S(2)}) collective-permute-start(f32[3,2,4,16,128]{4,3,2,1,0:T(8,128)} %get-tuple-element.59), channel_id=1, source_target_pairs={{0,4},{1,5},{2,6},{3,7},{4,0},{5,1},{6,2},{7,3},{8,12},{9,13},{10,... | collective-permute-start | bytes 589832 | tf_op jit(solution)/shard_map/ppermute | solution.py:373
  63.2 13.5 %collective-permute-start.11 = (f32[3,2,4,16,128]{4,3,2,1,0:T(8,128)}, f32[3,2,4,16,128]{4,3,2,1,0:T(8,128)}, u32[]{:S(2)}, u32[]{:S(2)}) collective-permute-start(f32[3,2,4,16,128]{4,3,2,1,0:T(8,128)} %get-tuple-element.60), channel_id=1, source_target_pairs={{0,5},{1,4},{2,7},{3,6},{4,1},{5,0},{6,3},{7,2},{8,13},{9,12},{10,... | collective-permute-start | bytes 589832 | tf_op jit(solution)/shard_map/ppermute | solution.py:373
  72.9 16.7 %copy-start.7 = (f32[3,2,4,16,128]{4,3,2,1,0:T(8,128)}, f32[3,2,4,16,128]{4,3,2,1,0:T(8,128)S(1)}, u32[]{:S(2)}) copy-start(f32[3,2,4,16,128]{4,3,2,1,0:T(8,128)S(1)} %collective-permute-done.7.refs_1_) | copy-start | bytes 589828
  72.9 7.4 %collective-permute-start.12 = (f32[3,2,4,16,128]{4,3,2,1,0:T(8,128)}, f32[3,2,4,16,128]{4,3,2,1,0:T(8,128)}, u32[]{:S(2)}, u32[]{:S(2)}) collective-permute-start(f32[3,2,4,16,128]{4,3,2,1,0:T(8,128)} %get-tuple-element.61), channel_id=1, source_target_pairs={{0,6},{1,7},{2,4},{3,5},{4,2},{5,3},{6,0},{7,1},{8,14},{9,15},{10,... | collective-permute-start | bytes 589832 | tf_op jit(solution)/shard_map/ppermute | solution.py:373
  74.2 15.4 %copy-start.8 = (f32[3,2,4,16,128]{4,3,2,1,0:T(8,128)}, f32[3,2,4,16,128]{4,3,2,1,0:T(8,128)S(1)}, u32[]{:S(2)}) copy-start(f32[3,2,4,16,128]{4,3,2,1,0:T(8,128)S(1)} %collective-permute-done.8.refs_2_) | copy-start | bytes 589828
  74.2 11.1 %collective-permute-start.13 = (f32[3,2,4,16,128]{4,3,2,1,0:T(8,128)}, f32[3,2,4,16,128]{4,3,2,1,0:T(8,128)}, u32[]{:S(2)}, u32[]{:S(2)}) collective-permute-start(f32[3,2,4,16,128]{4,3,2,1,0:T(8,128)} %get-tuple-element.62), channel_id=1, source_target_pairs={{0,7},{1,6},{2,5},{3,4},{4,3},{5,2},{6,1},{7,0},{8,15},{9,14},{10,... | collective-permute-start | bytes 589832 | tf_op jit(solution)/shard_map/ppermute | solution.py:373
  76.6 9.6 %collective-permute-start.21 = (f32[3,2,4,16,128]{4,3,2,1,0:T(8,128)}, f32[3,2,4,16,128]{4,3,2,1,0:T(8,128)}, u32[]{:S(2)}, u32[]{:S(2)}) collective-permute-start(f32[3,2,4,16,128]{4,3,2,1,0:T(8,128)} %get-tuple-element.71), channel_id=1, source_target_pairs={{0,1},{1,0},{2,3},{3,2},{4,5},{5,4},{6,7},{7,6},{8,9},{9,8},{10,11... | collective-permute-start | bytes 589832 | tf_op jit(solution)/shard_map/ppermute | solution.py:373
  76.6 11.3 %collective-permute-start.22 = (f32[3,2,4,16,128]{4,3,2,1,0:T(8,128)}, f32[3,2,4,16,128]{4,3,2,1,0:T(8,128)}, u32[]{:S(2)}, u32[]{:S(2)}) collective-permute-start(f32[3,2,4,16,128]{4,3,2,1,0:T(8,128)} %get-tuple-element.72), channel_id=1, source_target_pairs={{0,2},{1,3},{2,0},{3,1},{4,6},{5,7},{6,4},{7,5},{8,10},{9,11},{10,... | collective-permute-start | bytes 589832 | tf_op jit(solution)/shard_map/ppermute | solution.py:373
  76.7 21.0 %collective-permute-start.23 = (f32[3,2,4,16,128]{4,3,2,1,0:T(8,128)}, f32[3,2,4,16,128]{4,3,2,1,0:T(8,128)}, u32[]{:S(2)}, u32[]{:S(2)}) collective-permute-start(f32[3,2,4,16,128]{4,3,2,1,0:T(8,128)} %get-tuple-element.73), channel_id=1, source_target_pairs={{0,3},{1,2},{2,1},{3,0},{4,7},{5,6},{6,5},{7,4},{8,11},{9,10},{10,... | collective-permute-start | bytes 589832 | tf_op jit(solution)/shard_map/ppermute | solution.py:373
  80.3 17.4 %collective-permute-start.24 = (f32[3,2,4,16,128]{4,3,2,1,0:T(8,128)}, f32[3,2,4,16,128]{4,3,2,1,0:T(8,128)}, u32[]{:S(2)}, u32[]{:S(2)}) collective-permute-start(f32[3,2,4,16,128]{4,3,2,1,0:T(8,128)} %get-tuple-element.74), channel_id=1, source_target_pairs={{0,4},{1,5},{2,6},{3,7},{4,0},{5,1},{6,2},{7,3},{8,12},{9,13},{10,... | collective-permute-start | bytes 589832 | tf_op jit(solution)/shard_map/ppermute | solution.py:373
  85.4 12.3 %collective-permute-start.25 = (f32[3,2,4,16,128]{4,3,2,1,0:T(8,128)}, f32[3,2,4,16,128]{4,3,2,1,0:T(8,128)}, u32[]{:S(2)}, u32[]{:S(2)}) collective-permute-start(f32[3,2,4,16,128]{4,3,2,1,0:T(8,128)} %get-tuple-element.75), channel_id=1, source_target_pairs={{0,5},{1,4},{2,7},{3,6},{4,1},{5,0},{6,3},{7,2},{8,13},{9,12},{10,... | collective-permute-start | bytes 589832 | tf_op jit(solution)/shard_map/ppermute | solution.py:373
  86.1 15.0 %collective-permute-start.26 = (f32[3,2,4,16,128]{4,3,2,1,0:T(8,128)}, f32[3,2,4,16,128]{4,3,2,1,0:T(8,128)}, u32[]{:S(2)}, u32[]{:S(2)}) collective-permute-start(f32[3,2,4,16,128]{4,3,2,1,0:T(8,128)} %get-tuple-element.76), channel_id=1, source_target_pairs={{0,6},{1,7},{2,4},{3,5},{4,2},{5,3},{6,0},{7,1},{8,14},{9,15},{10,... | collective-permute-start | bytes 589832 | tf_op jit(solution)/shard_map/ppermute | solution.py:373
  87.9 17.4 %collective-permute-start.27 = (f32[3,2,4,16,128]{4,3,2,1,0:T(8,128)}, f32[3,2,4,16,128]{4,3,2,1,0:T(8,128)}, u32[]{:S(2)}, u32[]{:S(2)}) collective-permute-start(f32[3,2,4,16,128]{4,3,2,1,0:T(8,128)} %get-tuple-element.77), channel_id=1, source_target_pairs={{0,7},{1,6},{2,5},{3,4},{4,3},{5,2},{6,1},{7,0},{8,15},{9,14},{10,... | collective-permute-start | bytes 589832 | tf_op jit(solution)/shard_map/ppermute | solution.py:373
  97.7 19.3 %copy-start.14 = (f32[3,2,4,16,128]{4,3,2,1,0:T(8,128)S(1)}, f32[3,2,4,16,128]{4,3,2,1,0:T(8,128)}, u32[]{:S(2)}) copy-start(f32[3,2,4,16,128]{4,3,2,1,0:T(8,128)} %get-tuple-element.64) | copy-start | bytes 589828
  97.7 20.1 %copy-start.13 = (f32[3,2,4,16,128]{4,3,2,1,0:T(8,128)S(1)}, f32[3,2,4,16,128]{4,3,2,1,0:T(8,128)}, u32[]{:S(2)}) copy-start(f32[3,2,4,16,128]{4,3,2,1,0:T(8,128)} %get-tuple-element.65) | copy-start | bytes 589828
  110.1 38.2 %all-to-all-start.3 = ((f32[16,3,2,2,8,128]{5,4,3,2,1,0:T(8,128)}), f32[16,3,2,2,8,128]{5,4,3,2,1,0:T(8,128)}, u32[]{:S(2)}, u32[]{:S(2)}) async-start(f32[16,3,2,2,8,128]{5,4,3,2,1,0:T(8,128)} %shard_map.119), calls=%async_computation.3 | async-start | bytes 1572864 | tf_op jit(solution)/shard_map/all_to_all | solution.py:378
  117.0 5.8 %collective-permute-start.14 = (f32[3,2,4,16,128]{4,3,2,1,0:T(8,128)S(1)}, f32[3,2,4,16,128]{4,3,2,1,0:T(8,128)S(1)}, u32[]{:S(2)}, u32[]{:S(2)}) collective-permute-start(f32[3,2,4,16,128]{4,3,2,1,0:T(8,128)S(1)} %copy-done.14), channel_id=1, source_target_pairs={{0,1},{1,0},{2,3},{3,2},{4,5},{5,4},{6,7},{7,6},{8,9},{9,8},{10,11... | collective-permute-start | bytes 589832 | tf_op jit(solution)/shard_map/ppermute | solution.py:373
  117.8 6.9 %collective-permute-start.15 = (f32[3,2,4,16,128]{4,3,2,1,0:T(8,128)S(1)}, f32[3,2,4,16,128]{4,3,2,1,0:T(8,128)S(1)}, u32[]{:S(2)}, u32[]{:S(2)}) collective-permute-start(f32[3,2,4,16,128]{4,3,2,1,0:T(8,128)S(1)} %copy-done.13), channel_id=1, source_target_pairs={{0,2},{1,3},{2,0},{3,1},{4,6},{5,7},{6,4},{7,5},{8,10},{9,11},{10,... | collective-permute-start | bytes 589832 | tf_op jit(solution)/shard_map/ppermute | solution.py:373
  117.8 11.8 %collective-permute-start.16 = (f32[3,2,4,16,128]{4,3,2,1,0:T(8,128)}, f32[3,2,4,16,128]{4,3,2,1,0:T(8,128)}, u32[]{:S(2)}, u32[]{:S(2)}) collective-permute-start(f32[3,2,4,16,128]{4,3,2,1,0:T(8,128)} %get-tuple-element.66), channel_id=1, source_target_pairs={{0,3},{1,2},{2,1},{3,0},{4,7},{5,6},{6,5},{7,4},{8,11},{9,10},{10,... | collective-permute-start | bytes 589832 | tf_op jit(solution)/shard_map/ppermute | solution.py:373
  119.5 14.8 %collective-permute-start.17 = (f32[3,2,4,16,128]{4,3,2,1,0:T(8,128)}, f32[3,2,4,16,128]{4,3,2,1,0:T(8,128)}, u32[]{:S(2)}, u32[]{:S(2)}) collective-permute-start(f32[3,2,4,16,128]{4,3,2,1,0:T(8,128)} %get-tuple-element.67), channel_id=1, source_target_pairs={{0,4},{1,5},{2,6},{3,7},{4,0},{5,1},{6,2},{7,3},{8,12},{9,13},{10,... | collective-permute-start | bytes 589832 | tf_op jit(solution)/shard_map/ppermute | solution.py:373
  120.9 17.9 %collective-permute-start.18 = (f32[3,2,4,16,128]{4,3,2,1,0:T(8,128)}, f32[3,2,4,16,128]{4,3,2,1,0:T(8,128)}, u32[]{:S(2)}, u32[]{:S(2)}) collective-permute-start(f32[3,2,4,16,128]{4,3,2,1,0:T(8,128)} %get-tuple-element.68), channel_id=1, source_target_pairs={{0,5},{1,4},{2,7},{3,6},{4,1},{5,0},{6,3},{7,2},{8,13},{9,12},{10,... | collective-permute-start | bytes 589832 | tf_op jit(solution)/shard_map/ppermute | solution.py:373
  122.8 1.9 copy-start.11
  122.8 16.1 %collective-permute-start.19 = (f32[3,2,4,16,128]{4,3,2,1,0:T(8,128)}, f32[3,2,4,16,128]{4,3,2,1,0:T(8,128)}, u32[]{:S(2)}, u32[]{:S(2)}) collective-permute-start(f32[3,2,4,16,128]{4,3,2,1,0:T(8,128)} %get-tuple-element.69), channel_id=1, source_target_pairs={{0,6},{1,7},{2,4},{3,5},{4,2},{5,3},{6,0},{7,1},{8,14},{9,15},{10,... | collective-permute-start | bytes 589832 | tf_op jit(solution)/shard_map/ppermute | solution.py:373
  124.7 0.7 copy-start.12
  125.3 33.9 %copy-start.2 = (bf16[256,512]{1,0:T(8,128)(2,1)S(1)}, bf16[256,512]{1,0:T(8,128)(2,1)}, u32[]{:S(2)}) copy-start(bf16[256,512]{1,0:T(8,128)(2,1)} %constant.25.clone.refs_4_.refs_6_.sl_ref.refs_3_) | copy-start | bytes 786436
  125.3 33.9 %copy-start.6 = (f32[16,8,256]{2,1,0:T(8,128)S(1)}, f32[16,8,256]{2,1,0:T(8,128)}, u32[]{:S(2)}) copy-start(f32[16,8,256]{2,1,0:T(8,128)} %chi_ref.1) | copy-start | bytes 393220
  125.3 18.2 %collective-permute-start.20 = (f32[3,2,4,16,128]{4,3,2,1,0:T(8,128)}, f32[3,2,4,16,128]{4,3,2,1,0:T(8,128)}, u32[]{:S(2)}, u32[]{:S(2)}) collective-permute-start(f32[3,2,4,16,128]{4,3,2,1,0:T(8,128)} %get-tuple-element.70), channel_id=1, source_target_pairs={{0,7},{1,6},{2,5},{3,4},{4,3},{5,2},{6,1},{7,0},{8,15},{9,14},{10,... | collective-permute-start | bytes 589832 | tf_op jit(solution)/shard_map/ppermute | solution.py:373
  148.3 19.7 %all-to-all-start.2 = ((f32[16,3,2,2,8,128]{5,4,3,2,1,0:T(8,128)}), f32[16,3,2,2,8,128]{5,4,3,2,1,0:T(8,128)}, u32[]{:S(2)}, u32[]{:S(2)}) async-start(f32[16,3,2,2,8,128]{5,4,3,2,1,0:T(8,128)} %shard_map.118), calls=%async_computation.2 | async-start | bytes 1572864 | tf_op jit(solution)/shard_map/all_to_all | solution.py:378
  155.3 1.9 copy-start
  157.2 2.1 %copy-start.3 = (bf16[256,512]{1,0:T(8,128)(2,1)S(1)}, bf16[256,512]{1,0:T(8,128)(2,1)}, u32[]{:S(2)}) copy-start(bf16[256,512]{1,0:T(8,128)(2,1)} %constant.24.clone.refs_3_.refs_5_.sh_ref.refs_2_) | copy-start | bytes 786436
  157.2 2.1 %copy-start.4 = (bf16[256,512]{1,0:T(8,128)(2,1)S(1)}, bf16[256,512]{1,0:T(8,128)(2,1)}, u32[]{:S(2)}) copy-start(bf16[256,512]{1,0:T(8,128)(2,1)} %constant.23.clone.refs_2_.refs_4_.cl_ref.refs_1_) | copy-start | bytes 786436
  157.2 2.1 %copy-start.5 = (bf16[256,512]{1,0:T(8,128)(2,1)S(1)}, bf16[256,512]{1,0:T(8,128)(2,1)}, u32[]{:S(2)}) copy-start(bf16[256,512]{1,0:T(8,128)(2,1)} %constant.22.clone.refs_1_.refs_3_.ch_ref.refs_0_) | copy-start | bytes 786436
  159.3 8.7 %copy-start.1 = (f32[4,2,3,16,8,256]{5,4,3,2,1,0:T(8,128)S(1)}, f32[4,2,3,16,8,256]{5,4,3,2,1,0:T(8,128)}, u32[]{:S(2)}) copy-start(f32[4,2,3,16,8,256]{5,4,3,2,1,0:T(8,128)} %b_ref.5) | copy-start | bytes 9437188
